TPU v7x, 512 devices: a whole 4x8x8 slice. The times are simulated.
512 devices in a mesh: tier: 64 (over x, z, core), sys: 8 (over y).
Axes of the slice: x: 4, y: 8, z: 8, core: 2. Of those that a mesh axis runs over, the one named last changes fastest.
Arguments:
- state: float32 [256, 2, 512, 512], P('tier', None, 'sys'), may hold values from -6 to 6
- slope: float32 [256, 2, 512, 512], P('tier', None, 'sys'), may hold values from -6 to 6
- counts: int32 [64], replicated, may hold values from 1 to 4, 128 in all
- links: int32 [4, 256, 96], P(None, 'tier'), may hold values from 0 to 255, as said below
- mode_site: int32 [48], replicated, may hold values from 0 to 511, as said below
- mode_coef: float32 [2, 48], replicated, may hold values from -3 to 3
- mode_rate: float32 [48], replicated, may hold values from 0.01 to 0.1
- h_bands: float32 [9, 512], replicated, may hold values from -3 to 3
Outputs:
- slope_next: float32 [256, 2, 512, 512], P('tier', None, 'sys')
- partial_sum: float32 [256, 2, 512, 512], P('tier', None, 'sys')
Inputs may be any that keep to these rules, and one draw needn't show every extreme that they name: Index d of tier holds counts[d] live auxiliary operators, in its first slots; the counts sum to 128. links[0] is a global slot (index of tier times 4 plus the slot), links[1] a mode below 48, links[2] is 0 or 1, links[3] is 1 or 2. Each slot has exactly one link with direction 0 and one with direction 1 for every mode. Of the 384 links of the slots of one index of tier, exactly 6 name slots of each index of tier; of the links whose mode k has k // 6 equal to one row block's number, at most 2 name slots of one index of tier, and in every row block some index of tier is named by exactly 2 of them. `mode_site`: mode k's site lies in row block k // 6, that is in rows (k // 6) * 64 to (k // 6) * 64 + 63; the sites are distinct.
All inputs are finite; a program needn't handle non-finite values.
Results may differ from a plain program's by a relative error of at most 0.0003.
Values sent between devices are 32-bit elements; how exact they have to be, the bound alone decides.
No kernel may reach another device: no remote copies, remote signals or barrier semaphores. Data moves between devices by JAX's collectives and lax.ppermute only.
A program may use at most 64 MiB of HBM per device.

v0:
```python
import jax
import jax.numpy as jnp
from jax import lax
from jax.sharding import PartitionSpec as P

step_size = 0.05


def padded_2(block, sides, width):
    for axis, dim in sides:
        count = lax.axis_size(axis)
        forward = [(i, i + 1) for i in range(count - 1)]
        backward = [(target, source) for source, target in forward]
        low = lax.ppermute(
            lax.slice_in_dim(block, block.shape[dim] - width, None, axis=dim), axis, forward
        )
        high = lax.ppermute(lax.slice_in_dim(block, 0, width, axis=dim), axis, backward)
        block = jnp.concatenate([low, block, high], axis=dim)
    return block


def in_one_piece(arrays, axis, split_dim, concat_dim, along):
    both = jnp.concatenate(arrays, axis=along)
    filled, at, finished = (
        lax.all_to_all(both, axis, split_axis=split_dim, concat_axis=concat_dim, tiled=True),
        0,
        [],
    )
    for a in arrays:
        finished.append(lax.slice_in_dim(filled, at, at + a.shape[along], axis=along))
        at += a.shape[along]
    return tuple(finished)


def lookup(index, table):
    matches = index[..., None] == jnp.arange(table.shape[-1], dtype=jnp.int32)
    return jnp.sum(jnp.where(matches, table, jnp.zeros((), table.dtype)), axis=-1)


def place_values(keys, values, total):
    matches = keys[:, None] == jnp.arange(total, dtype=jnp.int32)[None, :]
    return jnp.sum(jnp.where(matches, values[:, None], 0), axis=0)


def shifted_band(h_bands):
    band_width = h_bands.shape[0] - 1
    length = h_bands.shape[1]
    padded = jnp.pad(h_bands, ((0, 0), (band_width, 0)))
    return jnp.stack(
        [
            padded[offset, band_width - offset : band_width - offset + length]
            for offset in range(band_width + 1)
        ]
    )


def band_rows(padded, upper_band, lower_band, band_width):
    length = upper_band.shape[1]
    summed = upper_band[0][:, None] * padded[..., band_width : band_width + length, :]
    for offset in range(1, band_width + 1):
        summed = (
            summed
            + upper_band[offset][:, None]
            * padded[..., band_width + offset : band_width + offset + length, :]
        )
        summed = (
            summed
            + lower_band[offset][:, None]
            * padded[..., band_width - offset : band_width - offset + length, :]
        )
    return summed


def band_cols(field, upper_band, lower_band, band_width):
    length = field.shape[-1]
    padded = jnp.pad(field, ((0, 0),) * (field.ndim - 1) + ((band_width, band_width),))
    summed = upper_band[0] * field
    for offset in range(1, band_width + 1):
        summed = (
            summed
            + upper_band[offset] * padded[..., band_width + offset : band_width + offset + length]
        )
        summed = (
            summed
            + lower_band[offset] * padded[..., band_width - offset : band_width - offset + length]
        )
    return summed


def exclusive_rank(matches):
    as_int = matches.astype(jnp.int32)
    before = jnp.cumsum(as_int, axis=0) - as_int
    return jnp.sum(jnp.where(matches, before, 0), axis=1)


def shards(state, slope, counts, links, mode_site, mode_coef, mode_rate, h_bands):
    slot_count = state.shape[0]
    row_count = state.shape[2]
    levels = state.shape[3]
    band_width = h_bands.shape[0] - 1
    link_total = links.shape[1] * links.shape[2]
    per_slot = links.shape[2]
    mode_total = mode_site.shape[0]
    block_modes = mode_total // lax.axis_size("sys")
    tier_index = lax.axis_index("tier")
    sys_index = lax.axis_index("sys")
    row_start = sys_index * row_count
    midpoint = state + 0.5 * step_size * slope
    padded = padded_2(midpoint, (("sys", 2),), band_width)
    neighbour = links[0].reshape(-1)
    link_mode = links[1].reshape(-1)
    link_kind = links[2].reshape(-1)
    link_level = links[3].reshape(-1).astype(jnp.float32)
    sites_of = lookup(link_mode, mode_site)
    holder = neighbour // slot_count
    target_slot = neighbour % slot_count
    in_block = link_mode // block_modes == sys_index
    local_row = jnp.clip(sites_of - row_start, 0, row_count - 1)
    neighbour_live = (target_slot < lookup(holder, counts)).astype(jnp.float32)
    downward = link_kind == 1
    weight_re = (
        jnp.where(downward, link_level * lookup(link_mode, mode_coef[0]), 1.0) * neighbour_live
    )
    weight_im = (
        jnp.where(downward, link_level * lookup(link_mode, mode_coef[1]), 0.0) * neighbour_live
    )
    rate_of = jnp.where(downward, link_level * lookup(link_mode, mode_rate), 0.0)
    damping = jnp.sum(rate_of.reshape(slot_count, per_slot), axis=1)
    tiers = lax.axis_size("tier")
    capacity = link_total // tiers
    block_capacity = 2 * ((slot_count * block_modes + tiers - 1) // tiers)
    matches = holder[:, None] == jnp.arange(tiers, dtype=jnp.int32)
    position = exclusive_rank(matches)
    block_position = exclusive_rank(matches & in_block[:, None])
    flat_key = holder * capacity + position
    block_key = jnp.where(
        in_block, holder * block_capacity + block_position, tiers * block_capacity
    )
    ask_slot = place_values(flat_key, target_slot, tiers * capacity).reshape(tiers, capacity)
    ask_site = place_values(flat_key, sites_of, tiers * capacity).reshape(tiers, capacity)
    row_slot = place_values(block_key, target_slot, tiers * block_capacity).reshape(
        tiers, block_capacity
    )
    row_site = place_values(block_key, sites_of, tiers * block_capacity).reshape(
        tiers, block_capacity
    )
    got_slot, got_site, got_row_slot, got_row_site = in_one_piece(
        (ask_slot, ask_site, row_slot, row_site), "tier", 0, 0, 1
    )
    answer_cols = midpoint[got_slot, :, :, got_site].reshape(tiers, capacity, 2 * row_count)
    answer_rows = midpoint[
        got_row_slot, :, jnp.clip(got_row_site - row_start, 0, row_count - 1), :
    ].reshape(tiers, block_capacity, 2 * levels)
    back_cols, back_rows = (
        lax.all_to_all(answer_cols, "tier", split_axis=0, concat_axis=0, tiled=True),
        lax.all_to_all(answer_rows, "tier", split_axis=0, concat_axis=0, tiled=True),
    )
    column_part = back_cols[holder, position]
    safe_holder = jnp.where(in_block, holder, 0)
    safe_position = jnp.where(in_block, block_position, 0)
    row_part = jnp.where(in_block[:, None], back_rows[safe_holder, safe_position], 0.0)
    lower_full = shifted_band(h_bands)
    upper_local = lax.dynamic_slice_in_dim(h_bands, row_start, row_count, 1)
    lower_local = lax.dynamic_slice_in_dim(lower_full, row_start, row_count, 1)
    commuted = band_rows(padded, upper_local, lower_local, band_width) - band_cols(
        midpoint, h_bands, lower_full, band_width
    )
    deriv_re = commuted[:, 1] - damping[:, None, None] * midpoint[:, 0]
    deriv_im = -commuted[:, 0] - damping[:, None, None] * midpoint[:, 1]
    column_part = column_part.reshape(link_total, 2, row_count)
    row_part = row_part.reshape(link_total, 2, levels)
    col_re = -(weight_re[:, None] * column_part[:, 1] - weight_im[:, None] * column_part[:, 0])
    col_im = weight_re[:, None] * column_part[:, 0] + weight_im[:, None] * column_part[:, 1]
    row_re = jnp.where(
        in_block[:, None],
        weight_re[:, None] * row_part[:, 1] + weight_im[:, None] * row_part[:, 0],
        0.0,
    )
    row_im = jnp.where(
        in_block[:, None],
        -(weight_re[:, None] * row_part[:, 0] - weight_im[:, None] * row_part[:, 1]),
        0.0,
    )
    col_pair = jnp.stack([col_re, col_im], axis=1).reshape(slot_count, per_slot, 2, row_count)
    row_pair = jnp.stack([row_re, row_im], axis=1).reshape(slot_count, per_slot, 2, levels)
    site_table = (
        (sites_of[:, None] == jnp.arange(levels, dtype=jnp.int32)[None, :])
        .astype(jnp.float32)
        .reshape(slot_count, per_slot, levels)
    )
    row_table = (
        (local_row[:, None] == jnp.arange(row_count, dtype=jnp.int32)[None, :])
        .astype(jnp.float32)
        .reshape(slot_count, per_slot, row_count)
    )
    added_cols = jnp.einsum("gkcr,gkl->gcrl", col_pair, site_table, precision=lax.Precision.HIGHEST)
    added_rows = jnp.einsum("gkr,gkcl->gcrl", row_table, row_pair, precision=lax.Precision.HIGHEST)
    live = (jnp.arange(slot_count, dtype=jnp.int32) < lookup(tier_index, counts)).astype(
        jnp.float32
    )
    slope_next = (jnp.stack([deriv_re, deriv_im], axis=1) + added_cols + added_rows) * live[
        :, None, None, None
    ]
    partial_sum = (state + step_size / 6.0 * slope + step_size / 3.0 * slope_next) * live[
        :, None, None, None
    ]
    return (slope_next, partial_sum)


def solution(mesh):
    in_specs = (
        P("tier", None, "sys", None),
        P("tier", None, "sys", None),
        P(),
        P(None, "tier", None),
        P(),
        P(),
        P(),
        P(),
    )
    out_specs = (P("tier", None, "sys", None), P("tier", None, "sys", None))
    return jax.shard_map(shards, mesh=mesh, in_specs=in_specs, out_specs=out_specs, check_vma=False)
```

profile of v0, /device:TPU:1, one launch (start us, length us, event | category | flops | bytes accessed | tf_op | source)
XLA Modules:
  0.0 93.3 jit_solution(2346561778025508693)
XLA Ops:
  0.7 1.8 %multiply_add_fusion = f32[4,2,64,512]{3,2,1,0:T(8,128)S(1)} fusion(f32[4,2,64,512]{3,2,1,0:T(8,128)} %param.8, f32[4,2,64,512]{3,2,1,0:T(8,128)} %param.9), kind=kLoop, calls=%fused_computation.139 | loop fusion | flops 524288 | bytes 3145728 | tf_op jit(solution)/shard_map/add | solution.py:108
  3.2 4.7 %collective-permute-start.1 = (f32[4,2,8,512]{3,2,1,0:T(8,128)}, f32[4,2,8,512]{3,2,1,0:T(8,128)}, u32[]{:S(2)}, u32[]{:S(2)}) collective-permute-start(f32[4,2,8,512]{3,2,1,0:T(8,128)} %get-tuple-element.24), channel_id=1, source_target_pairs={{0,1},{1,2},{2,3},{3,4},{4,5},{5,6},{6,7},{8,9},{9,10},{10,11},{11... | collective-permute-start | bytes 393224 | tf_op jit(solution)/shard_map/ppermute | solution.py:14
  7.9 1.3 %collective-permute-start = (f32[4,2,8,512]{3,2,1,0:T(8,128)}, f32[4,2,8,512]{3,2,1,0:T(8,128)}, u32[]{:S(2)}, u32[]{:S(2)}) collective-permute-start(f32[4,2,8,512]{3,2,1,0:T(8,128)} %get-tuple-element.23), channel_id=1, source_target_pairs={{1,0},{2,1},{3,2},{4,3},{5,4},{6,5},{7,6},{9,8},{10,9},{11,10},{12... | collective-permute-start | bytes 393224 | tf_op jit(solution)/shard_map/ppermute | solution.py:17
  10.9 0.9 reduce-window.16
  12.1 0.9 reduce-window.14
  15.9 14.3 %all-to-all-start = ((s32[64,1,16]{2,1,0:T(1,128)}), s32[64,1,16]{2,1,0:T(1,128)S(1)}, u32[]{:S(2)}, u32[]{:S(2)}) async-start(s32[64,1,16]{2,1,0:T(1,128)} %bitcast.40), calls=%async_computation | async-start | bytes 65536 | tf_op jit(solution)/shard_map/all_to_all | solution.py:25
  32.2 0.7 dynamic-slice_bitcast_fusion.14
  33.6 1.1 %copy.38 = f32[4,2,64,512]{2,1,3,0:T(2,128)S(1)} copy(f32[4,2,64,512]{3,2,1,0:T(8,128)S(1)} %multiply_add_fusion) | data formatting | bytes 2097152 | tf_op jit(solution)/shard_map/add | solution.py:108
  34.8 4.6 %all-to-all-done = s32[64,1,16]{2,1,0:T(1,128)S(1)} async-done(((s32[64,1,16]{2,1,0:T(1,128)}), s32[64,1,16]{2,1,0:T(1,128)S(1)}, u32[]{:S(2)}, u32[]{:S(2)}) %all-to-all-start) | async-done | bytes 4128 | tf_op jit(solution)/shard_map/all_to_all | solution.py:25
  40.1 2.3 %gather_fusion = f32[384,2,64]{2,1,0:T(2,128)S(1)} fusion(f32[4,2,64,512]{2,1,3,0:T(2,128)S(1)} %copy.38, s32[384]{0:T(512)S(1)} %reshape.553), kind=kCustom, calls=%fused_computation | custom fusion | bytes 396288 | tf_op jit(solution)/shard_map/gather | solution.py:150
  42.5 1.0 %reshape.550 = f32[64,6,128]{2,1,0:T(8,128)} reshape(f32[384,2,64]{2,1,0:T(2,128)S(1)} %gather_fusion) | data formatting | bytes 393216 | tf_op jit(solution)/shard_map/reshape | solution.py:150
  43.4 5.7 %all-to-all-start.1 = ((f32[64,6,128]{2,1,0:T(8,128)}), f32[64,6,128]{2,1,0:T(8,128)S(1)}, u32[]{:S(2)}, u32[]{:S(2)}) async-start(f32[64,6,128]{2,1,0:T(8,128)} %reshape.550), calls=%async_computation.1 | async-start | bytes 524288 | tf_op jit(solution)/shard_map/all_to_all | solution.py:155
  49.1 1.2 %compare_convert_fusion = f32[4]{0:T(128)} fusion(s32[]{:T(128)} %fusion.139), kind=kLoop, calls=%fused_computation.258 | loop fusion | flops 8 | bytes 20 | tf_op jit(solution)/shard_map/convert_element_type | solution.py:198
  51.8 0.8 copy.43
  53.3 1.3 %gather_fusion.2 = f32[128,2,512]{2,1,0:T(2,128)S(1)} fusion(f32[4,2,64,512]{3,1,2,0:T(2,128)S(1)} %copy.43, s32[128]{0:T(128)S(1)} %reshape.565), kind=kCustom, calls=%fused_computation.2 | custom fusion | bytes 1049600 | tf_op jit(solution)/shard_map/gather | solution.py:151
  54.5 1.4 %reshape.552 = f32[64,2,1024]{2,1,0:T(2,128)} reshape(f32[128,2,512]{2,1,0:T(2,128)S(1)} %gather_fusion.2) | data formatting | bytes 1048576 | tf_op jit(solution)/shard_map/reshape | solution.py:153
  56.0 5.1 %all-to-all-done.1 = f32[64,6,128]{2,1,0:T(8,128)S(1)} async-done(((f32[64,6,128]{2,1,0:T(8,128)}), f32[64,6,128]{2,1,0:T(8,128)S(1)}, u32[]{:S(2)}, u32[]{:S(2)}) %all-to-all-start.1) | async-done | bytes 196640 | tf_op jit(solution)/shard_map/all_to_all | solution.py:155
  61.1 6.0 %all-to-all-start.2 = ((f32[64,2,1024]{2,1,0:T(2,128)}), f32[64,2,1024]{2,1,0:T(2,128)S(1)}, u32[]{:S(2)}, u32[]{:S(2)}) async-start(f32[64,2,1024]{2,1,0:T(2,128)} %reshape.552), calls=%async_computation.2 | async-start | bytes 1048576 | tf_op jit(solution)/shard_map/all_to_all | solution.py:156
  67.5 9.2 %fusion.18 = f32[4,2,64,512]{3,2,1,0:T(8,128)S(1)} fusion(f32[4,2,64,512]{3,2,1,0:T(8,128)S(1)} %multiply_add_fusion, f32[4,2,8,512]{3,2,1,0:T(8,128)} %collective-permute-done.1, f32[4,2,8,512]{3,2,1,0:T(8,128)} %collective-permute-done, f32[512]{0:T(512)S(1)} %bitcast.146, f32[512]{0:T(512)S(1)} %bitcast.154, f32[512]{0:T(512)S(1)} %bitcast.145, ...), kind=kLoop, calls=%fused_computation.62 | loop fusion | flops 21757952 | bytes 2398464 | tf_op jit(solution)/shard_map/sub | solution.py:165
  77.0 3.6 %gather_fusion.1 = f32[384,128]{1,0:T(8,128)S(1)} fusion(f32[64,6,128]{2,0,1:T(8,128)S(1)} %copy.39, s32[384]{0:T(512)S(1)} %get-tuple-element.13), kind=kCustom, calls=%fused_computation.1 | custom fusion | bytes 396288 | tf_op jit(solution)/shard_map/gather | solution.py:158
  81.8 2.6 %all-to-all-done.2 = f32[64,2,1024]{2,1,0:T(2,128)S(1)} async-done(((f32[64,2,1024]{2,1,0:T(2,128)}), f32[64,2,1024]{2,1,0:T(2,128)S(1)}, u32[]{:S(2)}, u32[]{:S(2)}) %all-to-all-start.2) | async-done | bytes 524320 | tf_op jit(solution)/shard_map/all_to_all | solution.py:156
  84.4 4.8 %gather_fusion.3 = f32[384,1024]{1,0:T(8,128)S(1)} fusion(f32[64,2,1024]{2,1,0:T(2,128)S(1)} %all-to-all-done.2, s32[384]{0:T(512)S(1)} %get-tuple-element.12), kind=kCustom, calls=%fused_computation.3 | custom fusion | bytes 3148800 | tf_op jit(solution)/shard_map/gather | solution.py:161
  89.8 0.8 copy-done
  90.9 2.3 %add_multiply_fusion = (f32[4,2,64,512]{3,2,1,0:T(8,128)}, f32[4,2,64,512]{3,2,1,0:T(8,128)}) fusion(f32[4,2,64,512]{3,2,1,0:T(8,128)S(1)} %copy-done, f32[4,2,64,512]{3,2,1,0:T(8,128)S(1)} %copy-done.1, f32[4]{0:T(128)S(1)} %copy-done.61, f32[4,2,64,512]{3,2,1,0:T(8,128)S(1)} %convolution_add_fusion, s32[4,96]{1,0:T(4,128)S(1)} %copy-done.29, ...), kind=kOutput, calls=%fused_computation.138 | convolution fusion | flops 304242688 | bytes 6817296 | tf_op jit(solution)/shard_map/gkr,gkcl->gcrl/dot_general | solution.py:197
  (189 shorter events, 13.1 us)
Async XLA Ops:
  2.5 27.8 %copy-start.4 = (f32[9,512]{1,0:T(8,128)S(1)}, f32[9,512]{1,0:T(8,128)}, u32[]{:S(2)}) copy-start(f32[9,512]{1,0:T(8,128)} %param.15) | copy-start | bytes 55300
  3.2 63.9 %collective-permute-start.1 = (f32[4,2,8,512]{3,2,1,0:T(8,128)}, f32[4,2,8,512]{3,2,1,0:T(8,128)}, u32[]{:S(2)}, u32[]{:S(2)}) collective-permute-start(f32[4,2,8,512]{3,2,1,0:T(8,128)} %get-tuple-element.24), channel_id=1, source_target_pairs={{0,1},{1,2},{2,3},{3,4},{4,5},{5,6},{6,7},{8,9},{9,10},{10,11},{11... | collective-permute-start | bytes 393224 | tf_op jit(solution)/shard_map/ppermute | solution.py:14
  7.9 59.3 %collective-permute-start = (f32[4,2,8,512]{3,2,1,0:T(8,128)}, f32[4,2,8,512]{3,2,1,0:T(8,128)}, u32[]{:S(2)}, u32[]{:S(2)}) collective-permute-start(f32[4,2,8,512]{3,2,1,0:T(8,128)} %get-tuple-element.23), channel_id=1, source_target_pairs={{1,0},{2,1},{3,2},{4,3},{5,4},{6,5},{7,6},{9,8},{10,9},{11,10},{12... | collective-permute-start | bytes 393224 | tf_op jit(solution)/shard_map/ppermute | solution.py:17
  10.8 23.9 %copy-start.38 = (pred[384]{0:T(512)(128)(4,1)}, pred[384]{0:T(512)(128)(4,1)S(1)}, u32[]{:S(2)}) copy-start(pred[384]{0:T(512)(128)(4,1)S(1)} %fusion.128) | copy-start | bytes 1156
  13.5 21.3 %copy-start.19 = (s32[384]{0:T(512)}, s32[384]{0:T(512)S(1)}, u32[]{:S(2)}) copy-start(s32[384]{0:T(512)S(1)} %get-tuple-element.6) | copy-start | bytes 4612
  13.5 21.3 %copy-start.21 = (s32[384]{0:T(512)}, s32[384]{0:T(512)S(1)}, u32[]{:S(2)}) copy-start(s32[384]{0:T(512)S(1)} %get-tuple-element.7) | copy-start | bytes 4612
  15.9 23.5 %all-to-all-start = ((s32[64,1,16]{2,1,0:T(1,128)}), s32[64,1,16]{2,1,0:T(1,128)S(1)}, u32[]{:S(2)}, u32[]{:S(2)}) async-start(s32[64,1,16]{2,1,0:T(1,128)} %bitcast.40), calls=%async_computation | async-start | bytes 65536 | tf_op jit(solution)/shard_map/all_to_all | solution.py:25
  43.4 17.7 %all-to-all-start.1 = ((f32[64,6,128]{2,1,0:T(8,128)}), f32[64,6,128]{2,1,0:T(8,128)S(1)}, u32[]{:S(2)}, u32[]{:S(2)}) async-start(f32[64,6,128]{2,1,0:T(8,128)} %reshape.550), calls=%async_computation.1 | async-start | bytes 524288 | tf_op jit(solution)/shard_map/all_to_all | solution.py:155
  52.9 14.2 %copy-start.6 = (f32[1,512]{1,0:T(1,128)S(1)}, f32[1,512]{1,0:T(1,128)}, u32[]{:S(2)}) copy-start(f32[1,512]{1,0:T(1,128)} %copy-done.5) | copy-start | bytes 6148
  53.0 14.2 %copy-start.8 = (f32[1,512]{1,0:T(1,128)S(1)}, f32[1,512]{1,0:T(1,128)}, u32[]{:S(2)}) copy-start(f32[1,512]{1,0:T(1,128)} %copy-done.7) | copy-start | bytes 6148
  53.0 14.2 %copy-start.10 = (f32[1,512]{1,0:T(1,128)S(1)}, f32[1,512]{1,0:T(1,128)}, u32[]{:S(2)}) copy-start(f32[1,512]{1,0:T(1,128)} %copy-done.9) | copy-start | bytes 6148
  53.0 14.2 %copy-start.12 = (f32[1,512]{1,0:T(1,128)S(1)}, f32[1,512]{1,0:T(1,128)}, u32[]{:S(2)}) copy-start(f32[1,512]{1,0:T(1,128)} %copy-done.11) | copy-start | bytes 6148
  53.0 14.2 %copy-start.14 = (f32[1,512]{1,0:T(1,128)S(1)}, f32[1,512]{1,0:T(1,128)}, u32[]{:S(2)}) copy-start(f32[1,512]{1,0:T(1,128)} %copy-done.13) | copy-start | bytes 6148
  53.0 14.2 %copy-start.16 = (f32[1,512]{1,0:T(1,128)S(1)}, f32[1,512]{1,0:T(1,128)}, u32[]{:S(2)}) copy-start(f32[1,512]{1,0:T(1,128)} %copy-done.15) | copy-start | bytes 6148
  53.0 14.2 %copy-start.18 = (f32[1,512]{1,0:T(1,128)S(1)}, f32[1,512]{1,0:T(1,128)}, u32[]{:S(2)}) copy-start(f32[1,512]{1,0:T(1,128)} %copy-done.17) | copy-start | bytes 6148
  53.0 14.2 %copy-start.30 = (f32[1,512]{1,0:T(1,128)S(1)}, f32[1,512]{1,0:T(1,128)}, u32[]{:S(2)}) copy-start(f32[1,512]{1,0:T(1,128)} %get-tuple-element.52) | copy-start | bytes 6148
  53.0 14.2 %copy-start.31 = (f32[1,512]{1,0:T(1,128)S(1)}, f32[1,512]{1,0:T(1,128)}, u32[]{:S(2)}) copy-start(f32[1,512]{1,0:T(1,128)} %get-tuple-element.53) | copy-start | bytes 6148
  53.0 14.2 %copy-start.32 = (f32[1,512]{1,0:T(1,128)S(1)}, f32[1,512]{1,0:T(1,128)}, u32[]{:S(2)}) copy-start(f32[1,512]{1,0:T(1,128)} %get-tuple-element.54) | copy-start | bytes 6148
  53.0 14.2 %copy-start.33 = (f32[1,512]{1,0:T(1,128)S(1)}, f32[1,512]{1,0:T(1,128)}, u32[]{:S(2)}) copy-start(f32[1,512]{1,0:T(1,128)} %get-tuple-element.55) | copy-start | bytes 6148
  53.1 14.2 %copy-start.34 = (f32[1,512]{1,0:T(1,128)S(1)}, f32[1,512]{1,0:T(1,128)}, u32[]{:S(2)}) copy-start(f32[1,512]{1,0:T(1,128)} %get-tuple-element.56) | copy-start | bytes 6148
  53.1 14.2 %copy-start.35 = (f32[1,512]{1,0:T(1,128)S(1)}, f32[1,512]{1,0:T(1,128)}, u32[]{:S(2)}) copy-start(f32[1,512]{1,0:T(1,128)} %get-tuple-element.57) | copy-start | bytes 6148
  53.1 14.2 %copy-start.36 = (f32[1,512]{1,0:T(1,128)S(1)}, f32[1,512]{1,0:T(1,128)}, u32[]{:S(2)}) copy-start(f32[1,512]{1,0:T(1,128)} %get-tuple-element.59) | copy-start | bytes 6148
  56.0 20.7 %copy-start.58 = (f32[4]{0:T(128)S(1)}, f32[4]{0:T(128)}, u32[]{:S(2)}) copy-start(f32[4]{0:T(128)} %get-tuple-element.17) | copy-start | bytes 52
  61.1 23.3 %all-to-all-start.2 = ((f32[64,2,1024]{2,1,0:T(2,128)}), f32[64,2,1024]{2,1,0:T(2,128)S(1)}, u32[]{:S(2)}, u32[]{:S(2)}) async-start(f32[64,2,1024]{2,1,0:T(2,128)} %reshape.552), calls=%async_computation.2 | async-start | bytes 1048576 | tf_op jit(solution)/shard_map/all_to_all | solution.py:156
  (45 other events, 378.3 us)
where the time goes:
time: 94.9 us; the launch traced here: 93.3 us
  starting transfers between devices  32 us (34%)
  local copies, waits for them, and re-layouts  24.2 us (26%)
  other arithmetic  19.9 us (21%)
  waiting for transfers between devices  12.3 us (13%)
  matrix products  3.07 us (3%)
  between operations  1.84 us (2%)
    all_to_all x1, starting transfers between devices, in_one_piece(): lax.all_to_all(both, axis, split_axis=split_dim, concat_axis=concat_dim,...  14.3 us
    sub x1, other arithmetic, shards(): band_rows(padded, upper_local, lower_local, band_width)  9.15 us
    all_to_all x1, starting transfers between devices, shards(): lax.all_to_all(answer_rows, 'tier', split_axis=0, concat_axis=0, tiled=True)  6.04 us
    all_to_all x1, starting transfers between devices, shards(): lax.all_to_all(answer_cols, 'tier', split_axis=0, concat_axis=0, tiled=True)  5.7 us
    all_to_all x1, waiting for transfers between devices, shards(): lax.all_to_all(answer_cols, 'tier', split_axis=0, concat_axis=0, tiled=True)  5.12 us
    gather x1, local copies, waits for them, and re-layouts, shards(): back_rows[safe_holder, safe_position]  4.77 us
    ppermute x1, starting transfers between devices, padded_2(): lax.ppermute(lax.slice_in_dim(block, block.shape[dim] - width, None, axis...  4.68 us
    all_to_all x1, waiting for transfers between devices, in_one_piece(): lax.all_to_all(both, axis, split_axis=split_dim, concat_axis=concat_dim,...  4.63 us
  transfers between devices with their start and end apart: 5, of which 3 were waited for; matrix products, arithmetic and copies ran while one was open for 38% of the time, Pallas kernels for 0%

commit v1 on v0

v1 whole, which is shorter than its diff:
```python
import functools

import jax
import jax.numpy as jnp
from jax import lax
from jax.experimental import pallas as pl
from jax.experimental.pallas import tpu as pltpu
from jax.sharding import PartitionSpec as P

step_size = 0.05
LANES = 128
vmem_limit = 16 * 1024 * 1024
BF16 = jnp.bfloat16
F32 = jnp.float32
VMEM = pl.BlockSpec(memory_space=pltpu.VMEM)
SMEM = pl.BlockSpec(memory_space=pltpu.SMEM)
ANY = pl.BlockSpec(memory_space=pl.ANY)


def iota(shape, dim):
    return lax.broadcasted_iota(jnp.int32, shape, dim)


def round_up(value, multiple):
    return -(-value // multiple) * multiple


def dot_nn(a, b):
    return lax.dot_general(a, b, (((1,), (0,)), ((), ())), preferred_element_type=F32)


def dot_nt(a, b):
    return lax.dot_general(a, b, (((1,), (1,)), ((), ())), preferred_element_type=F32)


def dot_tn(a, b):
    return lax.dot_general(a, b, (((0,), (0,)), ((), ())), preferred_element_type=F32)


def thirds(x):
    first = x.astype(BF16)
    rest = x - first.astype(F32)
    second = rest.astype(BF16)
    third = (rest - second.astype(F32)).astype(BF16)
    return first, second, third


def picked(chooser, values):
    first, second, third = thirds(values)
    return dot_nn(chooser, first) + (dot_nn(chooser, second) + dot_nn(chooser, third))


def as_bf16(mask):
    return jnp.where(mask, 1.0, 0.0).astype(BF16)


def as_column(row, size):
    diagonal = iota((size, size), 0) == iota((size, size), 1)
    return jnp.sum(jnp.where(diagonal, row, jnp.zeros((), row.dtype)), axis=1, keepdims=True)


class Sizes:
    def __init__(self, state, links, h_bands, tiers, parts):
        self.slots = state.shape[0]
        self.rows = state.shape[2]
        self.levels = state.shape[3]
        self.band = h_bands.shape[0] - 1
        self.per_slot = links.shape[2]
        self.tiers = tiers
        self.parts = parts
        self.modes = self.per_slot // 2
        self.block_modes = self.modes // parts
        total = self.slots * self.per_slot
        self.cap = total // tiers
        self.row_cap = 2 * ((self.slots * self.block_modes + tiers - 1) // tiers)
        self.lane_tiles = 2 * self.levels // LANES
        self.message = self.cap + self.row_cap * self.lane_tiles
        self.ask = round_up(2 * self.cap, 16)
        self.shift = self.slots.bit_length() - 1
        self.row_pad = round_up(self.slots * self.block_modes, 16)
        self.group = round_up(self.block_modes, 8)


def holders_of(z, links_ref, g):
    neighbour = links_ref[0, g : g + 1, :]
    holder = lax.shift_right_logical(neighbour, z.shift)
    target = lax.bitwise_and(neighbour, z.slots - 1)
    hit = holder == iota((z.tiers, z.per_slot), 0)
    return hit, holder, target


def earlier_table(size):
    return as_bf16(iota((size, size), 0) < iota((size, size), 1))


def rank_of(hit, seen, earlier):
    before = dot_nn(as_bf16(hit), earlier) + seen
    return jnp.sum(jnp.where(hit, before, 0.0), axis=0, keepdims=True).astype(jnp.int32)


def ask_kernel(z, links_ref, out_ref):
    earlier = earlier_table(z.per_slot)
    ones = jnp.ones((z.per_slot, z.per_slot), BF16)
    seen = jnp.zeros((z.tiers, z.per_slot), F32)
    table = jnp.zeros((z.tiers, z.ask), F32)
    field = iota((z.ask, z.per_slot), 0)
    for g in range(z.slots):
        hit, _, target = holders_of(z, links_ref, g)
        mode = links_ref[1, g : g + 1, :]
        rank = rank_of(hit, seen, earlier)
        value = jnp.where(lax.bitwise_and(field, 1) == 0, target, mode)
        value = jnp.where(lax.shift_right_logical(field, 1) == rank, value, 0)
        chosen = as_bf16(hit)
        table = table + dot_nt(chosen, value.astype(F32).astype(BF16))
        seen = seen + dot_nn(chosen, ones)
    out_ref[...] = table.astype(jnp.int32)


def table_kernel(z, state_ref, slope_ref, sites_ref, mid_ref, low_ref, high_ref, col_ref, row_ref, rows_scr, site_scr):
    part = lax.axis_index("sys")
    span = z.slots * z.modes
    site_scr[...] = jnp.zeros_like(site_scr)
    lane = iota((1, z.levels), 1)
    for k in range(z.modes):
        site_scr[k : k + 1, :] = jnp.where(lane == sites_ref[k], 1.0, 0.0)
    at_site = site_scr[: z.modes, :].astype(BF16)
    rows_scr[...] = jnp.zeros_like(rows_scr)
    for g in range(z.slots):
        mid = state_ref[g] + (0.5 * step_size) * slope_ref[g]
        mid_ref[g] = mid
        for third, values in enumerate(thirds(mid)):
            at = third * span + g * z.modes
            col_ref[at : at + z.modes, :] = dot_nt(at_site, values).astype(BF16)
        for c in range(2):
            start = c * z.rows
            low_ref[g, c] = mid_ref[g, start : start + z.band, :]
            high_ref[g, c] = mid_ref[g, start + z.rows - z.band : start + z.rows, :]
            for k in range(z.block_modes):
                local = sites_ref[part * z.block_modes + k] - part * z.rows
                at = g * z.block_modes + k
                rows_scr[at : at + 1, c * z.levels : (c + 1) * z.levels] = mid_ref[
                    g, pl.ds(start + local, 1), :
                ]
    for third, values in enumerate(thirds(rows_scr[...])):
        row_ref[third * z.row_pad : (third + 1) * z.row_pad, :] = values


def answer_kernel(z, ask_ref, col_ref, row_ref, out_ref):
    part = lax.axis_index("sys")
    span = z.slots * z.modes
    low = part * z.block_modes
    asked = ask_ref[...]
    columns = []
    row_at = [jnp.full((z.tiers, 1), -1, jnp.int32) for _ in range(z.row_cap)]
    used = jnp.zeros((z.tiers, 1), jnp.int32)
    for p in range(z.cap):
        target = asked[:, 2 * p : 2 * p + 1]
        mode = asked[:, 2 * p + 1 : 2 * p + 2]
        columns.append(as_bf16(target * z.modes + mode == iota((z.tiers, span), 1)))
        inside = jnp.logical_and(mode >= low, mode < low + z.block_modes)
        where_row = target * z.block_modes + (mode - low)
        for j in range(z.row_cap):
            take = jnp.logical_and(inside, used == j)
            row_at[j] = jnp.where(take, where_row, row_at[j])
        used = used + jnp.where(inside, 1, 0)
    chosen = jnp.concatenate(columns, axis=0)
    found = dot_nn(chosen, col_ref[:span, :])
    for third in (1, 2):
        found = found + dot_nn(chosen, col_ref[third * span : (third + 1) * span, :])
    for p in range(z.cap):
        out_ref[pl.ds(p, z.tiers, stride=z.message), :] = found[p * z.tiers : (p + 1) * z.tiers, :]
    lanes = iota((z.tiers, z.row_pad), 1)
    chosen = jnp.concatenate([as_bf16(at == lanes) for at in row_at], axis=0)
    found = dot_nn(chosen, row_ref[: z.row_pad, :])
    for third in (1, 2):
        found = found + dot_nn(chosen, row_ref[third * z.row_pad : (third + 1) * z.row_pad, :])
    for j in range(z.row_cap):
        for t in range(z.lane_tiles):
            at = z.cap + j * z.lane_tiles + t
            out_ref[pl.ds(at, z.tiers, stride=z.message), :] = found[
                j * z.tiers : (j + 1) * z.tiers, t * LANES : (t + 1) * LANES
            ]


def choose_kernel(
    z, links_ref, counts_ref, coef_ref, rate_ref, col_ref, row_ref, col_coef_ref, row_coef_ref, damp_ref
):
    part = lax.axis_index("sys")
    low = part * z.block_modes
    earlier = earlier_table(z.per_slot)
    ones = jnp.ones((z.per_slot, z.per_slot), BF16)
    seen = jnp.zeros((z.tiers, z.per_slot), F32)
    seen_rows = jnp.zeros((z.tiers, z.per_slot), F32)
    counts = as_column(counts_ref[...], z.tiers)
    rate = as_column(rate_ref[...], z.modes)
    coefs = [as_column(coef_ref[c : c + 1, :], z.modes) for c in range(2)]
    total = z.slots * z.modes
    for g in range(z.slots):
        hit, holder, target = holders_of(z, links_ref, g)
        mode = links_ref[1, g : g + 1, :]
        kind = links_ref[2, g : g + 1, :]
        level = links_ref[3, g : g + 1, :]
        rank = rank_of(hit, seen, earlier)
        seen = seen + dot_nn(as_bf16(hit), ones)
        inside = jnp.logical_and(mode >= low, mode < low + z.block_modes)
        hit_rows = jnp.logical_and(hit, inside)
        row_rank = rank_of(hit_rows, seen_rows, earlier)
        seen_rows = seen_rows + dot_nn(as_bf16(hit_rows), ones)
        live = target < jnp.sum(jnp.where(hit, counts, 0), axis=0, keepdims=True)
        scale = jnp.where(kind == 1, level, 1)
        here = as_bf16(iota((z.cap * z.tiers, z.per_slot), 0) == rank * z.tiers + holder)
        here_row = as_bf16(
            iota((z.row_cap * z.tiers, z.per_slot), 0) == row_rank * z.tiers + holder
        )
        modes = iota((z.modes, z.per_slot), 0)
        group = iota((z.group, z.per_slot), 0)
        for way in range(2):
            wanted = jnp.logical_and(kind == way, live)
            chosen = jnp.where(jnp.logical_and(modes == mode, wanted), scale, 0)
            at = way * total + g * z.modes
            col_ref[at : at + z.modes, :] = dot_nt(
                chosen.astype(F32).astype(BF16), here
            ).astype(BF16)
            own = jnp.logical_and(group + low == mode, jnp.logical_and(inside, wanted))
            at = (way * z.slots + g) * z.group
            row_ref[at : at + z.group, :] = dot_nt(
                jnp.where(own, scale, 0).astype(F32).astype(BF16), here_row
            )
        falling = jnp.where(jnp.logical_and(modes == mode, kind == 1), level, 0).astype(F32)
        amount = jnp.sum(falling, axis=1, keepdims=True) * rate
        damp_ref[g] = jnp.broadcast_to(jnp.sum(amount, axis=0, keepdims=True), (8, LANES))
        for c in range(2):
            col_coef_ref[c, g * z.modes : (g + 1) * z.modes, :] = jnp.broadcast_to(
                coefs[c], (z.modes, LANES)
            )
            mine = jnp.where(
                iota((z.group, z.modes), 0) + low == iota((z.group, z.modes), 1),
                coef_ref[c : c + 1, :],
                0.0,
            )
            mine = jnp.where(iota((z.group, z.modes), 0) < z.block_modes, mine, 0.0)
            row_coef_ref[c, g * z.group : (g + 1) * z.group, :] = jnp.broadcast_to(
                jnp.sum(mine, axis=1, keepdims=True), (z.group, LANES)
            )


def band_kernel(z, mid_ref, low_ref, high_ref, bands_ref, damp_ref, out_ref, wide, spread, across_ref):
    part = lax.axis_index("sys")
    taps = 2 * z.band + 1
    across_ref[...] = jnp.zeros_like(across_ref)
    lane = iota((1, z.levels), 1)
    for t in range(taps):
        offset = t - z.band
        row = bands_ref[abs(offset) : abs(offset) + 1, :]
        if offset < 0:
            row = jnp.where(lane >= -offset, pltpu.roll(row, -offset, 1), 0.0)
        elif offset > 0:
            row = jnp.where(lane < z.levels - offset, row, 0.0)
        across_ref[t : t + 1, :] = row
    own = iota((z.rows, z.levels), 0) + part * z.rows == iota((z.rows, z.levels), 1)
    own = as_bf16(own)
    down = jnp.zeros((z.rows, across_ref.shape[0]), F32)
    for values in thirds(across_ref[...]):
        down = down + dot_nt(own, values)
    for t in range(taps):
        spread[t] = jnp.broadcast_to(down[:, t : t + 1], (z.rows, LANES))
    tiles = z.levels // LANES
    for g in range(z.slots):
        damp = damp_ref[g, 0:1, 0:1]
        for c in range(2):
            field = mid_ref[g, c * z.rows : (c + 1) * z.rows, :]
            wide[0 : z.band, :] = low_ref[g, c]
            wide[z.band : z.band + z.rows, :] = field
            wide[z.band + z.rows :, :] = high_ref[g, c]
            summed = across_ref[z.band : z.band + 1, :] * field
            for t in range(taps):
                if t != z.band:
                    moved = pltpu.roll(field, (z.band - t) % z.levels, 1)
                    summed = summed + across_ref[t : t + 1, :] * moved
            sides = []
            for q in range(tiles):
                lanes = slice(q * LANES, (q + 1) * LANES)
                total = spread[0] * wide[0 : z.rows, lanes]
                for t in range(1, taps):
                    total = total + spread[t] * wide[t : t + z.rows, lanes]
                sides.append(total)
            commuted = jnp.concatenate(sides, axis=1) - summed
            other = 1 - c
            sign = 1.0 if c == 1 else -1.0
            mine = mid_ref[g, other * z.rows : (other + 1) * z.rows, :]
            out_ref[g, other * z.rows : (other + 1) * z.rows, :] = sign * commuted - damp * mine


def apply_kernel(
    z, got_ref, col_ref, row_ref, col_coef_ref, row_coef_ref, deriv_ref, state_ref, slope_ref,
    counts_ref, sites_ref, next_ref, sum_ref, site_scr, next_scr, sum_scr, sem,
):
    part = lax.axis_index("sys")
    tier = lax.axis_index("tier")
    lane = iota((1, z.levels), 1)
    for k in range(z.modes):
        site_scr[k : k + 1, :] = jnp.where(lane == sites_ref[k], 1.0, 0.0)
    at_site = site_scr[: z.modes, :].astype(BF16)
    total = z.slots * z.modes
    pieces = jnp.concatenate(
        [got_ref[pl.ds(p, z.tiers, stride=z.message), :] for p in range(z.cap)], axis=0
    )
    found = picked(col_ref[...], pieces)
    up, down = found[:total], found[total:]
    sign = jnp.where(iota((1, 2 * z.rows), 1) < z.rows, -1.0, 1.0)
    cols = col_coef_ref[1] * down + sign * pltpu.roll(up + col_coef_ref[0] * down, z.rows, 1)
    pieces = jnp.concatenate(
        [
            jnp.concatenate(
                [
                    got_ref[pl.ds(z.cap + j * z.lane_tiles + t, z.tiers, stride=z.message), :]
                    for t in range(z.lane_tiles)
                ],
                axis=1,
            )
            for j in range(z.row_cap)
        ],
        axis=0,
    )
    found = picked(row_ref[...].astype(BF16), pieces)
    half = z.slots * z.group
    up, down = found[:half], found[half:]
    turned = up + row_coef_ref[0, :, 0:1] * down
    straight = row_coef_ref[1, :, 0:1] * down
    rows = (
        straight[:, : z.levels] + turned[:, z.levels :],
        straight[:, z.levels :] - turned[:, : z.levels],
    )
    for g in range(z.slots):
        mine = cols[g * z.modes : (g + 1) * z.modes, :]
        added = deriv_ref[g]
        for values in thirds(mine):
            added = added + dot_tn(values, at_site)
        next_scr[g] = added
        for k in range(z.block_modes):
            local = sites_ref[part * z.block_modes + k] - part * z.rows
            for c in range(2):
                at = pl.ds(c * z.rows + local, 1)
                next_scr[g, at, :] = (
                    next_scr[g, at, :] + rows[c][g * z.group + k : g * z.group + k + 1, :]
                )
        live = jnp.where(g < counts_ref[tier], 1.0, 0.0)
        slope_next = next_scr[g] * live
        next_scr[g] = slope_next
        sum_scr[g] = (
            state_ref[g] + (step_size / 6.0) * slope_ref[g] + (step_size / 3.0) * slope_next
        ) * live
        pltpu.make_async_copy(next_scr.at[g], next_ref.at[g], sem.at[0, g]).start()
        pltpu.make_async_copy(sum_scr.at[g], sum_ref.at[g], sem.at[1, g]).start()
    for g in range(z.slots):
        pltpu.make_async_copy(next_scr.at[g], next_ref.at[g], sem.at[0, g]).wait()
        pltpu.make_async_copy(sum_scr.at[g], sum_ref.at[g], sem.at[1, g]).wait()


def call(kernel, z, name, args, in_specs, outs, scratch=(), out_specs=None, micros=1):
    return pl.pallas_call(
        functools.partial(kernel, z),
        out_shape=outs,
        in_specs=in_specs,
        out_specs=[VMEM] * len(outs) if out_specs is None else out_specs,
        scratch_shapes=list(scratch),
        name=name,
        compiler_params=pltpu.CompilerParams(vmem_limit_bytes=vmem_limit),
        cost_estimate=pl.CostEstimate(
            flops=int(micros * 1e6), bytes_accessed=int(micros * 1e5), transcendentals=0
        ),
    )(*args)


def neighbours(low_edge, high_edge):
    count = lax.axis_size("sys")
    forward = [(i, i + 1) for i in range(count - 1)]
    backward = [(target, source) for source, target in forward]
    return lax.ppermute(high_edge, "sys", forward), lax.ppermute(low_edge, "sys", backward)


def shards(state, slope, counts, links, mode_site, mode_coef, mode_rate, h_bands):
    z = Sizes(state, links, h_bands, lax.axis_size("tier"), lax.axis_size("sys"))
    shape = jax.ShapeDtypeStruct
    flat = (z.slots, 2 * z.rows, z.levels)
    state_flat = state.reshape(flat)
    slope_flat = slope.reshape(flat)
    (ask,) = call(
        ask_kernel, z, "ask", (links,), [VMEM], [shape((z.tiers, z.ask), jnp.int32)]
    )
    asked = lax.all_to_all(
        ask.reshape(z.tiers, 1, z.ask), "tier", split_axis=0, concat_axis=0, tiled=True
    ).reshape(z.tiers, z.ask)
    edge = (z.slots, 2, z.band, z.levels)
    mid, low_edge, high_edge, col_table, row_table = call(
        table_kernel,
        z,
        "tables",
        (state_flat, slope_flat, mode_site),
        [VMEM, VMEM, SMEM],
        [
            shape(flat, F32),
            shape(edge, F32),
            shape(edge, F32),
            shape((3 * z.slots * z.modes, 2 * z.rows), BF16),
            shape((3 * z.row_pad, 2 * z.levels), BF16),
        ],
        [
            pltpu.VMEM((z.row_pad, 2 * z.levels), F32),
            pltpu.VMEM((round_up(z.modes, 16), z.levels), F32),
        ],
        micros=3,
    )
    (answer,) = call(
        answer_kernel,
        z,
        "answer",
        (asked, col_table, row_table),
        [VMEM] * 3,
        [shape((z.tiers * z.message, LANES), F32)],
    )
    got = lax.all_to_all(
        answer.reshape(z.tiers, 1, z.message * LANES),
        "tier",
        split_axis=0,
        concat_axis=0,
        tiled=True,
    ).reshape(z.tiers * z.message, LANES)
    low_edge, high_edge, answer_kept = lax.optimization_barrier((low_edge, high_edge, answer))
    above, below = neighbours(low_edge, high_edge)
    col_choice, row_choice, col_coef, row_coef, damp = call(
        choose_kernel,
        z,
        "choose",
        (links, counts[None], mode_coef, mode_rate[None]),
        [VMEM] * 4,
        [
            shape((2 * z.slots * z.modes, z.cap * z.tiers), BF16),
            shape((2 * z.slots * z.group, z.row_cap * z.tiers), F32),
            shape((2, z.slots * z.modes, LANES), F32),
            shape((2, z.slots * z.group, LANES), F32),
            shape((z.slots, 8, LANES), F32),
        ],
        micros=2,
    )
    (deriv,) = call(
        band_kernel,
        z,
        "band",
        (mid, above, below, h_bands, damp),
        [VMEM] * 5,
        [shape(flat, F32)],
        [
            pltpu.VMEM((z.rows + 2 * z.band, z.levels), F32),
            pltpu.VMEM((2 * z.band + 1, z.rows, LANES), F32),
            pltpu.VMEM((round_up(2 * z.band + 1, 16), z.levels), F32),
        ],
        micros=5,
    )
    slope_next, partial_sum = call(
        apply_kernel,
        z,
        "apply",
        (
            got, col_choice, row_choice, col_coef, row_coef, deriv, state_flat, slope_flat,
            counts, mode_site,
        ),
        [VMEM] * 8 + [SMEM] * 2,
        [shape(flat, F32), shape(flat, F32)],
        [
            pltpu.VMEM((round_up(z.modes, 8), z.levels), F32),
            pltpu.VMEM(flat, F32),
            pltpu.VMEM(flat, F32),
            pltpu.SemaphoreType.DMA((2, z.slots)),
        ],
        out_specs=[ANY, ANY],
        micros=4,
    )
    return slope_next.reshape(state.shape), partial_sum.reshape(state.shape)


def solution(mesh):
    in_specs = (
        P("tier", None, "sys", None),
        P("tier", None, "sys", None),
        P(),
        P(None, "tier", None),
        P(),
        P(),
        P(),
        P(),
    )
    out_specs = (P("tier", None, "sys", None), P("tier", None, "sys", None))
    return jax.shard_map(shards, mesh=mesh, in_specs=in_specs, out_specs=out_specs, check_vma=False)
```

time: 94.9 us -> 61.9 us (0.65); the launches traced: 93.3 us -> 61.3 us
  other arithmetic: 19.9 us -> 0 us
  local copies, waits for them, and re-layouts: 24.2 us -> 8.27 us
  Pallas kernels: 0 us -> 14.8 us
  starting transfers between devices: 32 us -> 26.1 us
  matrix products: 3.07 us -> 0 us
  between operations: 1.84 us -> 0.75 us
    pallas_call x0 -> x6, Pallas kernels: none -> 14.8 us  [call(): pl.pallas_call(functools.partial(kernel, z), out_shape=outs, in_specs=in_...]
    gather x5 -> x0, local copies, waits for them, and re-layouts: 12 us -> none  [the longest x1 4.77 us: shards(): back_rows[safe_holder, safe_position]]
    sub x2 -> x0, other arithmetic: 9.41 us -> none  [the longest x1 9.15 us: shards(): band_rows(padded, upper_local, lower_local, band_width)]
    unnamed x128 -> x30, local copies, waits for them, and re-layouts: 1.95 us -> 8.27 us
    all_to_all x3 -> x2, starting transfers between devices: 26 us -> 21.6 us  [the longest x1 14.8 us: shards(): lax.all_to_all(ask.reshape(z.tiers, 1, z.ask), 'tier', split_axis=0, conc...]
    all_to_all x3 -> x2, waiting for transfers between devices: 12.3 us -> 9.02 us  [the longest x1 5.2 us: shards(): lax.all_to_all(answer.reshape(z.tiers, 1, z.message * LANES), 'tier', spl...]
    dot_general x2 -> x0, matrix products: 3.07 us -> none  [the longest x1 2.35 us: shards(): jnp.einsum('gkr,gkcl->gcrl', row_table, row_pair, precision=lax.Precision...]
    reshape x6 -> x0, local copies, waits for them, and re-layouts: 2.91 us -> none  [the longest x1 1.42 us: shards(): answer_rows = midpoint[got_row_slot, :, jnp.clip(got_row_site - row_start...]
  transfers between devices with their start and end apart: 5 -> 4, of which waited for: 3 -> 3; matrix products, arithmetic and copies ran while one was open for 38% -> 0% of each run, Pallas kernels for 0% -> 13%
where the time goes in v1:
time: 61.9 us; the launch traced here: 61.3 us
  starting transfers between devices  26.1 us (42%)
  Pallas kernels  14.8 us (24%)
  waiting for transfers between devices  11.4 us (18%)
  local copies, waits for them, and re-layouts  8.27 us (13%)
  between operations  0.75 us (1%)
    all_to_all x1, starting transfers between devices, shards(): lax.all_to_all(ask.reshape(z.tiers, 1, z.ask), 'tier', split_axis=0, conc...  14.8 us
    pallas_call x6, Pallas kernels, call(): pl.pallas_call(functools.partial(kernel, z), out_shape=outs, in_specs=in_...  14.8 us
    unnamed x30, local copies, waits for them, and re-layouts  8.27 us
    all_to_all x1, starting transfers between devices, shards(): lax.all_to_all(answer.reshape(z.tiers, 1, z.message * LANES), 'tier', spl...  6.8 us
    all_to_all x1, waiting for transfers between devices, shards(): lax.all_to_all(answer.reshape(z.tiers, 1, z.message * LANES), 'tier', spl...  5.2 us
    all_to_all x1, waiting for transfers between devices, shards(): lax.all_to_all(ask.reshape(z.tiers, 1, z.ask), 'tier', split_axis=0, conc...  3.82 us
    ppermute x1, starting transfers between devices, neighbours(): lax.ppermute(high_edge, 'sys', forward)  3.21 us
    ppermute x1, waiting for transfers between devices, neighbours(): lax.ppermute(low_edge, 'sys', backward)  2.33 us
  transfers between devices with their start and end apart: 4, of which 3 were waited for; matrix products, arithmetic and copies ran while one was open for 0% of the time, Pallas kernels for 13%

profile of v1, /device:TPU:1, one launch (start us, length us, event | category | flops | bytes accessed | tf_op | source)
XLA Modules:
  0.0 61.3 jit_solution(12192388761095443037)
XLA Ops:
  0.6 0.7 %copy-done.9 = s32[4,4,96]{2,1,0:T(4,128)S(1)} copy-done((s32[4,4,96]{2,1,0:T(4,128)S(1)}, s32[4,4,96]{2,1,0:T(4,128)}, u32[]{:S(2)}) %copy-start.9) | copy-done | bytes 6168
  1.3 1.1 %ask.1 = s32[64,16]{1,0:T(8,128)} custom-call(s32[4,4,96]{2,1,0:T(4,128)S(1)} %copy-done.9), custom_call_target="tpu_custom_call" | custom-call | flops 1000000 | bytes 100000 | tf_op jit(solution)/shard_map/ask/pallas_call | solution.py:361
  2.4 14.8 %all-to-all-start = ((s32[64,1,16]{2,1,0:T(1,128)}), s32[64,1,16]{2,1,0:T(1,128)S(1)}, u32[]{:S(2)}, u32[]{:S(2)}) async-start(s32[64,1,16]{2,1,0:T(1,128)} %bitcast.1), calls=%async_computation | async-start | bytes 65536 | tf_op jit(solution)/shard_map/all_to_all | solution.py:391
  17.3 0.6 %copy-done.11 = s32[48]{0:T(128)S(1)} copy-done((s32[48]{0:T(128)S(1)}, s32[48]{0:T(128)}, u32[]{:S(2)}) %copy-start.11) | copy-done | bytes 216
  17.9 1.2 %copy-done = f32[4,2,64,512]{3,2,1,0:T(8,128)S(1)} copy-done((f32[4,2,64,512]{3,2,1,0:T(8,128)S(1)}, f32[4,2,64,512]{3,2,1,0:T(8,128)}, u32[]{:S(2)}) %copy-start) | copy-done | bytes 1048600
  19.1 1.2 %copy-done.2 = f32[4,2,64,512]{3,2,1,0:T(8,128)S(1)} copy-done((f32[4,2,64,512]{3,2,1,0:T(8,128)S(1)}, f32[4,2,64,512]{3,2,1,0:T(8,128)}, u32[]{:S(2)}) %copy-start.2) | copy-done | bytes 1048600
  20.4 1.3 %tables.1 = (f32[4,128,512]{2,1,0:T(8,128)S(1)}, f32[4,2,8,512]{3,2,1,0:T(8,128)S(1)}, f32[4,2,8,512]{3,2,1,0:T(8,128)S(1)}, bf16[576,128]{1,0:T(8,128)(2,1)S(1)}, bf16[96,1024]{1,0:T(8,128)(2,1)S(1)}) custom-call(f32[4,128,512]{2,1,0:T(8,128)S(1)} %bitcast.12, f32[4,128,512]{2,1,0:T(8,128)S(1)} %bitcast.14, s32[48]{0:T(128)S(1)} %copy-done.11), custom_call_target="tpu_custom_call" | custom-call | flops 3000000 | bytes 300000 | tf_op jit(solution)/shard_map/tables/pallas_call | solution.py:361
  21.7 0.0 copy-start.4
  21.7 1.0 %copy-done.4 = f32[4,128,512]{2,1,0:T(8,128)} copy-done((f32[4,128,512]{2,1,0:T(8,128)}, f32[4,128,512]{2,1,0:T(8,128)S(1)}, u32[]{:S(2)}) %copy-start.4) | copy-done | bytes 1048600
  22.7 3.8 %all-to-all-done = s32[64,1,16]{2,1,0:T(1,128)S(1)} async-done(((s32[64,1,16]{2,1,0:T(1,128)}), s32[64,1,16]{2,1,0:T(1,128)S(1)}, u32[]{:S(2)}, u32[]{:S(2)}) %all-to-all-start) | async-done | bytes 4128 | tf_op jit(solution)/shard_map/all_to_all | solution.py:391
  26.5 1.9 %answer.1 = f32[1408,128]{1,0:T(8,128)} custom-call(s32[64,16]{1,0:T(8,128)S(1)} %bitcast.16, bf16[576,128]{1,0:T(8,128)(2,1)S(1)} %get-tuple-element.16.col_ref, bf16[96,1024]{1,0:T(8,128)(2,1)S(1)} %get-tuple-element.17.row_ref), custom_call_target="tpu_custom_call" | custom-call | flops 1000000 | bytes 100000 | tf_op jit(solution)/shard_map/answer/pallas_call | solution.py:361
  28.4 6.8 %all-to-all-start.1 = ((f32[64,1,2816]{2,1,0:T(1,128)}), f32[64,1,2816]{2,1,0:T(1,128)}, u32[]{:S(2)}, u32[]{:S(2)}) async-start(f32[64,1,2816]{2,1,0:T(1,128)} %bitcast.5), calls=%async_computation.1 | async-start | bytes 1441792 | tf_op jit(solution)/shard_map/all_to_all | solution.py:422
  35.2 3.2 %collective-permute-start = (f32[4,2,8,512]{3,2,1,0:T(8,128)S(1)}, f32[4,2,8,512]{3,2,1,0:T(8,128)S(1)}, u32[]{:S(2)}, u32[]{:S(2)}) collective-permute-start(f32[4,2,8,512]{3,2,1,0:T(8,128)S(1)} %get-tuple-element.25), channel_id=1, source_target_pairs={{0,1},{1,2},{2,3},{3,4},{4,5},{5,6},{6,7},{8,9},{9,10},{10,11},{11... | collective-permute-start | bytes 393224 | tf_op jit(solution)/shard_map/ppermute | solution.py:379
  38.5 1.3 %collective-permute-start.1 = (f32[4,2,8,512]{3,2,1,0:T(8,128)S(1)}, f32[4,2,8,512]{3,2,1,0:T(8,128)S(1)}, u32[]{:S(2)}, u32[]{:S(2)}) collective-permute-start(f32[4,2,8,512]{3,2,1,0:T(8,128)S(1)} %get-tuple-element.26), channel_id=1, source_target_pairs={{1,0},{2,1},{3,2},{4,3},{5,4},{6,5},{7,6},{9,8},{10,9},{11,10},{12... | collective-permute-start | bytes 393224 | tf_op jit(solution)/shard_map/ppermute | solution.py:379
  39.8 0.6 %copy-done.12 = s32[64]{0:T(128)S(1)} copy-done((s32[64]{0:T(128)S(1)}, s32[64]{0:T(128)}, u32[]{:S(2)}) %copy-start.12) | copy-done | bytes 280
  40.4 0.0 copy-done.13
  40.4 1.2 %choose.1 = (bf16[384,384]{1,0:T(8,128)(2,1)S(1)}, f32[64,128]{1,0:T(8,128)S(1)}, f32[2,192,128]{2,1,0:T(8,128)S(1)}, f32[2,32,128]{2,1,0:T(8,128)S(1)}, f32[4,8,128]{2,1,0:T(8,128)S(1)}) custom-call(s32[4,4,96]{2,1,0:T(4,128)S(1)} %copy-done.10, s32[1,64]{1,0:T(1,128)S(1)} %bitcast.17, f32[2,48]{1,0:T(2,128)S(1)} %copy-done.13, f32[1,48]{1,0:T(1,128)S(1)} %bitcast.18), custom_call_target="tpu_custom_call" | custom-call | flops 2000000 | bytes 200000 | tf_op jit(solution)/shard_map/choose/pallas_call | solution.py:361
  41.7 0.7 %copy-done.6 = f32[2,192,128]{2,1,0:T(8,128)} copy-done((f32[2,192,128]{2,1,0:T(8,128)}, f32[2,192,128]{2,1,0:T(8,128)S(1)}, u32[]{:S(2)}) %copy-start.6) | copy-done | bytes 196632
  42.4 2.3 %collective-permute-done.1.high_ref = f32[4,2,8,512]{3,2,1,0:T(8,128)S(1)} collective-permute-done((f32[4,2,8,512]{3,2,1,0:T(8,128)S(1)}, f32[4,2,8,512]{3,2,1,0:T(8,128)S(1)}, u32[]{:S(2)}, u32[]{:S(2)}) %collective-permute-start.1) | collective-permute-done | bytes 131104 | tf_op jit(solution)/shard_map/ppermute | solution.py:379
  44.7 1.2 %copy-done.5 = f32[4,128,512]{2,1,0:T(8,128)S(1)} copy-done((f32[4,128,512]{2,1,0:T(8,128)S(1)}, f32[4,128,512]{2,1,0:T(8,128)}, u32[]{:S(2)}) %copy-start.5) | copy-done | bytes 1048600
  45.9 5.6 %band.1.deriv_ref = f32[4,128,512]{2,1,0:T(8,128)S(1)} custom-call(f32[4,128,512]{2,1,0:T(8,128)S(1)} %copy-done.5, f32[4,2,8,512]{3,2,1,0:T(8,128)S(1)} %collective-permute-done.low_ref, f32[4,2,8,512]{3,2,1,0:T(8,128)S(1)} %collective-permute-done.1.high_ref, f32[9,512]{1,0:T(8,128)S(1)} %copy-done.8, f32[4,8,128]{2,1,0:T(8,128)S(1)} %get-tuple-element.27.damp_ref), custom_call_target="tpu_custom_call" | custom-call | flops 5000000 | bytes 500000 | tf_op jit(solution)/shard_map/band/pallas_call | solution.py:361
  51.6 5.2 %all-to-all-done.1 = f32[64,1,2816]{2,1,0:T(1,128)} async-done(((f32[64,1,2816]{2,1,0:T(1,128)}), f32[64,1,2816]{2,1,0:T(1,128)}, u32[]{:S(2)}, u32[]{:S(2)}) %all-to-all-start.1) | async-done | bytes 720928 | tf_op jit(solution)/shard_map/all_to_all | solution.py:422
  56.8 0.9 %copy-done.7 = f32[2,192,128]{2,1,0:T(8,128)S(1)} copy-done((f32[2,192,128]{2,1,0:T(8,128)S(1)}, f32[2,192,128]{2,1,0:T(8,128)}, u32[]{:S(2)}) %copy-start.7) | copy-done | bytes 196632
  57.7 3.6 %apply.1 = (f32[4,128,512]{2,1,0:T(8,128)}, f32[4,128,512]{2,1,0:T(8,128)}) custom-call(f32[1408,128]{1,0:T(8,128)} %bitcast.6.got_ref, bf16[384,384]{1,0:T(8,128)(2,1)S(1)} %get-tuple-element.18.col_ref, f32[64,128]{1,0:T(8,128)S(1)} %get-tuple-element.19.row_ref, f32[2,192,128]{2,1,0:T(8,128)S(1)} %copy-done.7, ...), custom_call_target="tpu_custom_call" | custom-call | flops 4000000 | bytes 400000 | tf_op jit(solution)/shard_map/apply/pallas_call | solution.py:361
  (20 shorter events, 0.0 us)
Async XLA Ops:
  0.6 0.7 %copy-start.9 = (s32[4,4,96]{2,1,0:T(4,128)S(1)}, s32[4,4,96]{2,1,0:T(4,128)}, u32[]{:S(2)}) copy-start(s32[4,4,96]{2,1,0:T(4,128)} %links_ref.3) | copy-start | bytes 18436
  2.4 24.1 %all-to-all-start = ((s32[64,1,16]{2,1,0:T(1,128)}), s32[64,1,16]{2,1,0:T(1,128)S(1)}, u32[]{:S(2)}, u32[]{:S(2)}) async-start(s32[64,1,16]{2,1,0:T(1,128)} %bitcast.1), calls=%async_computation | async-start | bytes 65536 | tf_op jit(solution)/shard_map/all_to_all | solution.py:391
  17.2 0.7 %copy-start.11 = (s32[48]{0:T(128)S(1)}, s32[48]{0:T(128)}, u32[]{:S(2)}) copy-start(s32[48]{0:T(128)} %sites_ref.3) | copy-start | bytes 580
  17.9 1.2 %copy-start = (f32[4,2,64,512]{3,2,1,0:T(8,128)S(1)}, f32[4,2,64,512]{3,2,1,0:T(8,128)}, u32[]{:S(2)}) copy-start(f32[4,2,64,512]{3,2,1,0:T(8,128)} %param.8) | copy-start | bytes 3145732
  19.1 1.2 %copy-start.2 = (f32[4,2,64,512]{3,2,1,0:T(8,128)S(1)}, f32[4,2,64,512]{3,2,1,0:T(8,128)}, u32[]{:S(2)}) copy-start(f32[4,2,64,512]{3,2,1,0:T(8,128)} %param.9) | copy-start | bytes 3145732
  21.7 1.0 %copy-start.4 = (f32[4,128,512]{2,1,0:T(8,128)}, f32[4,128,512]{2,1,0:T(8,128)S(1)}, u32[]{:S(2)}) copy-start(f32[4,128,512]{2,1,0:T(8,128)S(1)} %get-tuple-element.22.mid_ref) | copy-start | bytes 3145732
  28.4 11.4 %copy-start.10 = (s32[4,4,96]{2,1,0:T(4,128)S(1)}, s32[4,4,96]{2,1,0:T(4,128)}, u32[]{:S(2)}) copy-start(s32[4,4,96]{2,1,0:T(4,128)} %links_ref.3) | copy-start | bytes 18436
  28.4 11.4 %copy-start.14 = (f32[48]{0:T(128)S(1)}, f32[48]{0:T(128)}, u32[]{:S(2)}) copy-start(f32[48]{0:T(128)} %param.14) | copy-start | bytes 580
  28.4 16.3 %copy-start.8 = (f32[9,512]{1,0:T(8,128)S(1)}, f32[9,512]{1,0:T(8,128)}, u32[]{:S(2)}) copy-start(f32[9,512]{1,0:T(8,128)} %bands_ref.1) | copy-start | bytes 55300
  28.4 28.3 %all-to-all-start.1 = ((f32[64,1,2816]{2,1,0:T(1,128)}), f32[64,1,2816]{2,1,0:T(1,128)}, u32[]{:S(2)}, u32[]{:S(2)}) async-start(f32[64,1,2816]{2,1,0:T(1,128)} %bitcast.5), calls=%async_computation.1 | async-start | bytes 1441792 | tf_op jit(solution)/shard_map/all_to_all | solution.py:422
  35.2 7.1 %collective-permute-start = (f32[4,2,8,512]{3,2,1,0:T(8,128)S(1)}, f32[4,2,8,512]{3,2,1,0:T(8,128)S(1)}, u32[]{:S(2)}, u32[]{:S(2)}) collective-permute-start(f32[4,2,8,512]{3,2,1,0:T(8,128)S(1)} %get-tuple-element.25), channel_id=1, source_target_pairs={{0,1},{1,2},{2,3},{3,4},{4,5},{5,6},{6,7},{8,9},{9,10},{10,11},{11... | collective-permute-start | bytes 393224 | tf_op jit(solution)/shard_map/ppermute | solution.py:379
  38.5 6.3 %collective-permute-start.1 = (f32[4,2,8,512]{3,2,1,0:T(8,128)S(1)}, f32[4,2,8,512]{3,2,1,0:T(8,128)S(1)}, u32[]{:S(2)}, u32[]{:S(2)}) collective-permute-start(f32[4,2,8,512]{3,2,1,0:T(8,128)S(1)} %get-tuple-element.26), channel_id=1, source_target_pairs={{1,0},{2,1},{3,2},{4,3},{5,4},{6,5},{7,6},{9,8},{10,9},{11,10},{12... | collective-permute-start | bytes 393224 | tf_op jit(solution)/shard_map/ppermute | solution.py:379
  39.8 0.7 %copy-start.12 = (s32[64]{0:T(128)S(1)}, s32[64]{0:T(128)}, u32[]{:S(2)}) copy-start(s32[64]{0:T(128)} %counts_ref.1) | copy-start | bytes 772
  39.8 0.7 %copy-start.13 = (f32[2,48]{1,0:T(2,128)S(1)}, f32[2,48]{1,0:T(2,128)}, u32[]{:S(2)}) copy-start(f32[2,48]{1,0:T(2,128)} %coef_ref.1) | copy-start | bytes 1156
  41.7 0.7 %copy-start.6 = (f32[2,192,128]{2,1,0:T(8,128)}, f32[2,192,128]{2,1,0:T(8,128)S(1)}, u32[]{:S(2)}) copy-start(f32[2,192,128]{2,1,0:T(8,128)S(1)} %get-tuple-element.20.col_coef_ref) | copy-start | bytes 589828
  44.7 1.2 %copy-start.5 = (f32[4,128,512]{2,1,0:T(8,128)S(1)}, f32[4,128,512]{2,1,0:T(8,128)}, u32[]{:S(2)}) copy-start(f32[4,128,512]{2,1,0:T(8,128)} %copy-done.4) | copy-start | bytes 3145732
  45.9 10.8 %copy-start.1 = (f32[4,2,64,512]{3,2,1,0:T(8,128)S(1)}, f32[4,2,64,512]{3,2,1,0:T(8,128)}, u32[]{:S(2)}) copy-start(f32[4,2,64,512]{3,2,1,0:T(8,128)} %param.8) | copy-start | bytes 3145732
  45.9 10.8 %copy-start.3 = (f32[4,2,64,512]{3,2,1,0:T(8,128)S(1)}, f32[4,2,64,512]{3,2,1,0:T(8,128)}, u32[]{:S(2)}) copy-start(f32[4,2,64,512]{3,2,1,0:T(8,128)} %param.9) | copy-start | bytes 3145732
  56.8 0.9 %copy-start.7 = (f32[2,192,128]{2,1,0:T(8,128)S(1)}, f32[2,192,128]{2,1,0:T(8,128)}, u32[]{:S(2)}) copy-start(f32[2,192,128]{2,1,0:T(8,128)} %copy-done.6) | copy-start | bytes 589828

commit v2 on v1

--- a/solution.py
+++ b/solution.py
@@ -9,12 +9,13 @@
 
 step_size = 0.05
 LANES = 128
-vmem_limit = 16 * 1024 * 1024
+mib = 1024 * 1024
+vmem_limits = {"tables": 16, "band": 16, "apply": 16}
 BF16 = jnp.bfloat16
 F32 = jnp.float32
 VMEM = pl.BlockSpec(memory_space=pltpu.VMEM)
 SMEM = pl.BlockSpec(memory_space=pltpu.SMEM)
-ANY = pl.BlockSpec(memory_space=pl.ANY)
+HBM = pl.BlockSpec(memory_space=pltpu.HBM)
 
 
 def iota(shape, dim):
@@ -116,29 +117,47 @@
     out_ref[...] = table.astype(jnp.int32)
 
 
-def table_kernel(z, state_ref, slope_ref, sites_ref, mid_ref, low_ref, high_ref, col_ref, row_ref, rows_scr, site_scr):
+def fetches(z, sources, targets, sem):
+    every = []
+    for g in range(z.slots):
+        pair = [
+            pltpu.make_async_copy(source.at[g], target.at[g], sem.at[i, g])
+            for i, (source, target) in enumerate(zip(sources, targets))
+        ]
+        for load in pair:
+            load.start()
+        every.append(pair)
+    return every
+
+
+def table_kernel(
+    z, state_hbm, slope_hbm, sites_ref, low_ref, high_ref, col_ref, row_ref,
+    mid_scr, rows_scr, site_scr, state_ref, slope_ref, sem,
+):
+    loads = fetches(z, (state_hbm, slope_hbm), (state_ref, slope_ref), sem)
     part = lax.axis_index("sys")
     span = z.slots * z.modes
-    site_scr[...] = jnp.zeros_like(site_scr)
     lane = iota((1, z.levels), 1)
     for k in range(z.modes):
         site_scr[k : k + 1, :] = jnp.where(lane == sites_ref[k], 1.0, 0.0)
     at_site = site_scr[: z.modes, :].astype(BF16)
     rows_scr[...] = jnp.zeros_like(rows_scr)
     for g in range(z.slots):
+        for load in loads[g]:
+            load.wait()
         mid = state_ref[g] + (0.5 * step_size) * slope_ref[g]
-        mid_ref[g] = mid
+        mid_scr[g] = mid
         for third, values in enumerate(thirds(mid)):
             at = third * span + g * z.modes
             col_ref[at : at + z.modes, :] = dot_nt(at_site, values).astype(BF16)
         for c in range(2):
             start = c * z.rows
-            low_ref[g, c] = mid_ref[g, start : start + z.band, :]
-            high_ref[g, c] = mid_ref[g, start + z.rows - z.band : start + z.rows, :]
+            low_ref[g, c] = mid_scr[g, start : start + z.band, :]
+            high_ref[g, c] = mid_scr[g, start + z.rows - z.band : start + z.rows, :]
             for k in range(z.block_modes):
                 local = sites_ref[part * z.block_modes + k] - part * z.rows
                 at = g * z.block_modes + k
-                rows_scr[at : at + 1, c * z.levels : (c + 1) * z.levels] = mid_ref[
+                rows_scr[at : at + 1, c * z.levels : (c + 1) * z.levels] = mid_scr[
                     g, pl.ds(start + local, 1), :
                 ]
     for third, values in enumerate(thirds(rows_scr[...])):
@@ -229,23 +248,25 @@
         falling = jnp.where(jnp.logical_and(modes == mode, kind == 1), level, 0).astype(F32)
         amount = jnp.sum(falling, axis=1, keepdims=True) * rate
         damp_ref[g] = jnp.broadcast_to(jnp.sum(amount, axis=0, keepdims=True), (8, LANES))
-        for c in range(2):
-            col_coef_ref[c, g * z.modes : (g + 1) * z.modes, :] = jnp.broadcast_to(
-                coefs[c], (z.modes, LANES)
-            )
-            mine = jnp.where(
-                iota((z.group, z.modes), 0) + low == iota((z.group, z.modes), 1),
-                coef_ref[c : c + 1, :],
-                0.0,
-            )
-            mine = jnp.where(iota((z.group, z.modes), 0) < z.block_modes, mine, 0.0)
-            row_coef_ref[c, g * z.group : (g + 1) * z.group, :] = jnp.broadcast_to(
-                jnp.sum(mine, axis=1, keepdims=True), (z.group, LANES)
-            )
-
-
-def band_kernel(z, mid_ref, low_ref, high_ref, bands_ref, damp_ref, out_ref, wide, spread, across_ref):
+    for c in range(2):
+        col_coef_ref[c] = jnp.broadcast_to(coefs[c], (z.modes, LANES))
+        mine = jnp.where(
+            iota((z.group, z.modes), 0) + low == iota((z.group, z.modes), 1),
+            coef_ref[c : c + 1, :],
+            0.0,
+        )
+        mine = jnp.where(iota((z.group, z.modes), 0) < z.block_modes, mine, 0.0)
+        row_coef_ref[c] = jnp.broadcast_to(
+            jnp.sum(mine, axis=1, keepdims=True), (z.group, LANES)
+        )
+
+
+def band_kernel(
+    z, state_hbm, slope_hbm, bands_ref, damp_ref, out_ref, base_hbm, down_ref, wide, spread, across_ref,
+    state_ref, slope_ref, base_ref, sem, base_sem,
+):
     part = lax.axis_index("sys")
+    loads = fetches(z, (state_hbm, slope_hbm), (state_ref, slope_ref), sem)
     taps = 2 * z.band + 1
     across_ref[...] = jnp.zeros_like(across_ref)
     lane = iota((1, z.levels), 1)
@@ -257,21 +278,31 @@
         elif offset > 0:
             row = jnp.where(lane < z.levels - offset, row, 0.0)
         across_ref[t : t + 1, :] = row
-    own = iota((z.rows, z.levels), 0) + part * z.rows == iota((z.rows, z.levels), 1)
-    own = as_bf16(own)
+    own = as_bf16(
+        iota((z.rows, z.levels), 0) + part * z.rows == iota((z.rows, z.levels), 1)
+    )
     down = jnp.zeros((z.rows, across_ref.shape[0]), F32)
     for values in thirds(across_ref[...]):
         down = down + dot_nt(own, values)
+    down_ref[...] = down
     for t in range(taps):
         spread[t] = jnp.broadcast_to(down[:, t : t + 1], (z.rows, LANES))
     tiles = z.levels // LANES
-    for g in range(z.slots):
+    wide[0 : z.band, :] = jnp.zeros((z.band, z.levels), F32)
+    wide[z.band + z.rows :, :] = jnp.zeros((z.band, z.levels), F32)
+    for g in range(z.slots):
+        for load in loads[g]:
+            load.wait()
         damp = damp_ref[g, 0:1, 0:1]
+        fields = []
         for c in range(2):
-            field = mid_ref[g, c * z.rows : (c + 1) * z.rows, :]
-            wide[0 : z.band, :] = low_ref[g, c]
+            rows = slice(c * z.rows, (c + 1) * z.rows)
+            base_ref[g, rows, :] = state_ref[g, rows, :] + (step_size / 6.0) * slope_ref[g, rows, :]
+            fields.append(state_ref[g, rows, :] + (0.5 * step_size) * slope_ref[g, rows, :])
+        pltpu.make_async_copy(base_ref.at[g], base_hbm.at[g], base_sem.at[g]).start()
+        for c in range(2):
+            field = fields[c]
             wide[z.band : z.band + z.rows, :] = field
-            wide[z.band + z.rows :, :] = high_ref[g, c]
             summed = across_ref[z.band : z.band + 1, :] * field
             for t in range(taps):
                 if t != z.band:
@@ -287,14 +318,43 @@
             commuted = jnp.concatenate(sides, axis=1) - summed
             other = 1 - c
             sign = 1.0 if c == 1 else -1.0
-            mine = mid_ref[g, other * z.rows : (other + 1) * z.rows, :]
-            out_ref[g, other * z.rows : (other + 1) * z.rows, :] = sign * commuted - damp * mine
+            out_ref[g, other * z.rows : (other + 1) * z.rows, :] = (
+                sign * commuted - damp * fields[other]
+            )
+    for g in range(z.slots):
+        pltpu.make_async_copy(base_ref.at[g], base_hbm.at[g], base_sem.at[g]).wait()
+
+
+def edge_kernel(z, low_ref, high_ref, down_ref, out_ref, wide):
+    band = z.band
+    nothing = jnp.zeros((band, z.levels), F32)
+    down = down_ref[...]
+    last = z.rows - band
+    for g in range(z.slots):
+        for c in range(2):
+            sign = 1.0 if c == 1 else -1.0
+            wide[0:band, :] = low_ref[g, c]
+            wide[band : 2 * band, :] = nothing
+            wide[2 * band : 3 * band, :] = high_ref[g, c]
+            top = nothing
+            bottom = nothing
+            for t in range(band):
+                top = top + down[0:band, t : t + 1] * wide[t : t + band, :]
+                bottom = (
+                    bottom
+                    + down[last:, band + 1 + t : band + 2 + t]
+                    * wide[band + 1 + t : 2 * band + 1 + t, :]
+                )
+            out_ref[g, 1 - c, 0] = sign * top
+            out_ref[g, 1 - c, 1] = sign * bottom
 
 
 def apply_kernel(
-    z, got_ref, col_ref, row_ref, col_coef_ref, row_coef_ref, deriv_ref, state_ref, slope_ref,
-    counts_ref, sites_ref, next_ref, sum_ref, site_scr, next_scr, sum_scr, sem,
+    z, got_ref, col_ref, row_ref, col_coef_ref, row_coef_ref, deriv_hbm, edge_ref, base_hbm,
+    counts_ref, sites_ref, next_ref, sum_ref, site_scr, rows_scr, next_scr, sum_scr, deriv_ref,
+    base_ref, sem, load_sem,
 ):
+    loads = fetches(z, (deriv_hbm, base_hbm), (deriv_ref, base_ref), load_sem)
     part = lax.axis_index("sys")
     tier = lax.axis_index("tier")
     lane = iota((1, z.levels), 1)
@@ -302,13 +362,6 @@
         site_scr[k : k + 1, :] = jnp.where(lane == sites_ref[k], 1.0, 0.0)
     at_site = site_scr[: z.modes, :].astype(BF16)
     total = z.slots * z.modes
-    pieces = jnp.concatenate(
-        [got_ref[pl.ds(p, z.tiers, stride=z.message), :] for p in range(z.cap)], axis=0
-    )
-    found = picked(col_ref[...], pieces)
-    up, down = found[:total], found[total:]
-    sign = jnp.where(iota((1, 2 * z.rows), 1) < z.rows, -1.0, 1.0)
-    cols = col_coef_ref[1] * down + sign * pltpu.roll(up + col_coef_ref[0] * down, z.rows, 1)
     pieces = jnp.concatenate(
         [
             jnp.concatenate(
@@ -325,31 +378,48 @@
     found = picked(row_ref[...].astype(BF16), pieces)
     half = z.slots * z.group
     up, down = found[:half], found[half:]
-    turned = up + row_coef_ref[0, :, 0:1] * down
-    straight = row_coef_ref[1, :, 0:1] * down
-    rows = (
-        straight[:, : z.levels] + turned[:, z.levels :],
-        straight[:, z.levels :] - turned[:, : z.levels],
-    )
-    for g in range(z.slots):
-        mine = cols[g * z.modes : (g + 1) * z.modes, :]
-        added = deriv_ref[g]
-        for values in thirds(mine):
+    real = jnp.concatenate([row_coef_ref[0, :, 0:1]] * z.slots, axis=0)
+    imag = jnp.concatenate([row_coef_ref[1, :, 0:1]] * z.slots, axis=0)
+    turned = up + real * down
+    straight = imag * down
+    rows_scr[0] = straight[:, : z.levels] + turned[:, z.levels :]
+    rows_scr[1] = straight[:, z.levels :] - turned[:, : z.levels]
+    pieces = thirds(
+        jnp.concatenate(
+            [got_ref[pl.ds(p, z.tiers, stride=z.message), :] for p in range(z.cap)], axis=0
+        )
+    )
+    sign = jnp.where(iota((1, 2 * z.rows), 1) < z.rows, -1.0, 1.0)
+    for g in range(z.slots):
+        up = jnp.zeros((z.modes, 2 * z.rows), F32)
+        down = up
+        for values in pieces:
+            up = up + dot_nn(col_ref[g * z.modes : (g + 1) * z.modes, :], values)
+            down = down + dot_nn(
+                col_ref[total + g * z.modes : total + (g + 1) * z.modes, :], values
+            )
+        cols = col_coef_ref[1] * down + sign * pltpu.roll(up + col_coef_ref[0] * down, z.rows, 1)
+        added = jnp.zeros((2 * z.rows, z.levels), F32)
+        for values in thirds(cols):
             added = added + dot_tn(values, at_site)
-        next_scr[g] = added
+        for load in loads[g]:
+            load.wait()
+        next_scr[g] = deriv_ref[g] + added
+        for c in range(2):
+            for side in range(2):
+                start = c * z.rows + side * (z.rows - z.band)
+                at = slice(start, start + z.band)
+                next_scr[g, at, :] = next_scr[g, at, :] + edge_ref[g, c, side]
         for k in range(z.block_modes):
             local = sites_ref[part * z.block_modes + k] - part * z.rows
             for c in range(2):
                 at = pl.ds(c * z.rows + local, 1)
-                next_scr[g, at, :] = (
-                    next_scr[g, at, :] + rows[c][g * z.group + k : g * z.group + k + 1, :]
-                )
+                row = g * z.group + k
+                next_scr[g, at, :] = next_scr[g, at, :] + rows_scr[c, row : row + 1, :]
         live = jnp.where(g < counts_ref[tier], 1.0, 0.0)
         slope_next = next_scr[g] * live
         next_scr[g] = slope_next
-        sum_scr[g] = (
-            state_ref[g] + (step_size / 6.0) * slope_ref[g] + (step_size / 3.0) * slope_next
-        ) * live
+        sum_scr[g] = (base_ref[g] + (step_size / 3.0) * slope_next) * live
         pltpu.make_async_copy(next_scr.at[g], next_ref.at[g], sem.at[0, g]).start()
         pltpu.make_async_copy(sum_scr.at[g], sum_ref.at[g], sem.at[1, g]).start()
     for g in range(z.slots):
@@ -357,7 +427,7 @@
         pltpu.make_async_copy(sum_scr.at[g], sum_ref.at[g], sem.at[1, g]).wait()
 
 
-def call(kernel, z, name, args, in_specs, outs, scratch=(), out_specs=None, micros=1):
+def call(kernel, z, name, args, in_specs, outs, scratch=(), out_specs=None, micros=1, aliases=()):
     return pl.pallas_call(
         functools.partial(kernel, z),
         out_shape=outs,
@@ -365,7 +435,8 @@
         out_specs=[VMEM] * len(outs) if out_specs is None else out_specs,
         scratch_shapes=list(scratch),
         name=name,
-        compiler_params=pltpu.CompilerParams(vmem_limit_bytes=vmem_limit),
+        input_output_aliases=dict(aliases),
+        compiler_params=pltpu.CompilerParams(vmem_limit_bytes=int(vmem_limits.get(name, 16) * mib)),
         cost_estimate=pl.CostEstimate(
             flops=int(micros * 1e6), bytes_accessed=int(micros * 1e5), transcendentals=0
         ),
@@ -392,22 +463,25 @@
         ask.reshape(z.tiers, 1, z.ask), "tier", split_axis=0, concat_axis=0, tiled=True
     ).reshape(z.tiers, z.ask)
     edge = (z.slots, 2, z.band, z.levels)
-    mid, low_edge, high_edge, col_table, row_table = call(
+    low_edge, high_edge, col_table, row_table = call(
         table_kernel,
         z,
         "tables",
         (state_flat, slope_flat, mode_site),
-        [VMEM, VMEM, SMEM],
+        [HBM, HBM, SMEM],
         [
-            shape(flat, F32),
             shape(edge, F32),
             shape(edge, F32),
             shape((3 * z.slots * z.modes, 2 * z.rows), BF16),
             shape((3 * z.row_pad, 2 * z.levels), BF16),
         ],
         [
+            pltpu.VMEM(flat, F32),
             pltpu.VMEM((z.row_pad, 2 * z.levels), F32),
             pltpu.VMEM((round_up(z.modes, 16), z.levels), F32),
+            pltpu.VMEM(flat, F32),
+            pltpu.VMEM(flat, F32),
+            pltpu.SemaphoreType.DMA((2, z.slots)),
         ],
         micros=3,
     )
@@ -437,43 +511,61 @@
         [
             shape((2 * z.slots * z.modes, z.cap * z.tiers), BF16),
             shape((2 * z.slots * z.group, z.row_cap * z.tiers), F32),
-            shape((2, z.slots * z.modes, LANES), F32),
-            shape((2, z.slots * z.group, LANES), F32),
+            shape((2, z.modes, LANES), F32),
+            shape((2, z.group, LANES), F32),
             shape((z.slots, 8, LANES), F32),
         ],
         micros=2,
     )
-    (deriv,) = call(
+    taps = round_up(2 * z.band + 1, 16)
+    deriv, base, down = call(
         band_kernel,
         z,
         "band",
-        (mid, above, below, h_bands, damp),
-        [VMEM] * 5,
-        [shape(flat, F32)],
+        (state_flat, slope_flat, h_bands, damp),
+        [HBM, HBM, VMEM, VMEM],
+        [shape(flat, F32), shape(flat, F32), shape((z.rows, taps), F32)],
         [
             pltpu.VMEM((z.rows + 2 * z.band, z.levels), F32),
             pltpu.VMEM((2 * z.band + 1, z.rows, LANES), F32),
-            pltpu.VMEM((round_up(2 * z.band + 1, 16), z.levels), F32),
+            pltpu.VMEM((taps, z.levels), F32),
+            pltpu.VMEM(flat, F32),
+            pltpu.VMEM(flat, F32),
+            pltpu.VMEM(flat, F32),
+            pltpu.SemaphoreType.DMA((2, z.slots)),
+            pltpu.SemaphoreType.DMA((z.slots,)),
         ],
+        out_specs=[VMEM, HBM, VMEM],
         micros=5,
+    )
+    (edges,) = call(
+        edge_kernel,
+        z,
+        "edges",
+        (above, below, down),
+        [VMEM] * 3,
+        [shape((z.slots, 2, 2, z.band, z.levels), F32)],
+        [pltpu.VMEM((3 * z.band, z.levels), F32)],
     )
     slope_next, partial_sum = call(
         apply_kernel,
         z,
         "apply",
-        (
-            got, col_choice, row_choice, col_coef, row_coef, deriv, state_flat, slope_flat,
-            counts, mode_site,
-        ),
-        [VMEM] * 8 + [SMEM] * 2,
+        (got, col_choice, row_choice, col_coef, row_coef, deriv, edges, base, counts, mode_site),
+        [VMEM] * 5 + [HBM, VMEM, HBM] + [SMEM] * 2,
         [shape(flat, F32), shape(flat, F32)],
         [
             pltpu.VMEM((round_up(z.modes, 8), z.levels), F32),
-            pltpu.VMEM(flat, F32),
-            pltpu.VMEM(flat, F32),
+            pltpu.VMEM((2, z.slots * z.group, z.levels), F32),
+            pltpu.VMEM(flat, F32),
+            pltpu.VMEM(flat, F32),
+            pltpu.VMEM(flat, F32),
+            pltpu.VMEM(flat, F32),
+            pltpu.SemaphoreType.DMA((2, z.slots)),
             pltpu.SemaphoreType.DMA((2, z.slots)),
         ],
-        out_specs=[ANY, ANY],
+        out_specs=[HBM, HBM],
+        aliases=((5, 0), (7, 1)),
         micros=4,
     )
     return slope_next.reshape(state.shape), partial_sum.reshape(state.shape)

time: 61.9 us -> 62.2 us (level)
  Pallas kernels: 14.8 us -> 20.7 us
  local copies, waits for them, and re-layouts: 8.27 us -> 4.47 us
  waiting for transfers between devices: 11.4 us -> 9.62 us
    pallas_call x6 -> x7, Pallas kernels: 14.8 us -> 20.7 us  [call(): pl.pallas_call(functools.partial(kernel, z), out_shape=outs, in_specs=in_...]
    unnamed x30 -> x22, local copies, waits for them, and re-layouts: 8.27 us -> 4.47 us
    ppermute x1, waiting for transfers between devices: 2.33 us -> 0.01 us  [neighbours(): lax.ppermute(low_edge, 'sys', backward)]
  transfers between devices with their start and end apart: 4 -> 4, of which waited for: 3 -> 2; matrix products, arithmetic and copies ran while one was open for 0% -> 0% of each run, Pallas kernels for 13% -> 21%
where the time goes in v2:
time: 62.2 us; the launch traced here: 61.7 us
  starting transfers between devices  26 us (42%)
  Pallas kernels  20.7 us (33%)
  waiting for transfers between devices  9.62 us (15%)
  local copies, waits for them, and re-layouts  4.47 us (7%)
  between operations  0.94 us (2%)
    pallas_call x7, Pallas kernels, call(): pl.pallas_call(functools.partial(kernel, z), out_shape=outs, in_specs=in_...  20.7 us
    all_to_all x1, starting transfers between devices, shards(): lax.all_to_all(ask.reshape(z.tiers, 1, z.ask), 'tier', split_axis=0, conc...  14.8 us
    all_to_all x1, starting transfers between devices, shards(): lax.all_to_all(answer.reshape(z.tiers, 1, z.message * LANES), 'tier', spl...  6.5 us
    all_to_all x1, waiting for transfers between devices, shards(): lax.all_to_all(answer.reshape(z.tiers, 1, z.message * LANES), 'tier', spl...  5.62 us
    unnamed x22, local copies, waits for them, and re-layouts  4.47 us
    all_to_all x1, waiting for transfers between devices, shards(): lax.all_to_all(ask.reshape(z.tiers, 1, z.ask), 'tier', split_axis=0, conc...  3.99 us
    ppermute x1, starting transfers between devices, neighbours(): lax.ppermute(high_edge, 'sys', forward)  3.2 us
    ppermute x1, starting transfers between devices, neighbours(): lax.ppermute(low_edge, 'sys', backward)  1.47 us
  transfers between devices with their start and end apart: 4, of which 2 were waited for; matrix products, arithmetic and copies ran while one was open for 0% of the time, Pallas kernels for 21%

profile of v2, /device:TPU:1, one launch (start us, length us, event | category | flops | bytes accessed | tf_op | source)
XLA Modules:
  0.0 61.7 jit_solution(17479574783674193380)
XLA Ops:
  0.6 0.0 copy-start.5
  0.6 0.7 %copy-done.5 = s32[4,4,96]{2,1,0:T(4,128)S(1)} copy-done((s32[4,4,96]{2,1,0:T(4,128)S(1)}, s32[4,4,96]{2,1,0:T(4,128)}, u32[]{:S(2)}) %copy-start.5) | copy-done | bytes 6168
  1.3 1.1 %ask.1 = s32[64,16]{1,0:T(8,128)} custom-call(s32[4,4,96]{2,1,0:T(4,128)S(1)} %copy-done.5), custom_call_target="tpu_custom_call" | custom-call | flops 1000000 | bytes 100000 | tf_op jit(solution)/shard_map/ask/pallas_call | solution.py:431
  2.4 14.8 %all-to-all-start = ((s32[64,1,16]{2,1,0:T(1,128)}), s32[64,1,16]{2,1,0:T(1,128)S(1)}, u32[]{:S(2)}, u32[]{:S(2)}) async-start(s32[64,1,16]{2,1,0:T(1,128)} %bitcast.1), calls=%async_computation | async-start | bytes 65536 | tf_op jit(solution)/shard_map/all_to_all | solution.py:462
  17.2 0.0 copy-start.7
  17.3 0.6 %copy-done.7 = s32[48]{0:T(128)S(1)} copy-done((s32[48]{0:T(128)S(1)}, s32[48]{0:T(128)}, u32[]{:S(2)}) %copy-start.7) | copy-done | bytes 216
  17.9 1.2 %copy-done = f32[4,2,64,512]{3,2,1,0:T(8,128)S(1)} copy-done((f32[4,2,64,512]{3,2,1,0:T(8,128)S(1)}, f32[4,2,64,512]{3,2,1,0:T(8,128)}, u32[]{:S(2)}) %copy-start) | copy-done | bytes 1048600
  19.1 1.2 %copy-done.2 = f32[4,2,64,512]{3,2,1,0:T(8,128)S(1)} copy-done((f32[4,2,64,512]{3,2,1,0:T(8,128)S(1)}, f32[4,2,64,512]{3,2,1,0:T(8,128)}, u32[]{:S(2)}) %copy-start.2) | copy-done | bytes 1048600
  20.4 2.1 %tables.1 = (f32[4,2,8,512]{3,2,1,0:T(8,128)S(1)}, f32[4,2,8,512]{3,2,1,0:T(8,128)S(1)}, bf16[576,128]{1,0:T(8,128)(2,1)S(1)}, bf16[96,1024]{1,0:T(8,128)(2,1)S(1)}) custom-call(f32[4,128,512]{2,1,0:T(8,128)S(1)} %bitcast.12, f32[4,128,512]{2,1,0:T(8,128)S(1)} %bitcast.14, s32[48]{0:T(128)S(1)} %copy-done.7), custom_call_target="tpu_custom_call" | custom-call | flops 3000000 | bytes 300000 | tf_op jit(solution)/shard_map/tables/pallas_call | solution.py:431
  22.5 4.0 %all-to-all-done = s32[64,1,16]{2,1,0:T(1,128)S(1)} async-done(((s32[64,1,16]{2,1,0:T(1,128)}), s32[64,1,16]{2,1,0:T(1,128)S(1)}, u32[]{:S(2)}, u32[]{:S(2)}) %all-to-all-start) | async-done | bytes 4128 | tf_op jit(solution)/shard_map/all_to_all | solution.py:462
  26.5 2.0 %answer.1 = f32[1408,128]{1,0:T(8,128)} custom-call(s32[64,16]{1,0:T(8,128)S(1)} %bitcast.17, bf16[576,128]{1,0:T(8,128)(2,1)S(1)} %get-tuple-element.18.col_ref, bf16[96,1024]{1,0:T(8,128)(2,1)S(1)} %get-tuple-element.19.row_ref), custom_call_target="tpu_custom_call" | custom-call | flops 1000000 | bytes 100000 | tf_op jit(solution)/shard_map/answer/pallas_call | solution.py:431
  28.5 6.5 %all-to-all-start.1 = ((f32[64,1,2816]{2,1,0:T(1,128)}), f32[64,1,2816]{2,1,0:T(1,128)S(1)}, u32[]{:S(2)}, u32[]{:S(2)}) async-start(f32[64,1,2816]{2,1,0:T(1,128)} %bitcast.5), calls=%async_computation.1 | async-start | bytes 1441792 | tf_op jit(solution)/shard_map/all_to_all | solution.py:496
  35.0 3.2 %collective-permute-start = (f32[4,2,8,512]{3,2,1,0:T(8,128)S(1)}, f32[4,2,8,512]{3,2,1,0:T(8,128)S(1)}, u32[]{:S(2)}, u32[]{:S(2)}) collective-permute-start(f32[4,2,8,512]{3,2,1,0:T(8,128)S(1)} %get-tuple-element.28), channel_id=1, source_target_pairs={{0,1},{1,2},{2,3},{3,4},{4,5},{5,6},{6,7},{8,9},{9,10},{10,11},{11... | collective-permute-start | bytes 393224 | tf_op jit(solution)/shard_map/ppermute | solution.py:450
  38.2 1.5 %collective-permute-start.1 = (f32[4,2,8,512]{3,2,1,0:T(8,128)S(1)}, f32[4,2,8,512]{3,2,1,0:T(8,128)S(1)}, u32[]{:S(2)}, u32[]{:S(2)}) collective-permute-start(f32[4,2,8,512]{3,2,1,0:T(8,128)S(1)} %get-tuple-element.29), channel_id=1, source_target_pairs={{1,0},{2,1},{3,2},{4,3},{5,4},{6,5},{7,6},{9,8},{10,9},{11,10},{12... | collective-permute-start | bytes 393224 | tf_op jit(solution)/shard_map/ppermute | solution.py:450
  39.7 0.0 copy-start.8
  39.7 0.0 copy-start.9
  39.7 0.6 copy-done.8
  40.3 0.0 copy-done.9
  40.4 1.2 %choose.1 = (bf16[384,384]{1,0:T(8,128)(2,1)S(1)}, f32[64,128]{1,0:T(8,128)S(1)}, f32[2,48,128]{2,1,0:T(8,128)S(1)}, f32[2,8,128]{2,1,0:T(8,128)S(1)}, f32[4,8,128]{2,1,0:T(8,128)S(1)}) custom-call(s32[4,4,96]{2,1,0:T(4,128)S(1)} %copy-done.6, s32[1,64]{1,0:T(1,128)S(1)} %bitcast.18, f32[2,48]{1,0:T(2,128)S(1)} %copy-done.9, f32[1,48]{1,0:T(1,128)S(1)} %bitcast.19), custom_call_target="tpu_custom_call" | custom-call | flops 2000000 | bytes 200000 | tf_op jit(solution)/shard_map/choose/pallas_call | solution.py:431
  41.6 8.8 %band.1 = (f32[4,128,512]{2,1,0:T(8,128)}, f32[4,128,512]{2,1,0:T(8,128)}, f32[64,32]{1,0:T(8,128)S(1)}) custom-call(f32[4,128,512]{2,1,0:T(8,128)S(1)} %bitcast.13, f32[4,128,512]{2,1,0:T(8,128)S(1)} %bitcast.15, f32[9,512]{1,0:T(8,128)S(1)} %copy-done.4, f32[4,8,128]{2,1,0:T(8,128)S(1)} %get-tuple-element.24.damp_ref), custom_call_target="tpu_custom_call" | custom-call | flops 5000000 | bytes 500000 | tf_op jit(solution)/shard_map/band/pallas_call | solution.py:431
  50.4 0.0 collective-permute-done.1.high_ref
  50.4 0.5 edges.1.edge_ref
  51.0 5.6 %all-to-all-done.1 = f32[64,1,2816]{2,1,0:T(1,128)S(1)} async-done(((f32[64,1,2816]{2,1,0:T(1,128)}), f32[64,1,2816]{2,1,0:T(1,128)S(1)}, u32[]{:S(2)}, u32[]{:S(2)}) %all-to-all-start.1) | async-done | bytes 720928 | tf_op jit(solution)/shard_map/all_to_all | solution.py:496
  56.6 5.0 %apply.1 = (f32[4,128,512]{2,1,0:T(8,128)}, f32[4,128,512]{2,1,0:T(8,128)}) custom-call(f32[1408,128]{1,0:T(8,128)S(1)} %bitcast.16, bf16[384,384]{1,0:T(8,128)(2,1)S(1)} %get-tuple-element.20.col_ref, f32[64,128]{1,0:T(8,128)S(1)} %get-tuple-element.21.row_ref, ...), custom_call_target="tpu_custom_call", output_to_operand_aliasing={{0}: (5, {}), {1}: (7, {})} | custom-call | flops 4000000 | bytes 400000 | tf_op jit(solution)/shard_map/apply/pallas_call | solution.py:431
  (13 shorter events, 0.0 us)
Async XLA Ops:
  0.6 0.7 %copy-start.5 = (s32[4,4,96]{2,1,0:T(4,128)S(1)}, s32[4,4,96]{2,1,0:T(4,128)}, u32[]{:S(2)}) copy-start(s32[4,4,96]{2,1,0:T(4,128)} %links_ref.3) | copy-start | bytes 18436
  2.4 24.1 %all-to-all-start = ((s32[64,1,16]{2,1,0:T(1,128)}), s32[64,1,16]{2,1,0:T(1,128)S(1)}, u32[]{:S(2)}, u32[]{:S(2)}) async-start(s32[64,1,16]{2,1,0:T(1,128)} %bitcast.1), calls=%async_computation | async-start | bytes 65536 | tf_op jit(solution)/shard_map/all_to_all | solution.py:462
  17.2 0.7 %copy-start.7 = (s32[48]{0:T(128)S(1)}, s32[48]{0:T(128)}, u32[]{:S(2)}) copy-start(s32[48]{0:T(128)} %sites_ref.3) | copy-start | bytes 580
  17.9 1.2 %copy-start = (f32[4,2,64,512]{3,2,1,0:T(8,128)S(1)}, f32[4,2,64,512]{3,2,1,0:T(8,128)}, u32[]{:S(2)}) copy-start(f32[4,2,64,512]{3,2,1,0:T(8,128)} %param.8) | copy-start | bytes 3145732
  19.1 1.2 %copy-start.2 = (f32[4,2,64,512]{3,2,1,0:T(8,128)S(1)}, f32[4,2,64,512]{3,2,1,0:T(8,128)}, u32[]{:S(2)}) copy-start(f32[4,2,64,512]{3,2,1,0:T(8,128)} %param.9) | copy-start | bytes 3145732
  26.5 15.1 %copy-start.1 = (f32[4,2,64,512]{3,2,1,0:T(8,128)S(1)}, f32[4,2,64,512]{3,2,1,0:T(8,128)}, u32[]{:S(2)}) copy-start(f32[4,2,64,512]{3,2,1,0:T(8,128)} %param.8) | copy-start | bytes 3145732
  26.5 15.1 %copy-start.3 = (f32[4,2,64,512]{3,2,1,0:T(8,128)S(1)}, f32[4,2,64,512]{3,2,1,0:T(8,128)}, u32[]{:S(2)}) copy-start(f32[4,2,64,512]{3,2,1,0:T(8,128)} %param.9) | copy-start | bytes 3145732
  28.4 11.2 %copy-start.6 = (s32[4,4,96]{2,1,0:T(4,128)S(1)}, s32[4,4,96]{2,1,0:T(4,128)}, u32[]{:S(2)}) copy-start(s32[4,4,96]{2,1,0:T(4,128)} %links_ref.3) | copy-start | bytes 18436
  28.5 11.2 %copy-start.10 = (f32[48]{0:T(128)S(1)}, f32[48]{0:T(128)}, u32[]{:S(2)}) copy-start(f32[48]{0:T(128)} %param.14) | copy-start | bytes 580
  28.5 13.2 %copy-start.4 = (f32[9,512]{1,0:T(8,128)S(1)}, f32[9,512]{1,0:T(8,128)}, u32[]{:S(2)}) copy-start(f32[9,512]{1,0:T(8,128)} %bands_ref.1) | copy-start | bytes 55300
  28.5 28.1 %all-to-all-start.1 = ((f32[64,1,2816]{2,1,0:T(1,128)}), f32[64,1,2816]{2,1,0:T(1,128)S(1)}, u32[]{:S(2)}, u32[]{:S(2)}) async-start(f32[64,1,2816]{2,1,0:T(1,128)} %bitcast.5), calls=%async_computation.1 | async-start | bytes 1441792 | tf_op jit(solution)/shard_map/all_to_all | solution.py:496
  35.0 15.4 %collective-permute-start = (f32[4,2,8,512]{3,2,1,0:T(8,128)S(1)}, f32[4,2,8,512]{3,2,1,0:T(8,128)S(1)}, u32[]{:S(2)}, u32[]{:S(2)}) collective-permute-start(f32[4,2,8,512]{3,2,1,0:T(8,128)S(1)} %get-tuple-element.28), channel_id=1, source_target_pairs={{0,1},{1,2},{2,3},{3,4},{4,5},{5,6},{6,7},{8,9},{9,10},{10,11},{11... | collective-permute-start | bytes 393224 | tf_op jit(solution)/shard_map/ppermute | solution.py:450
  38.2 12.2 %collective-permute-start.1 = (f32[4,2,8,512]{3,2,1,0:T(8,128)S(1)}, f32[4,2,8,512]{3,2,1,0:T(8,128)S(1)}, u32[]{:S(2)}, u32[]{:S(2)}) collective-permute-start(f32[4,2,8,512]{3,2,1,0:T(8,128)S(1)} %get-tuple-element.29), channel_id=1, source_target_pairs={{1,0},{2,1},{3,2},{4,3},{5,4},{6,5},{7,6},{9,8},{10,9},{11,10},{12... | collective-permute-start | bytes 393224 | tf_op jit(solution)/shard_map/ppermute | solution.py:450
  39.7 0.7 %copy-start.8 = (s32[64]{0:T(128)S(1)}, s32[64]{0:T(128)}, u32[]{:S(2)}) copy-start(s32[64]{0:T(128)} %counts_ref.1) | copy-start | bytes 772
  39.7 0.7 %copy-start.9 = (f32[2,48]{1,0:T(2,128)S(1)}, f32[2,48]{1,0:T(2,128)}, u32[]{:S(2)}) copy-start(f32[2,48]{1,0:T(2,128)} %coef_ref.1) | copy-start | bytes 1156

commit v3 on v1

--- a/solution.py
+++ b/solution.py
@@ -9,12 +9,13 @@
 
 step_size = 0.05
 LANES = 128
-vmem_limit = 16 * 1024 * 1024
+mib = 1024 * 1024
+vmem_limits = {"tables": 16, "band": 16, "apply": 16}
 BF16 = jnp.bfloat16
 F32 = jnp.float32
 VMEM = pl.BlockSpec(memory_space=pltpu.VMEM)
 SMEM = pl.BlockSpec(memory_space=pltpu.SMEM)
-ANY = pl.BlockSpec(memory_space=pl.ANY)
+HBM = pl.BlockSpec(memory_space=pltpu.HBM)
 
 
 def iota(shape, dim):
@@ -45,9 +46,14 @@
     return first, second, third
 
 
+def halves(x):
+    first = x.astype(BF16)
+    return first, (x - first.astype(F32)).astype(BF16)
+
+
 def picked(chooser, values):
-    first, second, third = thirds(values)
-    return dot_nn(chooser, first) + (dot_nn(chooser, second) + dot_nn(chooser, third))
+    first, second = halves(values)
+    return dot_nn(chooser, first) + dot_nn(chooser, second)
 
 
 def as_bf16(mask):
@@ -116,10 +122,12 @@
     out_ref[...] = table.astype(jnp.int32)
 
 
-def table_kernel(z, state_ref, slope_ref, sites_ref, mid_ref, low_ref, high_ref, col_ref, row_ref, rows_scr, site_scr):
+def table_kernel(
+    z, state_ref, slope_ref, sites_ref, low_ref, high_ref, col_ref, row_ref,
+    mid_scr, rows_scr, site_scr,
+):
     part = lax.axis_index("sys")
     span = z.slots * z.modes
-    site_scr[...] = jnp.zeros_like(site_scr)
     lane = iota((1, z.levels), 1)
     for k in range(z.modes):
         site_scr[k : k + 1, :] = jnp.where(lane == sites_ref[k], 1.0, 0.0)
@@ -127,25 +135,25 @@
     rows_scr[...] = jnp.zeros_like(rows_scr)
     for g in range(z.slots):
         mid = state_ref[g] + (0.5 * step_size) * slope_ref[g]
-        mid_ref[g] = mid
+        mid_scr[g] = mid
         for third, values in enumerate(thirds(mid)):
             at = third * span + g * z.modes
             col_ref[at : at + z.modes, :] = dot_nt(at_site, values).astype(BF16)
         for c in range(2):
             start = c * z.rows
-            low_ref[g, c] = mid_ref[g, start : start + z.band, :]
-            high_ref[g, c] = mid_ref[g, start + z.rows - z.band : start + z.rows, :]
+            low_ref[g, c] = mid_scr[g, start : start + z.band, :]
+            high_ref[g, c] = mid_scr[g, start + z.rows - z.band : start + z.rows, :]
             for k in range(z.block_modes):
                 local = sites_ref[part * z.block_modes + k] - part * z.rows
                 at = g * z.block_modes + k
-                rows_scr[at : at + 1, c * z.levels : (c + 1) * z.levels] = mid_ref[
+                rows_scr[at : at + 1, c * z.levels : (c + 1) * z.levels] = mid_scr[
                     g, pl.ds(start + local, 1), :
                 ]
     for third, values in enumerate(thirds(rows_scr[...])):
         row_ref[third * z.row_pad : (third + 1) * z.row_pad, :] = values
 
 
-def answer_kernel(z, ask_ref, col_ref, row_ref, out_ref):
+def answer_kernel(z, ask_ref, col_ref, row_ref, out_hbm, out_scr, sem):
     part = lax.axis_index("sys")
     span = z.slots * z.modes
     low = part * z.block_modes
@@ -163,29 +171,53 @@
             take = jnp.logical_and(inside, used == j)
             row_at[j] = jnp.where(take, where_row, row_at[j])
         used = used + jnp.where(inside, 1, 0)
-    chosen = jnp.concatenate(columns, axis=0)
-    found = dot_nn(chosen, col_ref[:span, :])
-    for third in (1, 2):
-        found = found + dot_nn(chosen, col_ref[third * span : (third + 1) * span, :])
-    for p in range(z.cap):
-        out_ref[pl.ds(p, z.tiers, stride=z.message), :] = found[p * z.tiers : (p + 1) * z.tiers, :]
     lanes = iota((z.tiers, z.row_pad), 1)
-    chosen = jnp.concatenate([as_bf16(at == lanes) for at in row_at], axis=0)
-    found = dot_nn(chosen, row_ref[: z.row_pad, :])
-    for third in (1, 2):
-        found = found + dot_nn(chosen, row_ref[third * z.row_pad : (third + 1) * z.row_pad, :])
-    for j in range(z.row_cap):
-        for t in range(z.lane_tiles):
-            at = z.cap + j * z.lane_tiles + t
-            out_ref[pl.ds(at, z.tiers, stride=z.message), :] = found[
-                j * z.tiers : (j + 1) * z.tiers, t * LANES : (t + 1) * LANES
+    row_choice = [as_bf16(at == lanes) for at in row_at]
+    parts = 2
+    size = z.tiers // parts
+    copies = []
+    for part in range(parts):
+        mine = slice(part * size, (part + 1) * size)
+        start = part * size * z.message
+        chosen = jnp.concatenate([choice[mine] for choice in row_choice], axis=0)
+        found = dot_nn(chosen, row_ref[: z.row_pad, :])
+        for third in (1, 2):
+            found = found + dot_nn(
+                chosen, row_ref[third * z.row_pad : (third + 1) * z.row_pad, :]
+            )
+        for j in range(z.row_cap):
+            for t in range(z.lane_tiles):
+                at = start + z.cap + j * z.lane_tiles + t
+                out_scr[pl.ds(at, size, stride=z.message), :] = found[
+                    j * size : (j + 1) * size, t * LANES : (t + 1) * LANES
+                ]
+        chosen = jnp.concatenate([choice[mine] for choice in columns], axis=0)
+        found = dot_nn(chosen, col_ref[:span, :])
+        for third in (1, 2):
+            found = found + dot_nn(chosen, col_ref[third * span : (third + 1) * span, :])
+        for p in range(z.cap):
+            out_scr[pl.ds(start + p, size, stride=z.message), :] = found[
+                p * size : (p + 1) * size, :
             ]
+        block = pl.ds(start, size * z.message)
+        copies.append(
+            pltpu.make_async_copy(out_scr.at[block], out_hbm.at[block], sem.at[part])
+        )
+        copies[-1].start()
+    for copy in copies:
+        copy.wait()
 
 
 def choose_kernel(
-    z, links_ref, counts_ref, coef_ref, rate_ref, col_ref, row_ref, col_coef_ref, row_coef_ref, damp_ref
+    z, links_ref, counts_ref, coef_ref, rate_ref, own_ref, sites_ref,
+    col_ref, row_ref, col_coef_ref, row_coef_ref, damp_ref, at_ref, site_scr,
 ):
     part = lax.axis_index("sys")
+    tier = lax.axis_index("tier")
+    lane = iota((1, z.levels), 1)
+    for k in range(z.modes):
+        site_scr[k : k + 1, :] = jnp.where(lane == sites_ref[k], 1.0, 0.0)
+    at_ref[...] = site_scr[: z.modes, :].astype(BF16)
     low = part * z.block_modes
     earlier = earlier_table(z.per_slot)
     ones = jnp.ones((z.per_slot, z.per_slot), BF16)
@@ -207,6 +239,7 @@
         row_rank = rank_of(hit_rows, seen_rows, earlier)
         seen_rows = seen_rows + dot_nn(as_bf16(hit_rows), ones)
         live = target < jnp.sum(jnp.where(hit, counts, 0), axis=0, keepdims=True)
+        live = jnp.logical_and(live, own_ref[tier] > g)
         scale = jnp.where(kind == 1, level, 1)
         here = as_bf16(iota((z.cap * z.tiers, z.per_slot), 0) == rank * z.tiers + holder)
         here_row = as_bf16(
@@ -229,23 +262,25 @@
         falling = jnp.where(jnp.logical_and(modes == mode, kind == 1), level, 0).astype(F32)
         amount = jnp.sum(falling, axis=1, keepdims=True) * rate
         damp_ref[g] = jnp.broadcast_to(jnp.sum(amount, axis=0, keepdims=True), (8, LANES))
-        for c in range(2):
-            col_coef_ref[c, g * z.modes : (g + 1) * z.modes, :] = jnp.broadcast_to(
-                coefs[c], (z.modes, LANES)
-            )
-            mine = jnp.where(
-                iota((z.group, z.modes), 0) + low == iota((z.group, z.modes), 1),
-                coef_ref[c : c + 1, :],
-                0.0,
-            )
-            mine = jnp.where(iota((z.group, z.modes), 0) < z.block_modes, mine, 0.0)
-            row_coef_ref[c, g * z.group : (g + 1) * z.group, :] = jnp.broadcast_to(
-                jnp.sum(mine, axis=1, keepdims=True), (z.group, LANES)
-            )
-
-
-def band_kernel(z, mid_ref, low_ref, high_ref, bands_ref, damp_ref, out_ref, wide, spread, across_ref):
+    for c in range(2):
+        col_coef_ref[c] = jnp.broadcast_to(coefs[c], (z.modes, LANES))
+        mine = jnp.where(
+            iota((z.group, z.modes), 0) + low == iota((z.group, z.modes), 1),
+            coef_ref[c : c + 1, :],
+            0.0,
+        )
+        mine = jnp.where(iota((z.group, z.modes), 0) < z.block_modes, mine, 0.0)
+        row_coef_ref[c] = jnp.broadcast_to(
+            jnp.sum(mine, axis=1, keepdims=True), (z.group, LANES)
+        )
+
+
+def band_kernel(
+    z, state_ref, slope_ref, low_ref, high_ref, bands_ref, damp_ref, counts_ref,
+    out_ref, wide, spread, across_ref,
+):
     part = lax.axis_index("sys")
+    own = counts_ref[lax.axis_index("tier")]
     taps = 2 * z.band + 1
     across_ref[...] = jnp.zeros_like(across_ref)
     lane = iota((1, z.levels), 1)
@@ -257,18 +292,24 @@
         elif offset > 0:
             row = jnp.where(lane < z.levels - offset, row, 0.0)
         across_ref[t : t + 1, :] = row
-    own = iota((z.rows, z.levels), 0) + part * z.rows == iota((z.rows, z.levels), 1)
-    own = as_bf16(own)
+    here = as_bf16(
+        iota((z.rows, z.levels), 0) + part * z.rows == iota((z.rows, z.levels), 1)
+    )
     down = jnp.zeros((z.rows, across_ref.shape[0]), F32)
     for values in thirds(across_ref[...]):
-        down = down + dot_nt(own, values)
+        down = down + dot_nt(here, values)
     for t in range(taps):
         spread[t] = jnp.broadcast_to(down[:, t : t + 1], (z.rows, LANES))
     tiles = z.levels // LANES
     for g in range(z.slots):
+        live = jnp.where(g < own, 1.0, 0.0)
         damp = damp_ref[g, 0:1, 0:1]
+        fields = []
         for c in range(2):
-            field = mid_ref[g, c * z.rows : (c + 1) * z.rows, :]
+            rows = slice(c * z.rows, (c + 1) * z.rows)
+            fields.append(state_ref[g, rows, :] + (0.5 * step_size) * slope_ref[g, rows, :])
+        for c in range(2):
+            field = fields[c]
             wide[0 : z.band, :] = low_ref[g, c]
             wide[z.band : z.band + z.rows, :] = field
             wide[z.band + z.rows :, :] = high_ref[g, c]
@@ -287,28 +328,26 @@
             commuted = jnp.concatenate(sides, axis=1) - summed
             other = 1 - c
             sign = 1.0 if c == 1 else -1.0
-            mine = mid_ref[g, other * z.rows : (other + 1) * z.rows, :]
-            out_ref[g, other * z.rows : (other + 1) * z.rows, :] = sign * commuted - damp * mine
+            out_ref[g, other * z.rows : (other + 1) * z.rows, :] = (
+                live * (sign * commuted - damp * fields[other])
+            )
 
 
 def apply_kernel(
-    z, got_ref, col_ref, row_ref, col_coef_ref, row_coef_ref, deriv_ref, state_ref, slope_ref,
-    counts_ref, sites_ref, next_ref, sum_ref, site_scr, next_scr, sum_scr, sem,
+    z, got_ref, col_ref, row_ref, col_coef_ref, row_coef_ref, deriv_hbm, state_ref, slope_ref,
+    at_ref, counts_ref, sites_ref, next_ref, sum_ref, rows_scr, next_scr, sum_scr, deriv_ref,
+    sem, load_sem,
 ):
+    loads = [
+        pltpu.make_async_copy(deriv_hbm.at[g], deriv_ref.at[g], load_sem.at[g])
+        for g in range(z.slots)
+    ]
+    for load in loads:
+        load.start()
     part = lax.axis_index("sys")
     tier = lax.axis_index("tier")
-    lane = iota((1, z.levels), 1)
-    for k in range(z.modes):
-        site_scr[k : k + 1, :] = jnp.where(lane == sites_ref[k], 1.0, 0.0)
-    at_site = site_scr[: z.modes, :].astype(BF16)
+    at_site = at_ref[...]
     total = z.slots * z.modes
-    pieces = jnp.concatenate(
-        [got_ref[pl.ds(p, z.tiers, stride=z.message), :] for p in range(z.cap)], axis=0
-    )
-    found = picked(col_ref[...], pieces)
-    up, down = found[:total], found[total:]
-    sign = jnp.where(iota((1, 2 * z.rows), 1) < z.rows, -1.0, 1.0)
-    cols = col_coef_ref[1] * down + sign * pltpu.roll(up + col_coef_ref[0] * down, z.rows, 1)
     pieces = jnp.concatenate(
         [
             jnp.concatenate(
@@ -325,39 +364,43 @@
     found = picked(row_ref[...].astype(BF16), pieces)
     half = z.slots * z.group
     up, down = found[:half], found[half:]
-    turned = up + row_coef_ref[0, :, 0:1] * down
-    straight = row_coef_ref[1, :, 0:1] * down
-    rows = (
-        straight[:, : z.levels] + turned[:, z.levels :],
-        straight[:, z.levels :] - turned[:, : z.levels],
-    )
+    real = jnp.concatenate([row_coef_ref[0, :, 0:1]] * z.slots, axis=0)
+    imag = jnp.concatenate([row_coef_ref[1, :, 0:1]] * z.slots, axis=0)
+    turned = up + real * down
+    straight = imag * down
+    rows_scr[0] = straight[:, : z.levels] + turned[:, z.levels :]
+    rows_scr[1] = straight[:, z.levels :] - turned[:, : z.levels]
+    pieces = jnp.concatenate(
+        [got_ref[pl.ds(p, z.tiers, stride=z.message), :] for p in range(z.cap)], axis=0
+    )
+    found = picked(col_ref[...], pieces)
+    sign = jnp.where(iota((1, 2 * z.rows), 1) < z.rows, -1.0, 1.0)
     for g in range(z.slots):
-        mine = cols[g * z.modes : (g + 1) * z.modes, :]
-        added = deriv_ref[g]
-        for values in thirds(mine):
-            added = added + dot_tn(values, at_site)
-        next_scr[g] = added
+        up = found[g * z.modes : (g + 1) * z.modes]
+        down = found[total + g * z.modes : total + (g + 1) * z.modes]
+        cols = col_coef_ref[1] * down + sign * pltpu.roll(up + col_coef_ref[0] * down, z.rows, 1)
+        first, second = halves(cols)
+        added = dot_tn(first, at_site) + dot_tn(second, at_site)
+        loads[g].wait()
+        next_scr[g] = deriv_ref[g] + added
         for k in range(z.block_modes):
             local = sites_ref[part * z.block_modes + k] - part * z.rows
             for c in range(2):
                 at = pl.ds(c * z.rows + local, 1)
-                next_scr[g, at, :] = (
-                    next_scr[g, at, :] + rows[c][g * z.group + k : g * z.group + k + 1, :]
-                )
+                row = g * z.group + k
+                next_scr[g, at, :] = next_scr[g, at, :] + rows_scr[c, row : row + 1, :]
+        pltpu.make_async_copy(next_scr.at[g], next_ref.at[g], sem.at[0, g]).start()
         live = jnp.where(g < counts_ref[tier], 1.0, 0.0)
-        slope_next = next_scr[g] * live
-        next_scr[g] = slope_next
-        sum_scr[g] = (
-            state_ref[g] + (step_size / 6.0) * slope_ref[g] + (step_size / 3.0) * slope_next
-        ) * live
-        pltpu.make_async_copy(next_scr.at[g], next_ref.at[g], sem.at[0, g]).start()
+        sum_scr[g] = (state_ref[g] + (step_size / 6.0) * slope_ref[g]) * live + (
+            step_size / 3.0
+        ) * next_scr[g]
         pltpu.make_async_copy(sum_scr.at[g], sum_ref.at[g], sem.at[1, g]).start()
     for g in range(z.slots):
         pltpu.make_async_copy(next_scr.at[g], next_ref.at[g], sem.at[0, g]).wait()
         pltpu.make_async_copy(sum_scr.at[g], sum_ref.at[g], sem.at[1, g]).wait()
 
 
-def call(kernel, z, name, args, in_specs, outs, scratch=(), out_specs=None, micros=1):
+def call(kernel, z, name, args, in_specs, outs, scratch=(), out_specs=None, micros=1, aliases=()):
     return pl.pallas_call(
         functools.partial(kernel, z),
         out_shape=outs,
@@ -365,7 +408,8 @@
         out_specs=[VMEM] * len(outs) if out_specs is None else out_specs,
         scratch_shapes=list(scratch),
         name=name,
-        compiler_params=pltpu.CompilerParams(vmem_limit_bytes=vmem_limit),
+        input_output_aliases=dict(aliases),
+        compiler_params=pltpu.CompilerParams(vmem_limit_bytes=int(vmem_limits.get(name, 16) * mib)),
         cost_estimate=pl.CostEstimate(
             flops=int(micros * 1e6), bytes_accessed=int(micros * 1e5), transcendentals=0
         ),
@@ -392,20 +436,20 @@
         ask.reshape(z.tiers, 1, z.ask), "tier", split_axis=0, concat_axis=0, tiled=True
     ).reshape(z.tiers, z.ask)
     edge = (z.slots, 2, z.band, z.levels)
-    mid, low_edge, high_edge, col_table, row_table = call(
+    low_edge, high_edge, col_table, row_table = call(
         table_kernel,
         z,
         "tables",
         (state_flat, slope_flat, mode_site),
         [VMEM, VMEM, SMEM],
         [
-            shape(flat, F32),
             shape(edge, F32),
             shape(edge, F32),
             shape((3 * z.slots * z.modes, 2 * z.rows), BF16),
             shape((3 * z.row_pad, 2 * z.levels), BF16),
         ],
         [
+            pltpu.VMEM(flat, F32),
             pltpu.VMEM((z.row_pad, 2 * z.levels), F32),
             pltpu.VMEM((round_up(z.modes, 16), z.levels), F32),
         ],
@@ -418,6 +462,8 @@
         (asked, col_table, row_table),
         [VMEM] * 3,
         [shape((z.tiers * z.message, LANES), F32)],
+        [pltpu.VMEM((z.tiers * z.message, LANES), F32), pltpu.SemaphoreType.DMA((2,))],
+        out_specs=[HBM],
     )
     got = lax.all_to_all(
         answer.reshape(z.tiers, 1, z.message * LANES),
@@ -428,32 +474,35 @@
     ).reshape(z.tiers * z.message, LANES)
     low_edge, high_edge, answer_kept = lax.optimization_barrier((low_edge, high_edge, answer))
     above, below = neighbours(low_edge, high_edge)
-    col_choice, row_choice, col_coef, row_coef, damp = call(
+    col_choice, row_choice, col_coef, row_coef, damp, at_site = call(
         choose_kernel,
         z,
         "choose",
-        (links, counts[None], mode_coef, mode_rate[None]),
-        [VMEM] * 4,
+        (links, counts[None], mode_coef, mode_rate[None], counts, mode_site),
+        [VMEM] * 4 + [SMEM] * 2,
         [
             shape((2 * z.slots * z.modes, z.cap * z.tiers), BF16),
             shape((2 * z.slots * z.group, z.row_cap * z.tiers), F32),
-            shape((2, z.slots * z.modes, LANES), F32),
-            shape((2, z.slots * z.group, LANES), F32),
+            shape((2, z.modes, LANES), F32),
+            shape((2, z.group, LANES), F32),
             shape((z.slots, 8, LANES), F32),
+            shape((z.modes, z.levels), BF16),
         ],
+        [pltpu.VMEM((round_up(z.modes, 16), z.levels), F32)],
         micros=2,
     )
+    taps = round_up(2 * z.band + 1, 16)
     (deriv,) = call(
         band_kernel,
         z,
         "band",
-        (mid, above, below, h_bands, damp),
-        [VMEM] * 5,
+        (state_flat, slope_flat, above, below, h_bands, damp, counts),
+        [VMEM] * 6 + [SMEM],
         [shape(flat, F32)],
         [
             pltpu.VMEM((z.rows + 2 * z.band, z.levels), F32),
             pltpu.VMEM((2 * z.band + 1, z.rows, LANES), F32),
-            pltpu.VMEM((round_up(2 * z.band + 1, 16), z.levels), F32),
+            pltpu.VMEM((taps, z.levels), F32),
         ],
         micros=5,
     )
@@ -463,17 +512,20 @@
         "apply",
         (
             got, col_choice, row_choice, col_coef, row_coef, deriv, state_flat, slope_flat,
-            counts, mode_site,
+            at_site, counts, mode_site,
         ),
-        [VMEM] * 8 + [SMEM] * 2,
+        [VMEM] * 5 + [HBM] + [VMEM] * 3 + [SMEM] * 2,
         [shape(flat, F32), shape(flat, F32)],
         [
-            pltpu.VMEM((round_up(z.modes, 8), z.levels), F32),
+            pltpu.VMEM((2, z.slots * z.group, z.levels), F32),
+            pltpu.VMEM(flat, F32),
             pltpu.VMEM(flat, F32),
             pltpu.VMEM(flat, F32),
             pltpu.SemaphoreType.DMA((2, z.slots)),
+            pltpu.SemaphoreType.DMA((z.slots,)),
         ],
-        out_specs=[ANY, ANY],
+        out_specs=[HBM, HBM],
+        aliases=((5, 0),),
         micros=4,
     )
     return slope_next.reshape(state.shape), partial_sum.reshape(state.shape)

time: 61.9 us -> 60.8 us (0.982)
  local copies, waits for them, and re-layouts: 8.27 us -> 4.48 us
  Pallas kernels: 14.8 us -> 18 us
    unnamed x30 -> x22, local copies, waits for them, and re-layouts: 8.27 us -> 4.48 us
    pallas_call x6, Pallas kernels: 14.8 us -> 18 us  [call(): pl.pallas_call(functools.partial(kernel, z), out_shape=outs, in_specs=in_...]
  transfers between devices with their start and end apart: 4 -> 4, of which waited for: 3 -> 3; matrix products, arithmetic and copies ran while one was open for 0% -> 0% of each run, Pallas kernels for 13% -> 18%
where the time goes in v3:
time: 60.8 us; the launch traced here: 60.3 us
  starting transfers between devices  25.5 us (42%)
  Pallas kernels  18 us (30%)
  waiting for transfers between devices  11.6 us (19%)
  local copies, waits for them, and re-layouts  4.48 us (7%)
  between operations  0.76 us (1%)
    pallas_call x6, Pallas kernels, call(): pl.pallas_call(functools.partial(kernel, z), out_shape=outs, in_specs=in_...  18 us
    all_to_all x1, starting transfers between devices, shards(): lax.all_to_all(ask.reshape(z.tiers, 1, z.ask), 'tier', split_axis=0, conc...  14.8 us
    all_to_all x1, starting transfers between devices, shards(): lax.all_to_all(answer.reshape(z.tiers, 1, z.message * LANES), 'tier', spl...  6.19 us
    all_to_all x1, waiting for transfers between devices, shards(): lax.all_to_all(answer.reshape(z.tiers, 1, z.message * LANES), 'tier', spl...  4.97 us
    unnamed x22, local copies, waits for them, and re-layouts  4.48 us
    all_to_all x1, waiting for transfers between devices, shards(): lax.all_to_all(ask.reshape(z.tiers, 1, z.ask), 'tier', split_axis=0, conc...  4.29 us
    ppermute x1, starting transfers between devices, neighbours(): lax.ppermute(high_edge, 'sys', forward)  3.21 us
    ppermute x1, waiting for transfers between devices, neighbours(): lax.ppermute(low_edge, 'sys', backward)  2.33 us
  transfers between devices with their start and end apart: 4, of which 3 were waited for; matrix products, arithmetic and copies ran while one was open for 0% of the time, Pallas kernels for 18%

profile of v3, /device:TPU:1, one launch (start us, length us, event | category | flops | bytes accessed | tf_op | source)
XLA Modules:
  0.0 60.3 jit_solution(14243664968139406047)
XLA Ops:
  0.6 0.0 copy-start.5
  0.6 0.7 %copy-done.5 = s32[4,4,96]{2,1,0:T(4,128)S(1)} copy-done((s32[4,4,96]{2,1,0:T(4,128)S(1)}, s32[4,4,96]{2,1,0:T(4,128)}, u32[]{:S(2)}) %copy-start.5) | copy-done | bytes 6168
  1.3 1.1 %ask.1 = s32[64,16]{1,0:T(8,128)} custom-call(s32[4,4,96]{2,1,0:T(4,128)S(1)} %copy-done.5), custom_call_target="tpu_custom_call" | custom-call | flops 1000000 | bytes 100000 | tf_op jit(solution)/shard_map/ask/pallas_call | solution.py:404
  2.4 14.8 %all-to-all-start = ((s32[64,1,16]{2,1,0:T(1,128)}), s32[64,1,16]{2,1,0:T(1,128)S(1)}, u32[]{:S(2)}, u32[]{:S(2)}) async-start(s32[64,1,16]{2,1,0:T(1,128)} %bitcast.1), calls=%async_computation | async-start | bytes 65536 | tf_op jit(solution)/shard_map/all_to_all | solution.py:435
  17.2 0.0 copy-start.8
  17.3 0.6 %copy-done.8 = s32[48]{0:T(128)S(1)} copy-done((s32[48]{0:T(128)S(1)}, s32[48]{0:T(128)}, u32[]{:S(2)}) %copy-start.8) | copy-done | bytes 216
  17.9 1.2 %copy-done = f32[4,2,64,512]{3,2,1,0:T(8,128)S(1)} copy-done((f32[4,2,64,512]{3,2,1,0:T(8,128)S(1)}, f32[4,2,64,512]{3,2,1,0:T(8,128)}, u32[]{:S(2)}) %copy-start) | copy-done | bytes 1048600
  19.1 1.2 %copy-done.2 = f32[4,2,64,512]{3,2,1,0:T(8,128)S(1)} copy-done((f32[4,2,64,512]{3,2,1,0:T(8,128)S(1)}, f32[4,2,64,512]{3,2,1,0:T(8,128)}, u32[]{:S(2)}) %copy-start.2) | copy-done | bytes 1048600
  20.4 1.8 %tables.1 = (f32[4,2,8,512]{3,2,1,0:T(8,128)S(1)}, f32[4,2,8,512]{3,2,1,0:T(8,128)}, bf16[576,128]{1,0:T(8,128)(2,1)S(1)}, bf16[96,1024]{1,0:T(8,128)(2,1)S(1)}) custom-call(f32[4,128,512]{2,1,0:T(8,128)S(1)} %bitcast.12, f32[4,128,512]{2,1,0:T(8,128)S(1)} %bitcast.15, s32[48]{0:T(128)S(1)} %copy-done.8), custom_call_target="tpu_custom_call" | custom-call | flops 3000000 | bytes 300000 | tf_op jit(solution)/shard_map/tables/pallas_call | solution.py:404
  22.2 4.3 %all-to-all-done = s32[64,1,16]{2,1,0:T(1,128)S(1)} async-done(((s32[64,1,16]{2,1,0:T(1,128)}), s32[64,1,16]{2,1,0:T(1,128)S(1)}, u32[]{:S(2)}, u32[]{:S(2)}) %all-to-all-start) | async-done | bytes 4128 | tf_op jit(solution)/shard_map/all_to_all | solution.py:435
  26.5 2.0 %answer.1 = f32[1408,128]{1,0:T(8,128)} custom-call(s32[64,16]{1,0:T(8,128)S(1)} %bitcast.19, bf16[576,128]{1,0:T(8,128)(2,1)S(1)} %get-tuple-element.16.col_ref, bf16[96,1024]{1,0:T(8,128)(2,1)S(1)} %get-tuple-element.17.row_ref), custom_call_target="tpu_custom_call" | custom-call | flops 1000000 | bytes 100000 | tf_op jit(solution)/shard_map/answer/pallas_call | solution.py:404
  28.5 0.0 copy-start.6
  28.5 0.0 copy-start.10
  28.6 6.2 %all-to-all-start.1 = ((f32[64,1,2816]{2,1,0:T(1,128)}), f32[64,1,2816]{2,1,0:T(1,128)S(1)}, u32[]{:S(2)}, u32[]{:S(2)}) async-start(f32[64,1,2816]{2,1,0:T(1,128)} %bitcast.5), calls=%async_computation.1 | async-start | bytes 1441792 | tf_op jit(solution)/shard_map/all_to_all | solution.py:468
  34.7 3.2 %collective-permute-start = (f32[4,2,8,512]{3,2,1,0:T(8,128)}, f32[4,2,8,512]{3,2,1,0:T(8,128)S(1)}, u32[]{:S(2)}, u32[]{:S(2)}) collective-permute-start(f32[4,2,8,512]{3,2,1,0:T(8,128)} %get-tuple-element.24), channel_id=1, source_target_pairs={{0,1},{1,2},{2,3},{3,4},{4,5},{5,6},{6,7},{8,9},{9,10},{10,11},{11... | collective-permute-start | bytes 393224 | tf_op jit(solution)/shard_map/ppermute | solution.py:423
  38.0 1.3 %collective-permute-start.1 = (f32[4,2,8,512]{3,2,1,0:T(8,128)S(1)}, f32[4,2,8,512]{3,2,1,0:T(8,128)S(1)}, u32[]{:S(2)}, u32[]{:S(2)}) collective-permute-start(f32[4,2,8,512]{3,2,1,0:T(8,128)S(1)} %get-tuple-element.25), channel_id=1, source_target_pairs={{1,0},{2,1},{3,2},{4,3},{5,4},{6,5},{7,6},{9,8},{10,9},{11,10},{12... | collective-permute-start | bytes 393224 | tf_op jit(solution)/shard_map/ppermute | solution.py:423
  39.3 0.0 copy-start.9
  39.3 0.6 %copy-done.7 = s32[64]{0:T(128)S(1)} copy-done((s32[64]{0:T(128)S(1)}, s32[64]{0:T(128)}, u32[]{:S(2)}) %copy-start.7) | copy-done | bytes 280
  39.9 0.0 copy-done.9
  40.0 1.9 %choose.1 = (bf16[384,384]{1,0:T(8,128)(2,1)S(1)}, f32[64,128]{1,0:T(8,128)S(1)}, f32[2,48,128]{2,1,0:T(8,128)S(1)}, f32[2,8,128]{2,1,0:T(8,128)S(1)}, f32[4,8,1...) custom-call(s32[4,4,96]{2,1,0:T(4,128)S(1)} %copy-done.6, s32[1,64]{1,0:T(1,128)S(1)} %bitcast.20, f32[2,48]{1,0:T(2,128)S(1)} %copy-done.9, ...), custom_call_target="tpu_custom_call" | custom-call | flops 2000000 | bytes 200000 | tf_op jit(solution)/shard_map/choose/pallas_call | solution.py:404
  41.8 2.3 %collective-permute-done.1.high_ref = f32[4,2,8,512]{3,2,1,0:T(8,128)S(1)} collective-permute-done((f32[4,2,8,512]{3,2,1,0:T(8,128)S(1)}, f32[4,2,8,512]{3,2,1,0:T(8,128)S(1)}, u32[]{:S(2)}, u32[]{:S(2)}) %collective-permute-start.1) | collective-permute-done | bytes 131104 | tf_op jit(solution)/shard_map/ppermute | solution.py:423
  44.2 7.2 %band.1.deriv_hbm = f32[4,128,512]{2,1,0:T(8,128)} custom-call(f32[4,128,512]{2,1,0:T(8,128)S(1)} %bitcast.13, f32[4,128,512]{2,1,0:T(8,128)S(1)} %bitcast.16, f32[4,2,8,512]{3,2,1,0:T(8,128)S(1)} %collective-permute-done.low_ref, f32[4,2,8,512]{3,2,1,0:T(8,128)S(1)} %collective-permute-done.1.high_ref, f32[9,512]{1,0:T(8,128)S(1)} %copy-done.4, ...), custom_call_target="tpu_custom_call" | custom-call | flops 5000000 | bytes 500000 | tf_op jit(solution)/shard_map/band/pallas_call | solution.py:404
  51.4 5.0 %all-to-all-done.1 = f32[64,1,2816]{2,1,0:T(1,128)S(1)} async-done(((f32[64,1,2816]{2,1,0:T(1,128)}), f32[64,1,2816]{2,1,0:T(1,128)S(1)}, u32[]{:S(2)}, u32[]{:S(2)}) %all-to-all-start.1) | async-done | bytes 720928 | tf_op jit(solution)/shard_map/all_to_all | solution.py:468
  56.4 4.0 %apply.1 = (f32[4,128,512]{2,1,0:T(8,128)}, f32[4,128,512]{2,1,0:T(8,128)}) custom-call(f32[1408,128]{1,0:T(8,128)S(1)} %bitcast.18, bf16[384,384]{1,0:T(8,128)(2,1)S(1)} %get-tuple-element.18.col_ref, f32[64,128]{1,0:T(8,128)S(1)} %get-tuple-element.19.row_ref, f32[2,48,128]{2,1,0:T(8,128)S(1)} %get-tuple-element.20.col_coef_ref, ...), custom_call_target="tpu_custom_call", output_to_operand_aliasing={{0}: (5, {})} | custom-call | flops 4000000 | bytes 400000 | tf_op jit(solution)/shard_map/apply/pallas_call | solution.py:404
  (12 shorter events, 0.0 us)
Async XLA Ops:
  0.6 0.7 %copy-start.5 = (s32[4,4,96]{2,1,0:T(4,128)S(1)}, s32[4,4,96]{2,1,0:T(4,128)}, u32[]{:S(2)}) copy-start(s32[4,4,96]{2,1,0:T(4,128)} %links_ref.3) | copy-start | bytes 18436
  2.4 24.1 %all-to-all-start = ((s32[64,1,16]{2,1,0:T(1,128)}), s32[64,1,16]{2,1,0:T(1,128)S(1)}, u32[]{:S(2)}, u32[]{:S(2)}) async-start(s32[64,1,16]{2,1,0:T(1,128)} %bitcast.1), calls=%async_computation | async-start | bytes 65536 | tf_op jit(solution)/shard_map/all_to_all | solution.py:435
  17.2 0.7 %copy-start.8 = (s32[48]{0:T(128)S(1)}, s32[48]{0:T(128)}, u32[]{:S(2)}) copy-start(s32[48]{0:T(128)} %sites_ref.5) | copy-start | bytes 580
  17.9 1.2 %copy-start = (f32[4,2,64,512]{3,2,1,0:T(8,128)S(1)}, f32[4,2,64,512]{3,2,1,0:T(8,128)}, u32[]{:S(2)}) copy-start(f32[4,2,64,512]{3,2,1,0:T(8,128)} %param.8) | copy-start | bytes 3145732
  19.1 1.2 %copy-start.2 = (f32[4,2,64,512]{3,2,1,0:T(8,128)S(1)}, f32[4,2,64,512]{3,2,1,0:T(8,128)}, u32[]{:S(2)}) copy-start(f32[4,2,64,512]{3,2,1,0:T(8,128)} %param.9) | copy-start | bytes 3145732
  26.5 17.7 %copy-start.1 = (f32[4,2,64,512]{3,2,1,0:T(8,128)S(1)}, f32[4,2,64,512]{3,2,1,0:T(8,128)}, u32[]{:S(2)}) copy-start(f32[4,2,64,512]{3,2,1,0:T(8,128)} %param.8) | copy-start | bytes 3145732
  26.5 17.7 %copy-start.3 = (f32[4,2,64,512]{3,2,1,0:T(8,128)S(1)}, f32[4,2,64,512]{3,2,1,0:T(8,128)}, u32[]{:S(2)}) copy-start(f32[4,2,64,512]{3,2,1,0:T(8,128)} %param.9) | copy-start | bytes 3145732
  28.5 10.8 %copy-start.6 = (s32[4,4,96]{2,1,0:T(4,128)S(1)}, s32[4,4,96]{2,1,0:T(4,128)}, u32[]{:S(2)}) copy-start(s32[4,4,96]{2,1,0:T(4,128)} %links_ref.3) | copy-start | bytes 18436
  28.5 10.8 %copy-start.10 = (f32[48]{0:T(128)S(1)}, f32[48]{0:T(128)}, u32[]{:S(2)}) copy-start(f32[48]{0:T(128)} %param.14) | copy-start | bytes 580
  28.5 15.6 %copy-start.4 = (f32[9,512]{1,0:T(8,128)S(1)}, f32[9,512]{1,0:T(8,128)}, u32[]{:S(2)}) copy-start(f32[9,512]{1,0:T(8,128)} %bands_ref.1) | copy-start | bytes 55300
  28.6 27.8 %all-to-all-start.1 = ((f32[64,1,2816]{2,1,0:T(1,128)}), f32[64,1,2816]{2,1,0:T(1,128)S(1)}, u32[]{:S(2)}, u32[]{:S(2)}) async-start(f32[64,1,2816]{2,1,0:T(1,128)} %bitcast.5), calls=%async_computation.1 | async-start | bytes 1441792 | tf_op jit(solution)/shard_map/all_to_all | solution.py:468
  34.7 7.1 %collective-permute-start = (f32[4,2,8,512]{3,2,1,0:T(8,128)}, f32[4,2,8,512]{3,2,1,0:T(8,128)S(1)}, u32[]{:S(2)}, u32[]{:S(2)}) collective-permute-start(f32[4,2,8,512]{3,2,1,0:T(8,128)} %get-tuple-element.24), channel_id=1, source_target_pairs={{0,1},{1,2},{2,3},{3,4},{4,5},{5,6},{6,7},{8,9},{9,10},{10,11},{11... | collective-permute-start | bytes 393224 | tf_op jit(solution)/shard_map/ppermute | solution.py:423
  38.0 6.2 %collective-permute-start.1 = (f32[4,2,8,512]{3,2,1,0:T(8,128)S(1)}, f32[4,2,8,512]{3,2,1,0:T(8,128)S(1)}, u32[]{:S(2)}, u32[]{:S(2)}) collective-permute-start(f32[4,2,8,512]{3,2,1,0:T(8,128)S(1)} %get-tuple-element.25), channel_id=1, source_target_pairs={{1,0},{2,1},{3,2},{4,3},{5,4},{6,5},{7,6},{9,8},{10,9},{11,10},{12... | collective-permute-start | bytes 393224 | tf_op jit(solution)/shard_map/ppermute | solution.py:423
  39.3 0.7 %copy-start.7 = (s32[64]{0:T(128)S(1)}, s32[64]{0:T(128)}, u32[]{:S(2)}) copy-start(s32[64]{0:T(128)} %counts_ref.3) | copy-start | bytes 772
  39.3 0.7 %copy-start.9 = (f32[2,48]{1,0:T(2,128)S(1)}, f32[2,48]{1,0:T(2,128)}, u32[]{:S(2)}) copy-start(f32[2,48]{1,0:T(2,128)} %coef_ref.1) | copy-start | bytes 1156

commit v4 on v3

--- a/solution.py
+++ b/solution.py
@@ -52,8 +52,9 @@
 
 
 def picked(chooser, values):
-    first, second = halves(values)
-    return dot_nn(chooser, first) + dot_nn(chooser, second)
+    return dot_nn(
+        jnp.concatenate([chooser, chooser], axis=1), jnp.concatenate(halves(values), axis=0)
+    )
 
 
 def as_bf16(mask):
@@ -83,6 +84,7 @@
         self.message = self.cap + self.row_cap * self.lane_tiles
         self.ask = round_up(2 * self.cap, 16)
         self.shift = self.slots.bit_length() - 1
+        self.span = round_up(self.slots * self.modes, LANES)
         self.row_pad = round_up(self.slots * self.block_modes, 16)
         self.group = round_up(self.block_modes, 8)
 
@@ -123,89 +125,77 @@
 
 
 def table_kernel(
-    z, state_ref, slope_ref, sites_ref, low_ref, high_ref, col_ref, row_ref,
-    mid_scr, rows_scr, site_scr,
+    z, state_ref, slope_ref, sites_ref, counts_ref, low_ref, high_ref, col_ref, row_ref, mid_ref,
+    base_ref, rows_scr, site_scr,
 ):
+    own = counts_ref[lax.axis_index("tier")]
     part = lax.axis_index("sys")
-    span = z.slots * z.modes
     lane = iota((1, z.levels), 1)
+    used = z.slots * z.modes
+    for third in range(3):
+        if z.span > used:
+            col_ref[third * z.span + used : (third + 1) * z.span, :] = jnp.zeros(
+                (z.span - used, 2 * z.rows), BF16
+            )
     for k in range(z.modes):
         site_scr[k : k + 1, :] = jnp.where(lane == sites_ref[k], 1.0, 0.0)
     at_site = site_scr[: z.modes, :].astype(BF16)
     rows_scr[...] = jnp.zeros_like(rows_scr)
     for g in range(z.slots):
+        live = jnp.where(g < own, 1.0, 0.0)
+        base_ref[g] = live * (state_ref[g] + (step_size / 6.0) * slope_ref[g])
         mid = state_ref[g] + (0.5 * step_size) * slope_ref[g]
-        mid_scr[g] = mid
+        mid_ref[g] = mid
         for third, values in enumerate(thirds(mid)):
-            at = third * span + g * z.modes
+            at = third * z.span + g * z.modes
             col_ref[at : at + z.modes, :] = dot_nt(at_site, values).astype(BF16)
         for c in range(2):
             start = c * z.rows
-            low_ref[g, c] = mid_scr[g, start : start + z.band, :]
-            high_ref[g, c] = mid_scr[g, start + z.rows - z.band : start + z.rows, :]
+            low_ref[g, c] = mid_ref[g, start : start + z.band, :]
+            high_ref[g, c] = mid_ref[g, start + z.rows - z.band : start + z.rows, :]
             for k in range(z.block_modes):
                 local = sites_ref[part * z.block_modes + k] - part * z.rows
                 at = g * z.block_modes + k
-                rows_scr[at : at + 1, c * z.levels : (c + 1) * z.levels] = mid_scr[
+                rows_scr[at : at + 1, c * z.levels : (c + 1) * z.levels] = mid_ref[
                     g, pl.ds(start + local, 1), :
                 ]
     for third, values in enumerate(thirds(rows_scr[...])):
         row_ref[third * z.row_pad : (third + 1) * z.row_pad, :] = values
 
 
-def answer_kernel(z, ask_ref, col_ref, row_ref, out_hbm, out_scr, sem):
+def answer_kernel(z, ask_ref, col_ref, row_ref, out_ref):
     part = lax.axis_index("sys")
-    span = z.slots * z.modes
     low = part * z.block_modes
     asked = ask_ref[...]
     columns = []
     row_at = [jnp.full((z.tiers, 1), -1, jnp.int32) for _ in range(z.row_cap)]
     used = jnp.zeros((z.tiers, 1), jnp.int32)
+    lanes = iota((z.tiers, z.span), 1)
     for p in range(z.cap):
         target = asked[:, 2 * p : 2 * p + 1]
         mode = asked[:, 2 * p + 1 : 2 * p + 2]
-        columns.append(as_bf16(target * z.modes + mode == iota((z.tiers, span), 1)))
+        columns.append(as_bf16(target * z.modes + mode == lanes))
         inside = jnp.logical_and(mode >= low, mode < low + z.block_modes)
         where_row = target * z.block_modes + (mode - low)
         for j in range(z.row_cap):
             take = jnp.logical_and(inside, used == j)
             row_at[j] = jnp.where(take, where_row, row_at[j])
         used = used + jnp.where(inside, 1, 0)
-    lanes = iota((z.tiers, z.row_pad), 1)
-    row_choice = [as_bf16(at == lanes) for at in row_at]
-    parts = 2
-    size = z.tiers // parts
-    copies = []
-    for part in range(parts):
-        mine = slice(part * size, (part + 1) * size)
-        start = part * size * z.message
-        chosen = jnp.concatenate([choice[mine] for choice in row_choice], axis=0)
-        found = dot_nn(chosen, row_ref[: z.row_pad, :])
-        for third in (1, 2):
-            found = found + dot_nn(
-                chosen, row_ref[third * z.row_pad : (third + 1) * z.row_pad, :]
-            )
-        for j in range(z.row_cap):
-            for t in range(z.lane_tiles):
-                at = start + z.cap + j * z.lane_tiles + t
-                out_scr[pl.ds(at, size, stride=z.message), :] = found[
-                    j * size : (j + 1) * size, t * LANES : (t + 1) * LANES
-                ]
-        chosen = jnp.concatenate([choice[mine] for choice in columns], axis=0)
-        found = dot_nn(chosen, col_ref[:span, :])
-        for third in (1, 2):
-            found = found + dot_nn(chosen, col_ref[third * span : (third + 1) * span, :])
-        for p in range(z.cap):
-            out_scr[pl.ds(start + p, size, stride=z.message), :] = found[
-                p * size : (p + 1) * size, :
+    lanes = iota((z.tiers, 3 * z.row_pad), 1)
+    for third in (2, 1):
+        lanes = jnp.where(lanes >= third * z.row_pad, lanes - third * z.row_pad, lanes)
+    chosen = jnp.concatenate([as_bf16(at == lanes) for at in row_at], axis=0)
+    found = dot_nn(chosen, row_ref[...])
+    for j in range(z.row_cap):
+        for t in range(z.lane_tiles):
+            at = z.cap + j * z.lane_tiles + t
+            out_ref[pl.ds(at, z.tiers, stride=z.message), :] = found[
+                j * z.tiers : (j + 1) * z.tiers, t * LANES : (t + 1) * LANES
             ]
-        block = pl.ds(start, size * z.message)
-        copies.append(
-            pltpu.make_async_copy(out_scr.at[block], out_hbm.at[block], sem.at[part])
-        )
-        copies[-1].start()
-    for copy in copies:
-        copy.wait()
+    chosen = jnp.concatenate(columns, axis=0)
+    found = dot_nn(jnp.concatenate([chosen] * 3, axis=1), col_ref[...])
+    for p in range(z.cap):
+        out_ref[pl.ds(p, z.tiers, stride=z.message), :] = found[p * z.tiers : (p + 1) * z.tiers, :]
 
 
 def choose_kernel(
@@ -276,8 +266,8 @@
 
 
 def band_kernel(
-    z, state_ref, slope_ref, low_ref, high_ref, bands_ref, damp_ref, counts_ref,
-    out_ref, wide, spread, across_ref,
+    z, mid_ref, low_ref, high_ref, bands_ref, damp_ref, counts_ref, out_ref, wide, spread,
+    across_ref, mid_scr,
 ):
     part = lax.axis_index("sys")
     own = counts_ref[lax.axis_index("tier")]
@@ -301,13 +291,11 @@
     for t in range(taps):
         spread[t] = jnp.broadcast_to(down[:, t : t + 1], (z.rows, LANES))
     tiles = z.levels // LANES
+    mid_scr[...] = mid_ref[...]
     for g in range(z.slots):
         live = jnp.where(g < own, 1.0, 0.0)
         damp = damp_ref[g, 0:1, 0:1]
-        fields = []
-        for c in range(2):
-            rows = slice(c * z.rows, (c + 1) * z.rows)
-            fields.append(state_ref[g, rows, :] + (0.5 * step_size) * slope_ref[g, rows, :])
+        fields = [mid_scr[g, c * z.rows : (c + 1) * z.rows, :] for c in range(2)]
         for c in range(2):
             field = fields[c]
             wide[0 : z.band, :] = low_ref[g, c]
@@ -334,19 +322,11 @@
 
 
 def apply_kernel(
-    z, got_ref, col_ref, row_ref, col_coef_ref, row_coef_ref, deriv_hbm, state_ref, slope_ref,
-    at_ref, counts_ref, sites_ref, next_ref, sum_ref, rows_scr, next_scr, sum_scr, deriv_ref,
-    sem, load_sem,
+    z, got_ref, col_ref, row_ref, col_coef_ref, row_coef_ref, deriv_ref, base_ref,
+    at_ref, sites_ref, next_ref, sum_ref, rows_scr, next_scr, sum_scr, sem,
 ):
-    loads = [
-        pltpu.make_async_copy(deriv_hbm.at[g], deriv_ref.at[g], load_sem.at[g])
-        for g in range(z.slots)
-    ]
-    for load in loads:
-        load.start()
     part = lax.axis_index("sys")
-    tier = lax.axis_index("tier")
-    at_site = at_ref[...]
+    at_site = jnp.concatenate([at_ref[...]] * 2, axis=0)
     total = z.slots * z.modes
     pieces = jnp.concatenate(
         [
@@ -379,9 +359,7 @@
         up = found[g * z.modes : (g + 1) * z.modes]
         down = found[total + g * z.modes : total + (g + 1) * z.modes]
         cols = col_coef_ref[1] * down + sign * pltpu.roll(up + col_coef_ref[0] * down, z.rows, 1)
-        first, second = halves(cols)
-        added = dot_tn(first, at_site) + dot_tn(second, at_site)
-        loads[g].wait()
+        added = dot_tn(jnp.concatenate(halves(cols), axis=0), at_site)
         next_scr[g] = deriv_ref[g] + added
         for k in range(z.block_modes):
             local = sites_ref[part * z.block_modes + k] - part * z.rows
@@ -390,10 +368,7 @@
                 row = g * z.group + k
                 next_scr[g, at, :] = next_scr[g, at, :] + rows_scr[c, row : row + 1, :]
         pltpu.make_async_copy(next_scr.at[g], next_ref.at[g], sem.at[0, g]).start()
-        live = jnp.where(g < counts_ref[tier], 1.0, 0.0)
-        sum_scr[g] = (state_ref[g] + (step_size / 6.0) * slope_ref[g]) * live + (
-            step_size / 3.0
-        ) * next_scr[g]
+        sum_scr[g] = base_ref[g] + (step_size / 3.0) * next_scr[g]
         pltpu.make_async_copy(sum_scr.at[g], sum_ref.at[g], sem.at[1, g]).start()
     for g in range(z.slots):
         pltpu.make_async_copy(next_scr.at[g], next_ref.at[g], sem.at[0, g]).wait()
@@ -436,20 +411,21 @@
         ask.reshape(z.tiers, 1, z.ask), "tier", split_axis=0, concat_axis=0, tiled=True
     ).reshape(z.tiers, z.ask)
     edge = (z.slots, 2, z.band, z.levels)
-    low_edge, high_edge, col_table, row_table = call(
+    low_edge, high_edge, col_table, row_table, mid, base = call(
         table_kernel,
         z,
         "tables",
-        (state_flat, slope_flat, mode_site),
-        [VMEM, VMEM, SMEM],
+        (state_flat, slope_flat, mode_site, counts),
+        [VMEM, VMEM, SMEM, SMEM],
         [
             shape(edge, F32),
             shape(edge, F32),
-            shape((3 * z.slots * z.modes, 2 * z.rows), BF16),
+            shape((3 * z.span, 2 * z.rows), BF16),
             shape((3 * z.row_pad, 2 * z.levels), BF16),
+            shape(flat, F32),
+            shape(flat, F32),
         ],
         [
-            pltpu.VMEM(flat, F32),
             pltpu.VMEM((z.row_pad, 2 * z.levels), F32),
             pltpu.VMEM((round_up(z.modes, 16), z.levels), F32),
         ],
@@ -462,8 +438,6 @@
         (asked, col_table, row_table),
         [VMEM] * 3,
         [shape((z.tiers * z.message, LANES), F32)],
-        [pltpu.VMEM((z.tiers * z.message, LANES), F32), pltpu.SemaphoreType.DMA((2,))],
-        out_specs=[HBM],
     )
     got = lax.all_to_all(
         answer.reshape(z.tiers, 1, z.message * LANES),
@@ -496,14 +470,16 @@
         band_kernel,
         z,
         "band",
-        (state_flat, slope_flat, above, below, h_bands, damp, counts),
-        [VMEM] * 6 + [SMEM],
+        (mid, above, below, h_bands, damp, counts),
+        [VMEM] * 5 + [SMEM],
         [shape(flat, F32)],
         [
             pltpu.VMEM((z.rows + 2 * z.band, z.levels), F32),
             pltpu.VMEM((2 * z.band + 1, z.rows, LANES), F32),
             pltpu.VMEM((taps, z.levels), F32),
+            pltpu.VMEM(flat, F32),
         ],
+        aliases=((0, 0),),
         micros=5,
     )
     slope_next, partial_sum = call(
@@ -511,21 +487,17 @@
         z,
         "apply",
         (
-            got, col_choice, row_choice, col_coef, row_coef, deriv, state_flat, slope_flat,
-            at_site, counts, mode_site,
+            got, col_choice, row_choice, col_coef, row_coef, deriv, base, at_site, mode_site,
         ),
-        [VMEM] * 5 + [HBM] + [VMEM] * 3 + [SMEM] * 2,
+        [VMEM] * 8 + [SMEM],
         [shape(flat, F32), shape(flat, F32)],
         [
             pltpu.VMEM((2, z.slots * z.group, z.levels), F32),
             pltpu.VMEM(flat, F32),
             pltpu.VMEM(flat, F32),
-            pltpu.VMEM(flat, F32),
             pltpu.SemaphoreType.DMA((2, z.slots)),
-            pltpu.SemaphoreType.DMA((z.slots,)),
         ],
         out_specs=[HBM, HBM],
-        aliases=((5, 0),),
         micros=4,
     )
     return slope_next.reshape(state.shape), partial_sum.reshape(state.shape)

time: 60.8 us -> 59.5 us (0.979)
  Pallas kernels: 18 us -> 15.7 us
  waiting for transfers between devices: 11.6 us -> 12.4 us
    pallas_call x6, Pallas kernels: 18 us -> 15.7 us  [call(): pl.pallas_call(functools.partial(kernel, z), out_shape=outs, in_specs=in_...]
    all_to_all x1, waiting for transfers between devices: 4.97 us -> 6.02 us  [shards(): lax.all_to_all(answer.reshape(z.tiers, 1, z.message * LANES), 'tier', spl...]
    unnamed x22 -> x18, local copies, waits for them, and re-layouts: 4.48 us -> 4.46 us
  transfers between devices with their start and end apart: 4 -> 4, of which waited for: 3 -> 3; matrix products, arithmetic and copies ran while one was open for 0% -> 0% of each run, Pallas kernels for 18% -> 17%
where the time goes in v4:
time: 59.5 us; the launch traced here: 59.1 us
  starting transfers between devices  25.7 us (43%)
  Pallas kernels  15.7 us (26%)
  waiting for transfers between devices  12.4 us (21%)
  local copies, waits for them, and re-layouts  4.46 us (7%)
  between operations  0.73 us (1%)
    pallas_call x6, Pallas kernels, call(): pl.pallas_call(functools.partial(kernel, z), out_shape=outs, in_specs=in_...  15.7 us
    all_to_all x1, starting transfers between devices, shards(): lax.all_to_all(ask.reshape(z.tiers, 1, z.ask), 'tier', split_axis=0, conc...  14.8 us
    all_to_all x1, starting transfers between devices, shards(): lax.all_to_all(answer.reshape(z.tiers, 1, z.message * LANES), 'tier', spl...  6.39 us
    all_to_all x1, waiting for transfers between devices, shards(): lax.all_to_all(answer.reshape(z.tiers, 1, z.message * LANES), 'tier', spl...  6.02 us
    unnamed x18, local copies, waits for them, and re-layouts  4.46 us
    all_to_all x1, waiting for transfers between devices, shards(): lax.all_to_all(ask.reshape(z.tiers, 1, z.ask), 'tier', split_axis=0, conc...  4.07 us
    ppermute x1, starting transfers between devices, neighbours(): lax.ppermute(high_edge, 'sys', forward)  3.21 us
    ppermute x1, waiting for transfers between devices, neighbours(): lax.ppermute(low_edge, 'sys', backward)  2.35 us
  transfers between devices with their start and end apart: 4, of which 3 were waited for; matrix products, arithmetic and copies ran while one was open for 0% of the time, Pallas kernels for 17%

profile of v4, /device:TPU:1, one launch (start us, length us, event | category | flops | bytes accessed | tf_op | source)
XLA Modules:
  0.0 59.1 jit_solution(4372665155699443110)
XLA Ops:
  0.6 0.0 copy-start.3
  0.6 0.7 %copy-done.3 = s32[4,4,96]{2,1,0:T(4,128)S(1)} copy-done((s32[4,4,96]{2,1,0:T(4,128)S(1)}, s32[4,4,96]{2,1,0:T(4,128)}, u32[]{:S(2)}) %copy-start.3) | copy-done | bytes 6168
  1.3 1.1 %ask.1 = s32[64,16]{1,0:T(8,128)} custom-call(s32[4,4,96]{2,1,0:T(4,128)S(1)} %copy-done.3), custom_call_target="tpu_custom_call" | custom-call | flops 1000000 | bytes 100000 | tf_op jit(solution)/shard_map/ask/pallas_call | solution.py:379
  2.4 14.8 %all-to-all-start = ((s32[64,1,16]{2,1,0:T(1,128)}), s32[64,1,16]{2,1,0:T(1,128)S(1)}, u32[]{:S(2)}, u32[]{:S(2)}) async-start(s32[64,1,16]{2,1,0:T(1,128)} %bitcast.1), calls=%async_computation | async-start | bytes 65536 | tf_op jit(solution)/shard_map/all_to_all | solution.py:410
  17.2 0.0 copy-start.5
  17.3 0.0 copy-start.6
  17.3 0.6 %copy-done.5 = s32[64]{0:T(128)S(1)} copy-done((s32[64]{0:T(128)S(1)}, s32[64]{0:T(128)}, u32[]{:S(2)}) %copy-start.5) | copy-done | bytes 280
  17.9 0.0 copy-done.6
  17.9 1.2 %copy-done = f32[4,2,64,512]{3,2,1,0:T(8,128)S(1)} copy-done((f32[4,2,64,512]{3,2,1,0:T(8,128)S(1)}, f32[4,2,64,512]{3,2,1,0:T(8,128)}, u32[]{:S(2)}) %copy-start) | copy-done | bytes 1048600
  19.1 1.2 %copy-done.1 = f32[4,2,64,512]{3,2,1,0:T(8,128)S(1)} copy-done((f32[4,2,64,512]{3,2,1,0:T(8,128)S(1)}, f32[4,2,64,512]{3,2,1,0:T(8,128)}, u32[]{:S(2)}) %copy-start.1) | copy-done | bytes 1048600
  20.4 2.0 %tables.1 = (f32[4,2,8,512]{3,2,1,0:T(8,128)S(1)}, f32[4,2,8,512]{3,2,1,0:T(8,128)}, bf16[768,128]{1,0:T(8,128)(2,1)S(1)}, bf16[96,1024]{1,0:T(8,128)(2,1)S(1)},...) custom-call(f32[4,128,512]{2,1,0:T(8,128)S(1)} %bitcast.13, f32[4,128,512]{2,1,0:T(8,128)S(1)} %bitcast.14, ...), custom_call_target="tpu_custom_call" | custom-call | flops 3000000 | bytes 300000 | tf_op jit(solution)/shard_map/tables/pallas_call | solution.py:379
  22.4 4.1 %all-to-all-done = s32[64,1,16]{2,1,0:T(1,128)S(1)} async-done(((s32[64,1,16]{2,1,0:T(1,128)}), s32[64,1,16]{2,1,0:T(1,128)S(1)}, u32[]{:S(2)}, u32[]{:S(2)}) %all-to-all-start) | async-done | bytes 4128 | tf_op jit(solution)/shard_map/all_to_all | solution.py:410
  26.5 1.8 %answer.1 = f32[1408,128]{1,0:T(8,128)} custom-call(s32[64,16]{1,0:T(8,128)S(1)} %bitcast.15, bf16[768,128]{1,0:T(8,128)(2,1)S(1)} %get-tuple-element.18.col_ref, bf16[96,1024]{1,0:T(8,128)(2,1)S(1)} %get-tuple-element.19.row_ref), custom_call_target="tpu_custom_call" | custom-call | flops 1000000 | bytes 100000 | tf_op jit(solution)/shard_map/answer/pallas_call | solution.py:379
  28.3 6.4 %all-to-all-start.1 = ((f32[64,1,2816]{2,1,0:T(1,128)}), f32[64,1,2816]{2,1,0:T(1,128)S(1)}, u32[]{:S(2)}, u32[]{:S(2)}) async-start(f32[64,1,2816]{2,1,0:T(1,128)} %bitcast.5), calls=%async_computation.1 | async-start | bytes 1441792 | tf_op jit(solution)/shard_map/all_to_all | solution.py:442
  34.7 3.2 %collective-permute-start = (f32[4,2,8,512]{3,2,1,0:T(8,128)}, f32[4,2,8,512]{3,2,1,0:T(8,128)S(1)}, u32[]{:S(2)}, u32[]{:S(2)}) collective-permute-start(f32[4,2,8,512]{3,2,1,0:T(8,128)} %get-tuple-element.27), channel_id=1, source_target_pairs={{0,1},{1,2},{2,3},{3,4},{4,5},{5,6},{6,7},{8,9},{9,10},{10,11},{11... | collective-permute-start | bytes 393224 | tf_op jit(solution)/shard_map/ppermute | solution.py:398
  37.9 1.3 %collective-permute-start.1 = (f32[4,2,8,512]{3,2,1,0:T(8,128)S(1)}, f32[4,2,8,512]{3,2,1,0:T(8,128)S(1)}, u32[]{:S(2)}, u32[]{:S(2)}) collective-permute-start(f32[4,2,8,512]{3,2,1,0:T(8,128)S(1)} %get-tuple-element.28), channel_id=1, source_target_pairs={{1,0},{2,1},{3,2},{4,3},{5,4},{6,5},{7,6},{9,8},{10,9},{11,10},{12... | collective-permute-start | bytes 393224 | tf_op jit(solution)/shard_map/ppermute | solution.py:398
  39.2 0.0 copy-start.7
  39.2 0.0 copy-start.8
  39.3 0.6 %copy-done.7 = f32[2,48]{1,0:T(2,128)S(1)} copy-done((f32[2,48]{1,0:T(2,128)S(1)}, f32[2,48]{1,0:T(2,128)}, u32[]{:S(2)}) %copy-start.7) | copy-done | bytes 408
  39.9 1.9 %choose.1 = (bf16[384,384]{1,0:T(8,128)(2,1)S(1)}, f32[64,128]{1,0:T(8,128)S(1)}, f32[2,48,128]{2,1,0:T(8,128)S(1)}, f32[2,8,128]{2,1,0:T(8,128)S(1)}, f32[4,8,1...) custom-call(s32[4,4,96]{2,1,0:T(4,128)S(1)} %copy-done.4, s32[1,64]{1,0:T(1,128)S(1)} %bitcast.16, f32[2,48]{1,0:T(2,128)S(1)} %copy-done.7, ...), custom_call_target="tpu_custom_call" | custom-call | flops 2000000 | bytes 200000 | tf_op jit(solution)/shard_map/choose/pallas_call | solution.py:379
  41.8 2.3 %collective-permute-done.1.high_ref = f32[4,2,8,512]{3,2,1,0:T(8,128)S(1)} collective-permute-done((f32[4,2,8,512]{3,2,1,0:T(8,128)S(1)}, f32[4,2,8,512]{3,2,1,0:T(8,128)S(1)}, u32[]{:S(2)}, u32[]{:S(2)}) %collective-permute-start.1) | collective-permute-done | bytes 131104 | tf_op jit(solution)/shard_map/ppermute | solution.py:398
  44.1 6.1 %band.1.deriv_ref = f32[4,128,512]{2,1,0:T(8,128)S(1)} custom-call(f32[4,128,512]{2,1,0:T(8,128)S(1)} %get-tuple-element.24.mid_ref, f32[4,2,8,512]{3,2,1,0:T(8,128)S(1)} %collective-permute-done.low_ref, f32[4,2,8,512]{3,2,1,0:T(8,128)S(1)} %collective-permute-done.1.high_ref, f32[9,512]{1,0:T(8,128)S(1)} %copy-done.2, ...), custom_call_target="tpu_custom_call", output_to_operand_aliasing={{}: (0, {})} | custom-call | flops 5000000 | bytes 500000 | tf_op jit(solution)/shard_map/band/pallas_call | solution.py:379
  50.3 6.0 %all-to-all-done.1 = f32[64,1,2816]{2,1,0:T(1,128)S(1)} async-done(((f32[64,1,2816]{2,1,0:T(1,128)}), f32[64,1,2816]{2,1,0:T(1,128)S(1)}, u32[]{:S(2)}, u32[]{:S(2)}) %all-to-all-start.1) | async-done | bytes 720928 | tf_op jit(solution)/shard_map/all_to_all | solution.py:442
  56.3 2.8 %apply.1 = (f32[4,128,512]{2,1,0:T(8,128)}, f32[4,128,512]{2,1,0:T(8,128)}) custom-call(f32[1408,128]{1,0:T(8,128)S(1)} %bitcast.12, bf16[384,384]{1,0:T(8,128)(2,1)S(1)} %get-tuple-element.20.col_ref, f32[64,128]{1,0:T(8,128)S(1)} %get-tuple-element.21.row_ref, f32[2,48,128]{2,1,0:T(8,128)S(1)} %get-tuple-element.22.col_coef_ref, ...), custom_call_target="tpu_custom_call" | custom-call | flops 4000000 | bytes 400000 | tf_op jit(solution)/shard_map/apply/pallas_call | solution.py:379
  (8 shorter events, 0.0 us)
Async XLA Ops:
  0.6 0.7 %copy-start.3 = (s32[4,4,96]{2,1,0:T(4,128)S(1)}, s32[4,4,96]{2,1,0:T(4,128)}, u32[]{:S(2)}) copy-start(s32[4,4,96]{2,1,0:T(4,128)} %links_ref.3) | copy-start | bytes 18436
  2.4 24.1 %all-to-all-start = ((s32[64,1,16]{2,1,0:T(1,128)}), s32[64,1,16]{2,1,0:T(1,128)S(1)}, u32[]{:S(2)}, u32[]{:S(2)}) async-start(s32[64,1,16]{2,1,0:T(1,128)} %bitcast.1), calls=%async_computation | async-start | bytes 65536 | tf_op jit(solution)/shard_map/all_to_all | solution.py:410
  17.2 0.7 %copy-start.5 = (s32[64]{0:T(128)S(1)}, s32[64]{0:T(128)}, u32[]{:S(2)}) copy-start(s32[64]{0:T(128)} %counts_ref.3) | copy-start | bytes 772
  17.3 0.7 %copy-start.6 = (s32[48]{0:T(128)S(1)}, s32[48]{0:T(128)}, u32[]{:S(2)}) copy-start(s32[48]{0:T(128)} %sites_ref.5) | copy-start | bytes 580
  17.9 1.2 %copy-start = (f32[4,2,64,512]{3,2,1,0:T(8,128)S(1)}, f32[4,2,64,512]{3,2,1,0:T(8,128)}, u32[]{:S(2)}) copy-start(f32[4,2,64,512]{3,2,1,0:T(8,128)} %param.8) | copy-start | bytes 3145732
  19.1 1.2 %copy-start.1 = (f32[4,2,64,512]{3,2,1,0:T(8,128)S(1)}, f32[4,2,64,512]{3,2,1,0:T(8,128)}, u32[]{:S(2)}) copy-start(f32[4,2,64,512]{3,2,1,0:T(8,128)} %param.9) | copy-start | bytes 3145732
  28.3 10.9 %copy-start.4 = (s32[4,4,96]{2,1,0:T(4,128)S(1)}, s32[4,4,96]{2,1,0:T(4,128)}, u32[]{:S(2)}) copy-start(s32[4,4,96]{2,1,0:T(4,128)} %links_ref.3) | copy-start | bytes 18436
  28.3 15.8 %copy-start.2 = (f32[9,512]{1,0:T(8,128)S(1)}, f32[9,512]{1,0:T(8,128)}, u32[]{:S(2)}) copy-start(f32[9,512]{1,0:T(8,128)} %bands_ref.1) | copy-start | bytes 55300
  28.3 28.0 %all-to-all-start.1 = ((f32[64,1,2816]{2,1,0:T(1,128)}), f32[64,1,2816]{2,1,0:T(1,128)S(1)}, u32[]{:S(2)}, u32[]{:S(2)}) async-start(f32[64,1,2816]{2,1,0:T(1,128)} %bitcast.5), calls=%async_computation.1 | async-start | bytes 1441792 | tf_op jit(solution)/shard_map/all_to_all | solution.py:442
  34.7 7.1 %collective-permute-start = (f32[4,2,8,512]{3,2,1,0:T(8,128)}, f32[4,2,8,512]{3,2,1,0:T(8,128)S(1)}, u32[]{:S(2)}, u32[]{:S(2)}) collective-permute-start(f32[4,2,8,512]{3,2,1,0:T(8,128)} %get-tuple-element.27), channel_id=1, source_target_pairs={{0,1},{1,2},{2,3},{3,4},{4,5},{5,6},{6,7},{8,9},{9,10},{10,11},{11... | collective-permute-start | bytes 393224 | tf_op jit(solution)/shard_map/ppermute | solution.py:398
  37.9 6.2 %collective-permute-start.1 = (f32[4,2,8,512]{3,2,1,0:T(8,128)S(1)}, f32[4,2,8,512]{3,2,1,0:T(8,128)S(1)}, u32[]{:S(2)}, u32[]{:S(2)}) collective-permute-start(f32[4,2,8,512]{3,2,1,0:T(8,128)S(1)} %get-tuple-element.28), channel_id=1, source_target_pairs={{1,0},{2,1},{3,2},{4,3},{5,4},{6,5},{7,6},{9,8},{10,9},{11,10},{12... | collective-permute-start | bytes 393224 | tf_op jit(solution)/shard_map/ppermute | solution.py:398
  39.2 0.7 %copy-start.7 = (f32[2,48]{1,0:T(2,128)S(1)}, f32[2,48]{1,0:T(2,128)}, u32[]{:S(2)}) copy-start(f32[2,48]{1,0:T(2,128)} %coef_ref.1) | copy-start | bytes 1156
  39.2 0.7 %copy-start.8 = (f32[48]{0:T(128)S(1)}, f32[48]{0:T(128)}, u32[]{:S(2)}) copy-start(f32[48]{0:T(128)} %param.14) | copy-start | bytes 580

commit v5 on v4

--- a/solution.py
+++ b/solution.py
@@ -10,7 +10,7 @@
 step_size = 0.05
 LANES = 128
 mib = 1024 * 1024
-vmem_limits = {"tables": 16, "band": 16, "apply": 16}
+vmem_limits = {"ask": 61}
 BF16 = jnp.bfloat16
 F32 = jnp.float32
 VMEM = pl.BlockSpec(memory_space=pltpu.VMEM)
@@ -163,7 +163,7 @@
         row_ref[third * z.row_pad : (third + 1) * z.row_pad, :] = values
 
 
-def answer_kernel(z, ask_ref, col_ref, row_ref, out_ref):
+def answer_kernel(z, ask_ref, col_ref, row_ref, out_hbm, out_scr, sem):
     part = lax.axis_index("sys")
     low = part * z.block_modes
     asked = ask_ref[...]
@@ -184,18 +184,33 @@
     lanes = iota((z.tiers, 3 * z.row_pad), 1)
     for third in (2, 1):
         lanes = jnp.where(lanes >= third * z.row_pad, lanes - third * z.row_pad, lanes)
-    chosen = jnp.concatenate([as_bf16(at == lanes) for at in row_at], axis=0)
-    found = dot_nn(chosen, row_ref[...])
-    for j in range(z.row_cap):
-        for t in range(z.lane_tiles):
-            at = z.cap + j * z.lane_tiles + t
-            out_ref[pl.ds(at, z.tiers, stride=z.message), :] = found[
-                j * z.tiers : (j + 1) * z.tiers, t * LANES : (t + 1) * LANES
+    row_choice = [as_bf16(at == lanes) for at in row_at]
+    pieces = 2
+    size = z.tiers // pieces
+    copies = []
+    for piece in range(pieces):
+        mine = slice(piece * size, (piece + 1) * size)
+        start = piece * size * z.message
+        found = dot_nn(jnp.concatenate([choice[mine] for choice in row_choice], axis=0), row_ref[...])
+        for j in range(z.row_cap):
+            for t in range(z.lane_tiles):
+                at = start + z.cap + j * z.lane_tiles + t
+                out_scr[pl.ds(at, size, stride=z.message), :] = found[
+                    j * size : (j + 1) * size, t * LANES : (t + 1) * LANES
+                ]
+        chosen = jnp.concatenate([choice[mine] for choice in columns], axis=0)
+        found = dot_nn(jnp.concatenate([chosen] * 3, axis=1), col_ref[...])
+        for p in range(z.cap):
+            out_scr[pl.ds(start + p, size, stride=z.message), :] = found[
+                p * size : (p + 1) * size, :
             ]
-    chosen = jnp.concatenate(columns, axis=0)
-    found = dot_nn(jnp.concatenate([chosen] * 3, axis=1), col_ref[...])
-    for p in range(z.cap):
-        out_ref[pl.ds(p, z.tiers, stride=z.message), :] = found[p * z.tiers : (p + 1) * z.tiers, :]
+        block = pl.ds(start, size * z.message)
+        copies.append(
+            pltpu.make_async_copy(out_scr.at[block], out_hbm.at[block], sem.at[piece])
+        )
+        copies[-1].start()
+    for copy in copies:
+        copy.wait()
 
 
 def choose_kernel(
@@ -438,6 +453,8 @@
         (asked, col_table, row_table),
         [VMEM] * 3,
         [shape((z.tiers * z.message, LANES), F32)],
+        [pltpu.VMEM((z.tiers * z.message, LANES), F32), pltpu.SemaphoreType.DMA((2,))],
+        out_specs=[HBM],
     )
     got = lax.all_to_all(
         answer.reshape(z.tiers, 1, z.message * LANES),

time: 59.5 us -> 59.4 us (level)
  Pallas kernels: 15.7 us -> 16.4 us
  local copies, waits for them, and re-layouts: 4.46 us -> 3.78 us
    pallas_call x6, Pallas kernels: 15.7 us -> 16.4 us  [call(): pl.pallas_call(functools.partial(kernel, z), out_shape=outs, in_specs=in_...]
    unnamed x18 -> x16, local copies, waits for them, and re-layouts: 4.46 us -> 3.78 us
where the time goes in v5:
time: 59.4 us; the launch traced here: 59 us
  starting transfers between devices  25.6 us (43%)
  Pallas kernels  16.4 us (28%)
  waiting for transfers between devices  12.4 us (21%)
  local copies, waits for them, and re-layouts  3.78 us (6%)
  between operations  0.74 us (1%)
    pallas_call x6, Pallas kernels, call(): pl.pallas_call(functools.partial(kernel, z), out_shape=outs, in_specs=in_...  16.4 us
    all_to_all x1, starting transfers between devices, shards(): lax.all_to_all(ask.reshape(z.tiers, 1, z.ask), 'tier', split_axis=0, conc...  14.8 us
    all_to_all x1, starting transfers between devices, shards(): lax.all_to_all(answer.reshape(z.tiers, 1, z.message * LANES), 'tier', spl...  6.28 us
    all_to_all x1, waiting for transfers between devices, shards(): lax.all_to_all(answer.reshape(z.tiers, 1, z.message * LANES), 'tier', spl...  6 us
    all_to_all x1, waiting for transfers between devices, shards(): lax.all_to_all(ask.reshape(z.tiers, 1, z.ask), 'tier', split_axis=0, conc...  4.06 us
    unnamed x16, local copies, waits for them, and re-layouts  3.78 us
    ppermute x1, starting transfers between devices, neighbours(): lax.ppermute(high_edge, 'sys', forward)  3.21 us
    ppermute x1, waiting for transfers between devices, neighbours(): lax.ppermute(low_edge, 'sys', backward)  2.34 us
  transfers between devices with their start and end apart: 4, of which 3 were waited for; matrix products, arithmetic and copies ran while one was open for 0% of the time, Pallas kernels for 17%

profile of v5, /device:TPU:1, one launch (start us, length us, event | category | flops | bytes accessed | tf_op | source)
XLA Modules:
  0.0 59.0 jit_solution(3159139834487783050)
XLA Ops:
  0.6 1.8 %ask.1 = s32[64,16]{1,0:T(8,128)} custom-call(s32[4,4,96]{2,1,0:T(4,128)} %links_ref.3), custom_call_target="tpu_custom_call" | custom-call | flops 1000000 | bytes 100000 | tf_op jit(solution)/shard_map/ask/pallas_call | solution.py:394
  2.4 14.8 %all-to-all-start = ((s32[64,1,16]{2,1,0:T(1,128)}), s32[64,1,16]{2,1,0:T(1,128)S(1)}, u32[]{:S(2)}, u32[]{:S(2)}) async-start(s32[64,1,16]{2,1,0:T(1,128)} %bitcast.18), calls=%async_computation | async-start | bytes 65536 | tf_op jit(solution)/shard_map/all_to_all | solution.py:425
  17.2 0.0 copy-start.4
  17.3 0.0 copy-start.5
  17.3 0.6 %copy-done.4 = s32[64]{0:T(128)S(1)} copy-done((s32[64]{0:T(128)S(1)}, s32[64]{0:T(128)}, u32[]{:S(2)}) %copy-start.4) | copy-done | bytes 280
  17.9 0.0 copy-done.5
  17.9 1.2 %copy-done = f32[4,2,64,512]{3,2,1,0:T(8,128)S(1)} copy-done((f32[4,2,64,512]{3,2,1,0:T(8,128)S(1)}, f32[4,2,64,512]{3,2,1,0:T(8,128)}, u32[]{:S(2)}) %copy-start) | copy-done | bytes 1048600
  19.1 1.2 %copy-done.1 = f32[4,2,64,512]{3,2,1,0:T(8,128)S(1)} copy-done((f32[4,2,64,512]{3,2,1,0:T(8,128)S(1)}, f32[4,2,64,512]{3,2,1,0:T(8,128)}, u32[]{:S(2)}) %copy-start.1) | copy-done | bytes 1048600
  20.4 2.1 %tables.1 = (f32[4,2,8,512]{3,2,1,0:T(8,128)S(1)}, f32[4,2,8,512]{3,2,1,0:T(8,128)}, bf16[768,128]{1,0:T(8,128)(2,1)S(1)}, bf16[96,1024]{1,0:T(8,128)(2,1)S(1)},...) custom-call(f32[4,128,512]{2,1,0:T(8,128)S(1)} %bitcast.13, f32[4,128,512]{2,1,0:T(8,128)S(1)} %bitcast.14, ...), custom_call_target="tpu_custom_call" | custom-call | flops 3000000 | bytes 300000 | tf_op jit(solution)/shard_map/tables/pallas_call | solution.py:394
  22.4 4.1 %all-to-all-done = s32[64,1,16]{2,1,0:T(1,128)S(1)} async-done(((s32[64,1,16]{2,1,0:T(1,128)}), s32[64,1,16]{2,1,0:T(1,128)S(1)}, u32[]{:S(2)}, u32[]{:S(2)}) %all-to-all-start) | async-done | bytes 4128 | tf_op jit(solution)/shard_map/all_to_all | solution.py:425
  26.5 1.8 %answer.1 = f32[1408,128]{1,0:T(8,128)} custom-call(s32[64,16]{1,0:T(8,128)S(1)} %bitcast.15, bf16[768,128]{1,0:T(8,128)(2,1)S(1)} %get-tuple-element.18.col_ref, bf16[96,1024]{1,0:T(8,128)(2,1)S(1)} %get-tuple-element.19.row_ref), custom_call_target="tpu_custom_call" | custom-call | flops 1000000 | bytes 100000 | tf_op jit(solution)/shard_map/answer/pallas_call | solution.py:394
  28.3 0.0 copy-start.3
  28.3 0.0 copy-start.2
  28.3 6.3 %all-to-all-start.1 = ((f32[64,1,2816]{2,1,0:T(1,128)}), f32[64,1,2816]{2,1,0:T(1,128)S(1)}, u32[]{:S(2)}, u32[]{:S(2)}) async-start(f32[64,1,2816]{2,1,0:T(1,128)} %bitcast.5), calls=%async_computation.1 | async-start | bytes 1441792 | tf_op jit(solution)/shard_map/all_to_all | solution.py:459
  34.6 3.2 %collective-permute-start = (f32[4,2,8,512]{3,2,1,0:T(8,128)}, f32[4,2,8,512]{3,2,1,0:T(8,128)S(1)}, u32[]{:S(2)}, u32[]{:S(2)}) collective-permute-start(f32[4,2,8,512]{3,2,1,0:T(8,128)} %get-tuple-element.27), channel_id=1, source_target_pairs={{0,1},{1,2},{2,3},{3,4},{4,5},{5,6},{6,7},{8,9},{9,10},{10,11},{11... | collective-permute-start | bytes 393224 | tf_op jit(solution)/shard_map/ppermute | solution.py:413
  37.8 1.3 %collective-permute-start.1 = (f32[4,2,8,512]{3,2,1,0:T(8,128)S(1)}, f32[4,2,8,512]{3,2,1,0:T(8,128)S(1)}, u32[]{:S(2)}, u32[]{:S(2)}) collective-permute-start(f32[4,2,8,512]{3,2,1,0:T(8,128)S(1)} %get-tuple-element.28), channel_id=1, source_target_pairs={{1,0},{2,1},{3,2},{4,3},{5,4},{6,5},{7,6},{9,8},{10,9},{11,10},{12... | collective-permute-start | bytes 393224 | tf_op jit(solution)/shard_map/ppermute | solution.py:413
  39.1 0.0 copy-start.6
  39.1 0.0 copy-start.7
  39.2 0.6 %copy-done.6 = f32[2,48]{1,0:T(2,128)S(1)} copy-done((f32[2,48]{1,0:T(2,128)S(1)}, f32[2,48]{1,0:T(2,128)}, u32[]{:S(2)}) %copy-start.6) | copy-done | bytes 408
  39.8 1.9 %choose.1 = (bf16[384,384]{1,0:T(8,128)(2,1)S(1)}, f32[64,128]{1,0:T(8,128)S(1)}, f32[2,48,128]{2,1,0:T(8,128)S(1)}, f32[2,8,128]{2,1,0:T(8,128)S(1)}, f32[4,8,1...) custom-call(s32[4,4,96]{2,1,0:T(4,128)S(1)} %copy-done.3, s32[1,64]{1,0:T(1,128)S(1)} %bitcast.16, f32[2,48]{1,0:T(2,128)S(1)} %copy-done.6, ...), custom_call_target="tpu_custom_call" | custom-call | flops 2000000 | bytes 200000 | tf_op jit(solution)/shard_map/choose/pallas_call | solution.py:394
  41.7 2.3 %collective-permute-done.1.high_ref = f32[4,2,8,512]{3,2,1,0:T(8,128)S(1)} collective-permute-done((f32[4,2,8,512]{3,2,1,0:T(8,128)S(1)}, f32[4,2,8,512]{3,2,1,0:T(8,128)S(1)}, u32[]{:S(2)}, u32[]{:S(2)}) %collective-permute-start.1) | collective-permute-done | bytes 131104 | tf_op jit(solution)/shard_map/ppermute | solution.py:413
  44.0 6.2 %band.1.deriv_ref = f32[4,128,512]{2,1,0:T(8,128)S(1)} custom-call(f32[4,128,512]{2,1,0:T(8,128)S(1)} %get-tuple-element.24.mid_ref, f32[4,2,8,512]{3,2,1,0:T(8,128)S(1)} %collective-permute-done.low_ref, f32[4,2,8,512]{3,2,1,0:T(8,128)S(1)} %collective-permute-done.1.high_ref, f32[9,512]{1,0:T(8,128)S(1)} %copy-done.2, ...), custom_call_target="tpu_custom_call", output_to_operand_aliasing={{}: (0, {})} | custom-call | flops 5000000 | bytes 500000 | tf_op jit(solution)/shard_map/band/pallas_call | solution.py:394
  50.2 6.0 %all-to-all-done.1 = f32[64,1,2816]{2,1,0:T(1,128)S(1)} async-done(((f32[64,1,2816]{2,1,0:T(1,128)}), f32[64,1,2816]{2,1,0:T(1,128)S(1)}, u32[]{:S(2)}, u32[]{:S(2)}) %all-to-all-start.1) | async-done | bytes 720928 | tf_op jit(solution)/shard_map/all_to_all | solution.py:459
  56.2 2.8 %apply.1 = (f32[4,128,512]{2,1,0:T(8,128)}, f32[4,128,512]{2,1,0:T(8,128)}) custom-call(f32[1408,128]{1,0:T(8,128)S(1)} %bitcast.12, bf16[384,384]{1,0:T(8,128)(2,1)S(1)} %get-tuple-element.20.col_ref, f32[64,128]{1,0:T(8,128)S(1)} %get-tuple-element.21.row_ref, f32[2,48,128]{2,1,0:T(8,128)S(1)} %get-tuple-element.22.col_coef_ref, ...), custom_call_target="tpu_custom_call" | custom-call | flops 4000000 | bytes 400000 | tf_op jit(solution)/shard_map/apply/pallas_call | solution.py:394
  (6 shorter events, 0.0 us)
Async XLA Ops:
  2.4 24.1 %all-to-all-start = ((s32[64,1,16]{2,1,0:T(1,128)}), s32[64,1,16]{2,1,0:T(1,128)S(1)}, u32[]{:S(2)}, u32[]{:S(2)}) async-start(s32[64,1,16]{2,1,0:T(1,128)} %bitcast.18), calls=%async_computation | async-start | bytes 65536 | tf_op jit(solution)/shard_map/all_to_all | solution.py:425
  17.2 0.7 %copy-start.4 = (s32[64]{0:T(128)S(1)}, s32[64]{0:T(128)}, u32[]{:S(2)}) copy-start(s32[64]{0:T(128)} %counts_ref.3) | copy-start | bytes 772
  17.3 0.7 %copy-start.5 = (s32[48]{0:T(128)S(1)}, s32[48]{0:T(128)}, u32[]{:S(2)}) copy-start(s32[48]{0:T(128)} %sites_ref.5) | copy-start | bytes 580
  17.9 1.2 %copy-start = (f32[4,2,64,512]{3,2,1,0:T(8,128)S(1)}, f32[4,2,64,512]{3,2,1,0:T(8,128)}, u32[]{:S(2)}) copy-start(f32[4,2,64,512]{3,2,1,0:T(8,128)} %param.8) | copy-start | bytes 3145732
  19.1 1.2 %copy-start.1 = (f32[4,2,64,512]{3,2,1,0:T(8,128)S(1)}, f32[4,2,64,512]{3,2,1,0:T(8,128)}, u32[]{:S(2)}) copy-start(f32[4,2,64,512]{3,2,1,0:T(8,128)} %param.9) | copy-start | bytes 3145732
  28.3 10.9 %copy-start.3 = (s32[4,4,96]{2,1,0:T(4,128)S(1)}, s32[4,4,96]{2,1,0:T(4,128)}, u32[]{:S(2)}) copy-start(s32[4,4,96]{2,1,0:T(4,128)} %links_ref.3) | copy-start | bytes 18436
  28.3 15.7 %copy-start.2 = (f32[9,512]{1,0:T(8,128)S(1)}, f32[9,512]{1,0:T(8,128)}, u32[]{:S(2)}) copy-start(f32[9,512]{1,0:T(8,128)} %bands_ref.1) | copy-start | bytes 55300
  28.3 27.9 %all-to-all-start.1 = ((f32[64,1,2816]{2,1,0:T(1,128)}), f32[64,1,2816]{2,1,0:T(1,128)S(1)}, u32[]{:S(2)}, u32[]{:S(2)}) async-start(f32[64,1,2816]{2,1,0:T(1,128)} %bitcast.5), calls=%async_computation.1 | async-start | bytes 1441792 | tf_op jit(solution)/shard_map/all_to_all | solution.py:459
  34.6 7.1 %collective-permute-start = (f32[4,2,8,512]{3,2,1,0:T(8,128)}, f32[4,2,8,512]{3,2,1,0:T(8,128)S(1)}, u32[]{:S(2)}, u32[]{:S(2)}) collective-permute-start(f32[4,2,8,512]{3,2,1,0:T(8,128)} %get-tuple-element.27), channel_id=1, source_target_pairs={{0,1},{1,2},{2,3},{3,4},{4,5},{5,6},{6,7},{8,9},{9,10},{10,11},{11... | collective-permute-start | bytes 393224 | tf_op jit(solution)/shard_map/ppermute | solution.py:413
  37.8 6.2 %collective-permute-start.1 = (f32[4,2,8,512]{3,2,1,0:T(8,128)S(1)}, f32[4,2,8,512]{3,2,1,0:T(8,128)S(1)}, u32[]{:S(2)}, u32[]{:S(2)}) collective-permute-start(f32[4,2,8,512]{3,2,1,0:T(8,128)S(1)} %get-tuple-element.28), channel_id=1, source_target_pairs={{1,0},{2,1},{3,2},{4,3},{5,4},{6,5},{7,6},{9,8},{10,9},{11,10},{12... | collective-permute-start | bytes 393224 | tf_op jit(solution)/shard_map/ppermute | solution.py:413
  39.1 0.7 %copy-start.6 = (f32[2,48]{1,0:T(2,128)S(1)}, f32[2,48]{1,0:T(2,128)}, u32[]{:S(2)}) copy-start(f32[2,48]{1,0:T(2,128)} %coef_ref.1) | copy-start | bytes 1156
  39.1 0.7 %copy-start.7 = (f32[48]{0:T(128)S(1)}, f32[48]{0:T(128)}, u32[]{:S(2)}) copy-start(f32[48]{0:T(128)} %param.14) | copy-start | bytes 580

commit v6 on v4

--- a/solution.py
+++ b/solution.py
@@ -323,7 +323,7 @@
 
 def apply_kernel(
     z, got_ref, col_ref, row_ref, col_coef_ref, row_coef_ref, deriv_ref, base_ref,
-    at_ref, sites_ref, next_ref, sum_ref, rows_scr, next_scr, sum_scr, sem,
+    at_ref, sites_ref, next_ref, sum_ref, next_scr, sum_scr, sem,
 ):
     part = lax.axis_index("sys")
     at_site = jnp.concatenate([at_ref[...]] * 2, axis=0)
@@ -348,8 +348,15 @@
     imag = jnp.concatenate([row_coef_ref[1, :, 0:1]] * z.slots, axis=0)
     turned = up + real * down
     straight = imag * down
-    rows_scr[0] = straight[:, : z.levels] + turned[:, z.levels :]
-    rows_scr[1] = straight[:, z.levels :] - turned[:, : z.levels]
+    real_rows = straight[:, : z.levels] + turned[:, z.levels :]
+    imag_rows = straight[:, z.levels :] - turned[:, : z.levels]
+    target = jnp.full((2 * z.group, 2 * z.rows), -1, jnp.int32)
+    line = iota((2 * z.group, 2 * z.rows), 0)
+    for k in range(z.block_modes):
+        local = sites_ref[part * z.block_modes + k] - part * z.rows
+        for c in range(2):
+            target = jnp.where(line == c * z.group + k, c * z.rows + local, target)
+    at_row = as_bf16(iota((2 * z.group, 2 * z.rows), 1) == target)
     pieces = jnp.concatenate(
         [got_ref[pl.ds(p, z.tiers, stride=z.message), :] for p in range(z.cap)], axis=0
     )
@@ -359,16 +366,15 @@
         up = found[g * z.modes : (g + 1) * z.modes]
         down = found[total + g * z.modes : total + (g + 1) * z.modes]
         cols = col_coef_ref[1] * down + sign * pltpu.roll(up + col_coef_ref[0] * down, z.rows, 1)
-        added = dot_tn(jnp.concatenate(halves(cols), axis=0), at_site)
-        next_scr[g] = deriv_ref[g] + added
-        for k in range(z.block_modes):
-            local = sites_ref[part * z.block_modes + k] - part * z.rows
-            for c in range(2):
-                at = pl.ds(c * z.rows + local, 1)
-                row = g * z.group + k
-                next_scr[g, at, :] = next_scr[g, at, :] + rows_scr[c, row : row + 1, :]
+        mine = slice(g * z.group, (g + 1) * z.group)
+        own = halves(jnp.concatenate([real_rows[mine], imag_rows[mine]], axis=0))
+        slope_next = deriv_ref[g] + dot_tn(
+            jnp.concatenate([*halves(cols), at_row, at_row], axis=0),
+            jnp.concatenate([at_site, *own], axis=0),
+        )
+        next_scr[g] = slope_next
         pltpu.make_async_copy(next_scr.at[g], next_ref.at[g], sem.at[0, g]).start()
-        sum_scr[g] = base_ref[g] + (step_size / 3.0) * next_scr[g]
+        sum_scr[g] = base_ref[g] + (step_size / 3.0) * slope_next
         pltpu.make_async_copy(sum_scr.at[g], sum_ref.at[g], sem.at[1, g]).start()
     for g in range(z.slots):
         pltpu.make_async_copy(next_scr.at[g], next_ref.at[g], sem.at[0, g]).wait()
@@ -492,7 +498,6 @@
         [VMEM] * 8 + [SMEM],
         [shape(flat, F32), shape(flat, F32)],
         [
-            pltpu.VMEM((2, z.slots * z.group, z.levels), F32),
             pltpu.VMEM(flat, F32),
             pltpu.VMEM(flat, F32),
             pltpu.SemaphoreType.DMA((2, z.slots)),

time: 59.5 us -> 59.5 us (level)
  no operation moved by 1% of the time
where the time goes in v6:
time: 59.5 us; the launch traced here: 59 us
  starting transfers between devices  25.7 us (43%)
  Pallas kernels  15.7 us (26%)
  waiting for transfers between devices  12.4 us (21%)
  local copies, waits for them, and re-layouts  4.46 us (7%)
  between operations  0.73 us (1%)
    pallas_call x6, Pallas kernels, call(): pl.pallas_call(functools.partial(kernel, z), out_shape=outs, in_specs=in_...  15.7 us
    all_to_all x1, starting transfers between devices, shards(): lax.all_to_all(ask.reshape(z.tiers, 1, z.ask), 'tier', split_axis=0, conc...  14.8 us
    all_to_all x1, starting transfers between devices, shards(): lax.all_to_all(answer.reshape(z.tiers, 1, z.message * LANES), 'tier', spl...  6.39 us
    all_to_all x1, waiting for transfers between devices, shards(): lax.all_to_all(answer.reshape(z.tiers, 1, z.message * LANES), 'tier', spl...  6.02 us
    unnamed x18, local copies, waits for them, and re-layouts  4.46 us
    all_to_all x1, waiting for transfers between devices, shards(): lax.all_to_all(ask.reshape(z.tiers, 1, z.ask), 'tier', split_axis=0, conc...  4.07 us
    ppermute x1, starting transfers between devices, neighbours(): lax.ppermute(high_edge, 'sys', forward)  3.21 us
    ppermute x1, waiting for transfers between devices, neighbours(): lax.ppermute(low_edge, 'sys', backward)  2.35 us
  transfers between devices with their start and end apart: 4, of which 3 were waited for; matrix products, arithmetic and copies ran while one was open for 0% of the time, Pallas kernels for 17%

profile of v6, /device:TPU:1, one launch (start us, length us, event | category | flops | bytes accessed | tf_op | source)
XLA Modules:
  0.0 59.0 jit_solution(17269633647830257772)
XLA Ops:
  0.6 0.0 copy-start.3
  0.6 0.7 %copy-done.3 = s32[4,4,96]{2,1,0:T(4,128)S(1)} copy-done((s32[4,4,96]{2,1,0:T(4,128)S(1)}, s32[4,4,96]{2,1,0:T(4,128)}, u32[]{:S(2)}) %copy-start.3) | copy-done | bytes 6168
  1.3 1.1 %ask.1 = s32[64,16]{1,0:T(8,128)} custom-call(s32[4,4,96]{2,1,0:T(4,128)S(1)} %copy-done.3), custom_call_target="tpu_custom_call" | custom-call | flops 1000000 | bytes 100000 | tf_op jit(solution)/shard_map/ask/pallas_call | solution.py:385
  2.4 14.8 %all-to-all-start = ((s32[64,1,16]{2,1,0:T(1,128)}), s32[64,1,16]{2,1,0:T(1,128)S(1)}, u32[]{:S(2)}, u32[]{:S(2)}) async-start(s32[64,1,16]{2,1,0:T(1,128)} %bitcast.1), calls=%async_computation | async-start | bytes 65536 | tf_op jit(solution)/shard_map/all_to_all | solution.py:416
  17.2 0.0 copy-start.5
  17.3 0.0 copy-start.6
  17.3 0.6 %copy-done.5 = s32[64]{0:T(128)S(1)} copy-done((s32[64]{0:T(128)S(1)}, s32[64]{0:T(128)}, u32[]{:S(2)}) %copy-start.5) | copy-done | bytes 280
  17.9 0.0 copy-done.6
  17.9 1.2 %copy-done = f32[4,2,64,512]{3,2,1,0:T(8,128)S(1)} copy-done((f32[4,2,64,512]{3,2,1,0:T(8,128)S(1)}, f32[4,2,64,512]{3,2,1,0:T(8,128)}, u32[]{:S(2)}) %copy-start) | copy-done | bytes 1048600
  19.1 1.2 %copy-done.1 = f32[4,2,64,512]{3,2,1,0:T(8,128)S(1)} copy-done((f32[4,2,64,512]{3,2,1,0:T(8,128)S(1)}, f32[4,2,64,512]{3,2,1,0:T(8,128)}, u32[]{:S(2)}) %copy-start.1) | copy-done | bytes 1048600
  20.4 2.0 %tables.1 = (f32[4,2,8,512]{3,2,1,0:T(8,128)S(1)}, f32[4,2,8,512]{3,2,1,0:T(8,128)}, bf16[768,128]{1,0:T(8,128)(2,1)S(1)}, bf16[96,1024]{1,0:T(8,128)(2,1)S(1)},...) custom-call(f32[4,128,512]{2,1,0:T(8,128)S(1)} %bitcast.13, f32[4,128,512]{2,1,0:T(8,128)S(1)} %bitcast.14, ...), custom_call_target="tpu_custom_call" | custom-call | flops 3000000 | bytes 300000 | tf_op jit(solution)/shard_map/tables/pallas_call | solution.py:385
  22.4 4.1 %all-to-all-done = s32[64,1,16]{2,1,0:T(1,128)S(1)} async-done(((s32[64,1,16]{2,1,0:T(1,128)}), s32[64,1,16]{2,1,0:T(1,128)S(1)}, u32[]{:S(2)}, u32[]{:S(2)}) %all-to-all-start) | async-done | bytes 4128 | tf_op jit(solution)/shard_map/all_to_all | solution.py:416
  26.5 1.8 %answer.1 = f32[1408,128]{1,0:T(8,128)} custom-call(s32[64,16]{1,0:T(8,128)S(1)} %bitcast.15, bf16[768,128]{1,0:T(8,128)(2,1)S(1)} %get-tuple-element.18.col_ref, bf16[96,1024]{1,0:T(8,128)(2,1)S(1)} %get-tuple-element.19.row_ref), custom_call_target="tpu_custom_call" | custom-call | flops 1000000 | bytes 100000 | tf_op jit(solution)/shard_map/answer/pallas_call | solution.py:385
  28.3 6.4 %all-to-all-start.1 = ((f32[64,1,2816]{2,1,0:T(1,128)}), f32[64,1,2816]{2,1,0:T(1,128)S(1)}, u32[]{:S(2)}, u32[]{:S(2)}) async-start(f32[64,1,2816]{2,1,0:T(1,128)} %bitcast.5), calls=%async_computation.1 | async-start | bytes 1441792 | tf_op jit(solution)/shard_map/all_to_all | solution.py:448
  34.7 3.2 %collective-permute-start = (f32[4,2,8,512]{3,2,1,0:T(8,128)}, f32[4,2,8,512]{3,2,1,0:T(8,128)S(1)}, u32[]{:S(2)}, u32[]{:S(2)}) collective-permute-start(f32[4,2,8,512]{3,2,1,0:T(8,128)} %get-tuple-element.27), channel_id=1, source_target_pairs={{0,1},{1,2},{2,3},{3,4},{4,5},{5,6},{6,7},{8,9},{9,10},{10,11},{11... | collective-permute-start | bytes 393224 | tf_op jit(solution)/shard_map/ppermute | solution.py:404
  37.9 1.3 %collective-permute-start.1 = (f32[4,2,8,512]{3,2,1,0:T(8,128)S(1)}, f32[4,2,8,512]{3,2,1,0:T(8,128)S(1)}, u32[]{:S(2)}, u32[]{:S(2)}) collective-permute-start(f32[4,2,8,512]{3,2,1,0:T(8,128)S(1)} %get-tuple-element.28), channel_id=1, source_target_pairs={{1,0},{2,1},{3,2},{4,3},{5,4},{6,5},{7,6},{9,8},{10,9},{11,10},{12... | collective-permute-start | bytes 393224 | tf_op jit(solution)/shard_map/ppermute | solution.py:404
  39.2 0.0 copy-start.7
  39.2 0.0 copy-start.8
  39.3 0.6 %copy-done.7 = f32[2,48]{1,0:T(2,128)S(1)} copy-done((f32[2,48]{1,0:T(2,128)S(1)}, f32[2,48]{1,0:T(2,128)}, u32[]{:S(2)}) %copy-start.7) | copy-done | bytes 408
  39.9 1.9 %choose.1 = (bf16[384,384]{1,0:T(8,128)(2,1)S(1)}, f32[64,128]{1,0:T(8,128)S(1)}, f32[2,48,128]{2,1,0:T(8,128)S(1)}, f32[2,8,128]{2,1,0:T(8,128)S(1)}, f32[4,8,1...) custom-call(s32[4,4,96]{2,1,0:T(4,128)S(1)} %copy-done.4, s32[1,64]{1,0:T(1,128)S(1)} %bitcast.16, f32[2,48]{1,0:T(2,128)S(1)} %copy-done.7, ...), custom_call_target="tpu_custom_call" | custom-call | flops 2000000 | bytes 200000 | tf_op jit(solution)/shard_map/choose/pallas_call | solution.py:385
  41.8 2.3 %collective-permute-done.1.high_ref = f32[4,2,8,512]{3,2,1,0:T(8,128)S(1)} collective-permute-done((f32[4,2,8,512]{3,2,1,0:T(8,128)S(1)}, f32[4,2,8,512]{3,2,1,0:T(8,128)S(1)}, u32[]{:S(2)}, u32[]{:S(2)}) %collective-permute-start.1) | collective-permute-done | bytes 131104 | tf_op jit(solution)/shard_map/ppermute | solution.py:404
  44.1 6.1 %band.1.deriv_ref = f32[4,128,512]{2,1,0:T(8,128)S(1)} custom-call(f32[4,128,512]{2,1,0:T(8,128)S(1)} %get-tuple-element.24.mid_ref, f32[4,2,8,512]{3,2,1,0:T(8,128)S(1)} %collective-permute-done.low_ref, f32[4,2,8,512]{3,2,1,0:T(8,128)S(1)} %collective-permute-done.1.high_ref, f32[9,512]{1,0:T(8,128)S(1)} %copy-done.2, ...), custom_call_target="tpu_custom_call", output_to_operand_aliasing={{}: (0, {})} | custom-call | flops 5000000 | bytes 500000 | tf_op jit(solution)/shard_map/band/pallas_call | solution.py:385
  50.3 6.0 %all-to-all-done.1 = f32[64,1,2816]{2,1,0:T(1,128)S(1)} async-done(((f32[64,1,2816]{2,1,0:T(1,128)}), f32[64,1,2816]{2,1,0:T(1,128)S(1)}, u32[]{:S(2)}, u32[]{:S(2)}) %all-to-all-start.1) | async-done | bytes 720928 | tf_op jit(solution)/shard_map/all_to_all | solution.py:448
  56.3 2.7 %apply.1 = (f32[4,128,512]{2,1,0:T(8,128)}, f32[4,128,512]{2,1,0:T(8,128)}) custom-call(f32[1408,128]{1,0:T(8,128)S(1)} %bitcast.12, bf16[384,384]{1,0:T(8,128)(2,1)S(1)} %get-tuple-element.20.col_ref, f32[64,128]{1,0:T(8,128)S(1)} %get-tuple-element.21.row_ref, f32[2,48,128]{2,1,0:T(8,128)S(1)} %get-tuple-element.22.col_coef_ref, ...), custom_call_target="tpu_custom_call" | custom-call | flops 4000000 | bytes 400000 | tf_op jit(solution)/shard_map/apply/pallas_call | solution.py:385
  (8 shorter events, 0.0 us)
Async XLA Ops:
  0.6 0.7 %copy-start.3 = (s32[4,4,96]{2,1,0:T(4,128)S(1)}, s32[4,4,96]{2,1,0:T(4,128)}, u32[]{:S(2)}) copy-start(s32[4,4,96]{2,1,0:T(4,128)} %links_ref.3) | copy-start | bytes 18436
  2.4 24.1 %all-to-all-start = ((s32[64,1,16]{2,1,0:T(1,128)}), s32[64,1,16]{2,1,0:T(1,128)S(1)}, u32[]{:S(2)}, u32[]{:S(2)}) async-start(s32[64,1,16]{2,1,0:T(1,128)} %bitcast.1), calls=%async_computation | async-start | bytes 65536 | tf_op jit(solution)/shard_map/all_to_all | solution.py:416
  17.2 0.7 %copy-start.5 = (s32[64]{0:T(128)S(1)}, s32[64]{0:T(128)}, u32[]{:S(2)}) copy-start(s32[64]{0:T(128)} %counts_ref.3) | copy-start | bytes 772
  17.3 0.7 %copy-start.6 = (s32[48]{0:T(128)S(1)}, s32[48]{0:T(128)}, u32[]{:S(2)}) copy-start(s32[48]{0:T(128)} %sites_ref.5) | copy-start | bytes 580
  17.9 1.2 %copy-start = (f32[4,2,64,512]{3,2,1,0:T(8,128)S(1)}, f32[4,2,64,512]{3,2,1,0:T(8,128)}, u32[]{:S(2)}) copy-start(f32[4,2,64,512]{3,2,1,0:T(8,128)} %param.8) | copy-start | bytes 3145732
  19.1 1.2 %copy-start.1 = (f32[4,2,64,512]{3,2,1,0:T(8,128)S(1)}, f32[4,2,64,512]{3,2,1,0:T(8,128)}, u32[]{:S(2)}) copy-start(f32[4,2,64,512]{3,2,1,0:T(8,128)} %param.9) | copy-start | bytes 3145732
  28.3 10.9 %copy-start.4 = (s32[4,4,96]{2,1,0:T(4,128)S(1)}, s32[4,4,96]{2,1,0:T(4,128)}, u32[]{:S(2)}) copy-start(s32[4,4,96]{2,1,0:T(4,128)} %links_ref.3) | copy-start | bytes 18436
  28.3 15.8 %copy-start.2 = (f32[9,512]{1,0:T(8,128)S(1)}, f32[9,512]{1,0:T(8,128)}, u32[]{:S(2)}) copy-start(f32[9,512]{1,0:T(8,128)} %bands_ref.1) | copy-start | bytes 55300
  28.3 28.0 %all-to-all-start.1 = ((f32[64,1,2816]{2,1,0:T(1,128)}), f32[64,1,2816]{2,1,0:T(1,128)S(1)}, u32[]{:S(2)}, u32[]{:S(2)}) async-start(f32[64,1,2816]{2,1,0:T(1,128)} %bitcast.5), calls=%async_computation.1 | async-start | bytes 1441792 | tf_op jit(solution)/shard_map/all_to_all | solution.py:448
  34.7 7.1 %collective-permute-start = (f32[4,2,8,512]{3,2,1,0:T(8,128)}, f32[4,2,8,512]{3,2,1,0:T(8,128)S(1)}, u32[]{:S(2)}, u32[]{:S(2)}) collective-permute-start(f32[4,2,8,512]{3,2,1,0:T(8,128)} %get-tuple-element.27), channel_id=1, source_target_pairs={{0,1},{1,2},{2,3},{3,4},{4,5},{5,6},{6,7},{8,9},{9,10},{10,11},{11... | collective-permute-start | bytes 393224 | tf_op jit(solution)/shard_map/ppermute | solution.py:404
  37.9 6.2 %collective-permute-start.1 = (f32[4,2,8,512]{3,2,1,0:T(8,128)S(1)}, f32[4,2,8,512]{3,2,1,0:T(8,128)S(1)}, u32[]{:S(2)}, u32[]{:S(2)}) collective-permute-start(f32[4,2,8,512]{3,2,1,0:T(8,128)S(1)} %get-tuple-element.28), channel_id=1, source_target_pairs={{1,0},{2,1},{3,2},{4,3},{5,4},{6,5},{7,6},{9,8},{10,9},{11,10},{12... | collective-permute-start | bytes 393224 | tf_op jit(solution)/shard_map/ppermute | solution.py:404
  39.2 0.7 %copy-start.7 = (f32[2,48]{1,0:T(2,128)S(1)}, f32[2,48]{1,0:T(2,128)}, u32[]{:S(2)}) copy-start(f32[2,48]{1,0:T(2,128)} %coef_ref.1) | copy-start | bytes 1156
  39.2 0.7 %copy-start.8 = (f32[48]{0:T(128)S(1)}, f32[48]{0:T(128)}, u32[]{:S(2)}) copy-start(f32[48]{0:T(128)} %param.14) | copy-start | bytes 580

commit v7 on v6

--- a/solution.py
+++ b/solution.py
@@ -375,7 +375,7 @@
         next_scr[g] = slope_next
         pltpu.make_async_copy(next_scr.at[g], next_ref.at[g], sem.at[0, g]).start()
         sum_scr[g] = base_ref[g] + (step_size / 3.0) * slope_next
-        pltpu.make_async_copy(sum_scr.at[g], sum_ref.at[g], sem.at[1, g]).start()
+        pltpu.make_async_copy(sum_scr.at[g], sum_ref.at[g], sem.at[1, g]).start(priority=1)
     for g in range(z.slots):
         pltpu.make_async_copy(next_scr.at[g], next_ref.at[g], sem.at[0, g]).wait()
         pltpu.make_async_copy(sum_scr.at[g], sum_ref.at[g], sem.at[1, g]).wait()

time: 59.5 us -> 59.5 us (level)
  no operation moved by 1% of the time
where the time goes in v7:
time: 59.5 us; the launch traced here: 59 us
  starting transfers between devices  25.7 us (43%)
  Pallas kernels  15.7 us (26%)
  waiting for transfers between devices  12.4 us (21%)
  local copies, waits for them, and re-layouts  4.46 us (7%)
  between operations  0.73 us (1%)
    pallas_call x6, Pallas kernels, call(): pl.pallas_call(functools.partial(kernel, z), out_shape=outs, in_specs=in_...  15.7 us
    all_to_all x1, starting transfers between devices, shards(): lax.all_to_all(ask.reshape(z.tiers, 1, z.ask), 'tier', split_axis=0, conc...  14.8 us
    all_to_all x1, starting transfers between devices, shards(): lax.all_to_all(answer.reshape(z.tiers, 1, z.message * LANES), 'tier', spl...  6.39 us
    all_to_all x1, waiting for transfers between devices, shards(): lax.all_to_all(answer.reshape(z.tiers, 1, z.message * LANES), 'tier', spl...  6.02 us
    unnamed x18, local copies, waits for them, and re-layouts  4.46 us
    all_to_all x1, waiting for transfers between devices, shards(): lax.all_to_all(ask.reshape(z.tiers, 1, z.ask), 'tier', split_axis=0, conc...  4.07 us
    ppermute x1, starting transfers between devices, neighbours(): lax.ppermute(high_edge, 'sys', forward)  3.21 us
    ppermute x1, waiting for transfers between devices, neighbours(): lax.ppermute(low_edge, 'sys', backward)  2.35 us
  transfers between devices with their start and end apart: 4, of which 3 were waited for; matrix products, arithmetic and copies ran while one was open for 0% of the time, Pallas kernels for 17%

profile of v7, /device:TPU:1, one launch (start us, length us, event | category | flops | bytes accessed | tf_op | source)
XLA Modules:
  0.0 59.0 jit_solution(17829736256712759431)
XLA Ops:
  0.6 0.0 copy-start.3
  0.6 0.7 %copy-done.3 = s32[4,4,96]{2,1,0:T(4,128)S(1)} copy-done((s32[4,4,96]{2,1,0:T(4,128)S(1)}, s32[4,4,96]{2,1,0:T(4,128)}, u32[]{:S(2)}) %copy-start.3) | copy-done | bytes 6168
  1.3 1.1 %ask.1 = s32[64,16]{1,0:T(8,128)} custom-call(s32[4,4,96]{2,1,0:T(4,128)S(1)} %copy-done.3), custom_call_target="tpu_custom_call" | custom-call | flops 1000000 | bytes 100000 | tf_op jit(solution)/shard_map/ask/pallas_call | solution.py:385
  2.4 14.8 %all-to-all-start = ((s32[64,1,16]{2,1,0:T(1,128)}), s32[64,1,16]{2,1,0:T(1,128)S(1)}, u32[]{:S(2)}, u32[]{:S(2)}) async-start(s32[64,1,16]{2,1,0:T(1,128)} %bitcast.1), calls=%async_computation | async-start | bytes 65536 | tf_op jit(solution)/shard_map/all_to_all | solution.py:416
  17.2 0.0 copy-start.5
  17.3 0.0 copy-start.6
  17.3 0.6 %copy-done.5 = s32[64]{0:T(128)S(1)} copy-done((s32[64]{0:T(128)S(1)}, s32[64]{0:T(128)}, u32[]{:S(2)}) %copy-start.5) | copy-done | bytes 280
  17.9 0.0 copy-done.6
  17.9 1.2 %copy-done = f32[4,2,64,512]{3,2,1,0:T(8,128)S(1)} copy-done((f32[4,2,64,512]{3,2,1,0:T(8,128)S(1)}, f32[4,2,64,512]{3,2,1,0:T(8,128)}, u32[]{:S(2)}) %copy-start) | copy-done | bytes 1048600
  19.1 1.2 %copy-done.1 = f32[4,2,64,512]{3,2,1,0:T(8,128)S(1)} copy-done((f32[4,2,64,512]{3,2,1,0:T(8,128)S(1)}, f32[4,2,64,512]{3,2,1,0:T(8,128)}, u32[]{:S(2)}) %copy-start.1) | copy-done | bytes 1048600
  20.4 2.0 %tables.1 = (f32[4,2,8,512]{3,2,1,0:T(8,128)S(1)}, f32[4,2,8,512]{3,2,1,0:T(8,128)}, bf16[768,128]{1,0:T(8,128)(2,1)S(1)}, bf16[96,1024]{1,0:T(8,128)(2,1)S(1)},...) custom-call(f32[4,128,512]{2,1,0:T(8,128)S(1)} %bitcast.13, f32[4,128,512]{2,1,0:T(8,128)S(1)} %bitcast.14, ...), custom_call_target="tpu_custom_call" | custom-call | flops 3000000 | bytes 300000 | tf_op jit(solution)/shard_map/tables/pallas_call | solution.py:385
  22.4 4.1 %all-to-all-done = s32[64,1,16]{2,1,0:T(1,128)S(1)} async-done(((s32[64,1,16]{2,1,0:T(1,128)}), s32[64,1,16]{2,1,0:T(1,128)S(1)}, u32[]{:S(2)}, u32[]{:S(2)}) %all-to-all-start) | async-done | bytes 4128 | tf_op jit(solution)/shard_map/all_to_all | solution.py:416
  26.5 1.8 %answer.1 = f32[1408,128]{1,0:T(8,128)} custom-call(s32[64,16]{1,0:T(8,128)S(1)} %bitcast.15, bf16[768,128]{1,0:T(8,128)(2,1)S(1)} %get-tuple-element.18.col_ref, bf16[96,1024]{1,0:T(8,128)(2,1)S(1)} %get-tuple-element.19.row_ref), custom_call_target="tpu_custom_call" | custom-call | flops 1000000 | bytes 100000 | tf_op jit(solution)/shard_map/answer/pallas_call | solution.py:385
  28.3 6.4 %all-to-all-start.1 = ((f32[64,1,2816]{2,1,0:T(1,128)}), f32[64,1,2816]{2,1,0:T(1,128)S(1)}, u32[]{:S(2)}, u32[]{:S(2)}) async-start(f32[64,1,2816]{2,1,0:T(1,128)} %bitcast.5), calls=%async_computation.1 | async-start | bytes 1441792 | tf_op jit(solution)/shard_map/all_to_all | solution.py:448
  34.7 3.2 %collective-permute-start = (f32[4,2,8,512]{3,2,1,0:T(8,128)}, f32[4,2,8,512]{3,2,1,0:T(8,128)S(1)}, u32[]{:S(2)}, u32[]{:S(2)}) collective-permute-start(f32[4,2,8,512]{3,2,1,0:T(8,128)} %get-tuple-element.27), channel_id=1, source_target_pairs={{0,1},{1,2},{2,3},{3,4},{4,5},{5,6},{6,7},{8,9},{9,10},{10,11},{11... | collective-permute-start | bytes 393224 | tf_op jit(solution)/shard_map/ppermute | solution.py:404
  37.9 1.3 %collective-permute-start.1 = (f32[4,2,8,512]{3,2,1,0:T(8,128)S(1)}, f32[4,2,8,512]{3,2,1,0:T(8,128)S(1)}, u32[]{:S(2)}, u32[]{:S(2)}) collective-permute-start(f32[4,2,8,512]{3,2,1,0:T(8,128)S(1)} %get-tuple-element.28), channel_id=1, source_target_pairs={{1,0},{2,1},{3,2},{4,3},{5,4},{6,5},{7,6},{9,8},{10,9},{11,10},{12... | collective-permute-start | bytes 393224 | tf_op jit(solution)/shard_map/ppermute | solution.py:404
  39.2 0.0 copy-start.7
  39.2 0.0 copy-start.8
  39.3 0.6 %copy-done.7 = f32[2,48]{1,0:T(2,128)S(1)} copy-done((f32[2,48]{1,0:T(2,128)S(1)}, f32[2,48]{1,0:T(2,128)}, u32[]{:S(2)}) %copy-start.7) | copy-done | bytes 408
  39.9 1.9 %choose.1 = (bf16[384,384]{1,0:T(8,128)(2,1)S(1)}, f32[64,128]{1,0:T(8,128)S(1)}, f32[2,48,128]{2,1,0:T(8,128)S(1)}, f32[2,8,128]{2,1,0:T(8,128)S(1)}, f32[4,8,1...) custom-call(s32[4,4,96]{2,1,0:T(4,128)S(1)} %copy-done.4, s32[1,64]{1,0:T(1,128)S(1)} %bitcast.16, f32[2,48]{1,0:T(2,128)S(1)} %copy-done.7, ...), custom_call_target="tpu_custom_call" | custom-call | flops 2000000 | bytes 200000 | tf_op jit(solution)/shard_map/choose/pallas_call | solution.py:385
  41.8 2.3 %collective-permute-done.1.high_ref = f32[4,2,8,512]{3,2,1,0:T(8,128)S(1)} collective-permute-done((f32[4,2,8,512]{3,2,1,0:T(8,128)S(1)}, f32[4,2,8,512]{3,2,1,0:T(8,128)S(1)}, u32[]{:S(2)}, u32[]{:S(2)}) %collective-permute-start.1) | collective-permute-done | bytes 131104 | tf_op jit(solution)/shard_map/ppermute | solution.py:404
  44.1 6.1 %band.1.deriv_ref = f32[4,128,512]{2,1,0:T(8,128)S(1)} custom-call(f32[4,128,512]{2,1,0:T(8,128)S(1)} %get-tuple-element.24.mid_ref, f32[4,2,8,512]{3,2,1,0:T(8,128)S(1)} %collective-permute-done.low_ref, f32[4,2,8,512]{3,2,1,0:T(8,128)S(1)} %collective-permute-done.1.high_ref, f32[9,512]{1,0:T(8,128)S(1)} %copy-done.2, ...), custom_call_target="tpu_custom_call", output_to_operand_aliasing={{}: (0, {})} | custom-call | flops 5000000 | bytes 500000 | tf_op jit(solution)/shard_map/band/pallas_call | solution.py:385
  50.3 6.0 %all-to-all-done.1 = f32[64,1,2816]{2,1,0:T(1,128)S(1)} async-done(((f32[64,1,2816]{2,1,0:T(1,128)}), f32[64,1,2816]{2,1,0:T(1,128)S(1)}, u32[]{:S(2)}, u32[]{:S(2)}) %all-to-all-start.1) | async-done | bytes 720928 | tf_op jit(solution)/shard_map/all_to_all | solution.py:448
  56.3 2.7 %apply.1 = (f32[4,128,512]{2,1,0:T(8,128)}, f32[4,128,512]{2,1,0:T(8,128)}) custom-call(f32[1408,128]{1,0:T(8,128)S(1)} %bitcast.12, bf16[384,384]{1,0:T(8,128)(2,1)S(1)} %get-tuple-element.20.col_ref, f32[64,128]{1,0:T(8,128)S(1)} %get-tuple-element.21.row_ref, f32[2,48,128]{2,1,0:T(8,128)S(1)} %get-tuple-element.22.col_coef_ref, ...), custom_call_target="tpu_custom_call" | custom-call | flops 4000000 | bytes 400000 | tf_op jit(solution)/shard_map/apply/pallas_call | solution.py:385
  (8 shorter events, 0.0 us)
Async XLA Ops:
  0.6 0.7 %copy-start.3 = (s32[4,4,96]{2,1,0:T(4,128)S(1)}, s32[4,4,96]{2,1,0:T(4,128)}, u32[]{:S(2)}) copy-start(s32[4,4,96]{2,1,0:T(4,128)} %links_ref.3) | copy-start | bytes 18436
  2.4 24.1 %all-to-all-start = ((s32[64,1,16]{2,1,0:T(1,128)}), s32[64,1,16]{2,1,0:T(1,128)S(1)}, u32[]{:S(2)}, u32[]{:S(2)}) async-start(s32[64,1,16]{2,1,0:T(1,128)} %bitcast.1), calls=%async_computation | async-start | bytes 65536 | tf_op jit(solution)/shard_map/all_to_all | solution.py:416
  17.2 0.7 %copy-start.5 = (s32[64]{0:T(128)S(1)}, s32[64]{0:T(128)}, u32[]{:S(2)}) copy-start(s32[64]{0:T(128)} %counts_ref.3) | copy-start | bytes 772
  17.3 0.7 %copy-start.6 = (s32[48]{0:T(128)S(1)}, s32[48]{0:T(128)}, u32[]{:S(2)}) copy-start(s32[48]{0:T(128)} %sites_ref.5) | copy-start | bytes 580
  17.9 1.2 %copy-start = (f32[4,2,64,512]{3,2,1,0:T(8,128)S(1)}, f32[4,2,64,512]{3,2,1,0:T(8,128)}, u32[]{:S(2)}) copy-start(f32[4,2,64,512]{3,2,1,0:T(8,128)} %param.8) | copy-start | bytes 3145732
  19.1 1.2 %copy-start.1 = (f32[4,2,64,512]{3,2,1,0:T(8,128)S(1)}, f32[4,2,64,512]{3,2,1,0:T(8,128)}, u32[]{:S(2)}) copy-start(f32[4,2,64,512]{3,2,1,0:T(8,128)} %param.9) | copy-start | bytes 3145732
  28.3 10.9 %copy-start.4 = (s32[4,4,96]{2,1,0:T(4,128)S(1)}, s32[4,4,96]{2,1,0:T(4,128)}, u32[]{:S(2)}) copy-start(s32[4,4,96]{2,1,0:T(4,128)} %links_ref.3) | copy-start | bytes 18436
  28.3 15.8 %copy-start.2 = (f32[9,512]{1,0:T(8,128)S(1)}, f32[9,512]{1,0:T(8,128)}, u32[]{:S(2)}) copy-start(f32[9,512]{1,0:T(8,128)} %bands_ref.1) | copy-start | bytes 55300
  28.3 28.0 %all-to-all-start.1 = ((f32[64,1,2816]{2,1,0:T(1,128)}), f32[64,1,2816]{2,1,0:T(1,128)S(1)}, u32[]{:S(2)}, u32[]{:S(2)}) async-start(f32[64,1,2816]{2,1,0:T(1,128)} %bitcast.5), calls=%async_computation.1 | async-start | bytes 1441792 | tf_op jit(solution)/shard_map/all_to_all | solution.py:448
  34.7 7.1 %collective-permute-start = (f32[4,2,8,512]{3,2,1,0:T(8,128)}, f32[4,2,8,512]{3,2,1,0:T(8,128)S(1)}, u32[]{:S(2)}, u32[]{:S(2)}) collective-permute-start(f32[4,2,8,512]{3,2,1,0:T(8,128)} %get-tuple-element.27), channel_id=1, source_target_pairs={{0,1},{1,2},{2,3},{3,4},{4,5},{5,6},{6,7},{8,9},{9,10},{10,11},{11... | collective-permute-start | bytes 393224 | tf_op jit(solution)/shard_map/ppermute | solution.py:404
  37.9 6.2 %collective-permute-start.1 = (f32[4,2,8,512]{3,2,1,0:T(8,128)S(1)}, f32[4,2,8,512]{3,2,1,0:T(8,128)S(1)}, u32[]{:S(2)}, u32[]{:S(2)}) collective-permute-start(f32[4,2,8,512]{3,2,1,0:T(8,128)S(1)} %get-tuple-element.28), channel_id=1, source_target_pairs={{1,0},{2,1},{3,2},{4,3},{5,4},{6,5},{7,6},{9,8},{10,9},{11,10},{12... | collective-permute-start | bytes 393224 | tf_op jit(solution)/shard_map/ppermute | solution.py:404
  39.2 0.7 %copy-start.7 = (f32[2,48]{1,0:T(2,128)S(1)}, f32[2,48]{1,0:T(2,128)}, u32[]{:S(2)}) copy-start(f32[2,48]{1,0:T(2,128)} %coef_ref.1) | copy-start | bytes 1156
  39.2 0.7 %copy-start.8 = (f32[48]{0:T(128)S(1)}, f32[48]{0:T(128)}, u32[]{:S(2)}) copy-start(f32[48]{0:T(128)} %param.14) | copy-start | bytes 580
